TPU v7x, 32 devices: a whole 2x2x4 slice. The times are simulated.
32 devices in a mesh: blk: 16 (over z, y, core), tile: 2 (over x).
Axes of the slice: x: 2, y: 2, z: 4, core: 2. Of those that a mesh axis runs over, the one named last changes fastest.
Arguments:
- positions: float32 [3, 2048], P(None, ('blk', 'tile')), as said below
- noise_vectors: float32 [3, 32, 2048], P(None, None, ('blk', 'tile')), may hold values from -6 to 6
- spectrum_bounds: float32 [2], replicated, as said below
Outputs:
- displacement: float32 [3, 32, 2048], P(None, None, ('blk', 'tile'))
- images: float32 [2, 3, 32, 2048], P(None, None, None, ('blk', 'tile'))
Inputs may be any that keep to these rules, and one draw needn't show every extreme that they name: `positions`: coordinates lie in a cube whose edge is the cube root of 41.9 * 2048; particle n's third coordinate lies between n and n + 1 times that edge divided by 2048. `spectrum_bounds`: the first entry lies between 0.15 and 0.35; the second exceeds 50 times the first.
All inputs are finite; a program needn't handle non-finite values.
Results may differ from a plain program's by a relative error of at most 0.0003.
Values sent between devices are 32-bit elements; how exact they have to be, the bound alone decides.
No kernel may reach another device: no remote copies, remote signals or barrier semaphores. Data moves between devices by JAX's collectives and lax.ppermute only.
A program may use at most 64 MiB of HBM per device.

v0:
```python
import math

import jax
import jax.numpy as jnp
from jax import lax
from jax.sharding import PartitionSpec as P

soft_core = 1e-06
node_count = 32


def from_partner(block, axis, apart):
    count = lax.axis_size(axis)
    route = []
    for low in range(count):
        high = low | 1 << apart
        if high != low and high < count:
            route += [(low, high), (high, low)]
    return lax.ppermute(block, axis, route)


def kernel(targets, sources):
    offset = targets[:, :, None] - sources[:, None, :]
    squared = jnp.sum(offset * offset, axis=0) + soft_core
    distance = jnp.sqrt(squared)
    inverse = 1.0 / distance
    cubed = inverse * inverse * inverse
    intersection = distance < 2.0
    scalar_part = jnp.where(intersection, 1.0 - 0.28125 * distance, 0.75 * inverse + 0.5 * cubed)
    dyadic_part = jnp.where(
        intersection, 0.09375 * inverse, 0.75 * cubed - 1.5 * cubed * inverse * inverse
    )
    identity = jnp.eye(3, dtype=targets.dtype)
    return (
        identity[:, :, None, None] * scalar_part[None, None]
        + dyadic_part[None, None] * offset[:, None] * offset[None, :]
    )


def contract(tensor, vectors):
    return jnp.einsum("abij,bkj->aki", tensor, vectors, precision=lax.Precision.HIGHEST)


def weights_from(bounds):
    lowest = bounds[0]
    highest = bounds[1]
    center = 0.5 * (highest + lowest)
    spread = 0.5 * (highest - lowest)
    angles = math.pi * (jnp.arange(node_count, dtype=bounds.dtype) + 0.5) / node_count
    samples = jnp.sqrt(center + spread * jnp.cos(angles))
    weights = [2.0 / node_count * jnp.sum(samples * jnp.cos(order * angles)) for order in range(3)]
    return (center, spread, weights)


def apply_blocks(targets, incoming):
    return contract(kernel(targets, incoming[:, 0, :]), incoming[:, 1:, :])


def grid_product(packed, positions):
    half_bits = (lax.axis_size("blk").bit_length() - 1) // 2
    block_number = lax.axis_index("blk")
    sources = lax.all_gather(packed, "tile", axis=2, tiled=True)
    for bit_number in range(half_bits, 2 * half_bits):
        partner = from_partner(sources, "blk", bit_number)
        sources = jnp.concatenate([sources, partner], axis=2)
    targets = positions
    for bit_number in range(half_bits):
        partner = from_partner(targets, "blk", bit_number)
        own_bit = block_number // (1 << bit_number) % 2
        targets = jnp.where(
            own_bit == 1,
            jnp.concatenate([partner, targets], axis=1),
            jnp.concatenate([targets, partner], axis=1),
        )
    partial_value = apply_blocks(targets, sources)
    for bit_number in reversed(range(half_bits)):
        half_width = partial_value.shape[2] // 2
        own_bit = block_number // (1 << bit_number) % 2
        kept_half = lax.dynamic_slice_in_dim(partial_value, own_bit * half_width, half_width, 2)
        sent_half = lax.dynamic_slice_in_dim(
            partial_value, (1 - own_bit) * half_width, half_width, 2
        )
        partial_value = kept_half + from_partner(sent_half, "blk", bit_number)
    return partial_value


def mobility(vectors, positions):
    packed = jnp.concatenate([positions[:, None, :], vectors], axis=1)
    return grid_product(packed, positions)


def body(positions, noise_vectors, spectrum_bounds):
    center, spread, weights = weights_from(spectrum_bounds)
    first_image = mobility(noise_vectors, positions)
    linear_term = (first_image - center * noise_vectors) / spread
    second_image = mobility(linear_term, positions)
    quadratic_term = 2.0 * (second_image - center * linear_term) / spread - noise_vectors
    displacement = (
        0.5 * weights[0] * noise_vectors + weights[1] * linear_term + weights[2] * quadratic_term
    )
    return (displacement, jnp.stack([first_image, second_image]))


def solution(mesh):
    return jax.shard_map(
        body,
        mesh=mesh,
        in_specs=(P(None, ("blk", "tile")), P(None, None, ("blk", "tile")), P()),
        out_specs=(P(None, None, ("blk", "tile")), P(None, None, None, ("blk", "tile"))),
        check_vma=False,
    )
```

profile of v0, /device:TPU:0, one launch (start us, length us, event | category | flops | bytes accessed | tf_op | source)
XLA Modules:
  0.0 68.6 jit_solution(18296448946351239026)
XLA Ops:
  0.6 0.6 collective-permute-start.2
  1.2 0.7 broadcast_in_dim.2
  1.9 0.8 %pad_maximum_fusion.6 = f32[3,33,64]{2,1,0:T(8,128)S(1)} fusion(f32[3,1,64]{2,1,0:T(1,128)S(1)} %broadcast_in_dim.2, f32[3,32,64]{2,1,0:T(8,128)} %param.4), kind=kLoop, calls=%fused_computation.52 | loop fusion | flops 6336 | bytes 50688 | tf_op jit(solution)/shard_map/concatenate | solution.py:88
  2.7 0.1 copy.14
  2.8 7.3 %all_gather.6 = f32[3,33,128]{1,0,2:T(4,128)S(1)} all-gather(f32[3,33,64]{1,0,2:T(4,128)S(1)} %copy.14), channel_id=1, replica_groups=mesh['blk'=16,'tile'=2] {'tile'}, dimensions={2}, use_global_device_ids=true | all-gather | bytes 76032 | tf_op jit(solution)/shard_map/all_gather | solution.py:62
  10.1 0.1 copy.17
  10.2 1.9 %collective-permute-start = (f32[3,33,128]{2,1,0:T(8,128)S(1)}, f32[3,33,128]{2,1,0:T(8,128)S(1)}, u32[]{:S(2)}, u32[]{:S(2)}) collective-permute-start(f32[3,33,128]{2,1,0:T(8,128)S(1)} %copy.17), channel_id=1, source_target_pairs={{0,8},{8,0},{2,10},{10,2},{4,12},{12,4},{6,14},{14,6},{16,24},{24,... | collective-permute-start | bytes 152072 | tf_op jit(solution)/shard_map/ppermute | solution.py:19
  12.1 0.0 collective-permute-done.2
  12.1 0.8 %maximum_select_fusion.1 = f32[3,128]{1,0:T(4,128)S(1)} fusion(f32[3,64]{1,0:T(4,128)} %param.3, f32[3,64]{1,0:T(4,128)S(1)} %collective-permute-done.2, pred[]{:T(512)S(6)} %eq.29), kind=kLoop, calls=%fused_computation.68 | loop fusion | flops 1152 | bytes 3073 | tf_op jit(solution)/shard_map/jit(_where)/select_n | solution.py:70
  13.0 1.5 %collective-permute-start.3 = (f32[3,128]{1,0:T(4,128)S(1)}, f32[3,128]{1,0:T(4,128)S(1)}, u32[]{:S(2)}, u32[]{:S(2)}) collective-permute-start(f32[3,128]{1,0:T(4,128)S(1)} %maximum_select_fusion.1), channel_id=1, source_target_pairs={{0,4},{4,0},{2,6},{6,2},{8,12},{12,8},{10,14},{14,10},{16,20},{20,... | collective-permute-start | bytes 4616 | tf_op jit(solution)/shard_map/ppermute | solution.py:19
  14.5 0.0 collective-permute-done
  14.5 2.9 %collective-permute-start.1 = (f32[3,33,256]{2,1,0:T(8,128)S(1)}, f32[3,33,256]{2,1,0:T(8,128)S(1)}, u32[]{:S(2)}, u32[]{:S(2)}) collective-permute-start(f32[3,33,256]{2,1,0:T(8,128)S(1)} %pad_maximum_fusion.2), channel_id=1, source_target_pairs={{0,16},{16,0},{2,18},{18,2},{4,20},{20,4},{6,22},{22,6},{8,24},{24... | collective-permute-start | bytes 304136 | tf_op jit(solution)/shard_map/ppermute | solution.py:19
  17.4 0.0 collective-permute-done.3
  17.4 5.0 %collective-permute-done.1 = f32[3,33,256]{2,1,0:T(8,128)S(1)} collective-permute-done((f32[3,33,256]{2,1,0:T(8,128)S(1)}, f32[3,33,256]{2,1,0:T(8,128)S(1)}, u32[]{:S(2)}, u32[]{:S(2)}) %collective-permute-start.1) | collective-permute-done | bytes 101408 | tf_op jit(solution)/shard_map/ppermute | solution.py:19
  22.4 0.2 multiply_reduce_fusion.1
  22.6 0.4 fusion.31
  23.1 0.3 subtract_multiply_fusion.1
  23.4 0.0 copy-start.1
  23.4 0.0 copy-start
  23.4 4.6 %fusion.16 = f32[32,3,256]{2,0,1:T(8,128)S(1)} fusion(f32[3,256,512]{2,1,0:T(8,128)S(1)} %get-tuple-element.13, f32[3,256,512]{2,1,0:T(8,128)S(1)} %get-tuple-element.12, f32[256,512]{1,0:T(8,128)S(1)} %get-tuple-element.4, f32[3,3]{1,0:T(4,128)S(1)} %fusion.38, f32[3,33,512]{2,1,0:T(8,128)S(1)} %pad_maximum_fusion), kind=kOutput, calls=%fused_computation.20 | convolution fusion | flops 456523776 | bytes 3966976 | tf_op jit(solution)/shard_map/abij,bkj->aki/dot_general | solution.py:41
  28.0 1.3 %collective-permute-start.4 = (f32[3,32,128]{2,1,0:T(8,128)S(1)}, f32[3,32,128]{2,1,0:T(8,128)S(1)}, u32[]{:S(2)}, u32[]{:S(2)}) collective-permute-start(f32[3,32,128]{2,1,0:T(8,128)S(1)} %dynamic-slice_bitcast_fusion.1), channel_id=1, source_target_pairs={{0,4},{4,0},{2,6},{6,2},{8,12},{12,8},{10,14},{14,10},{16,20},{20,... | collective-permute-start | bytes 147464 | tf_op jit(solution)/shard_map/ppermute | solution.py:19
  29.3 2.9 %collective-permute-done.4 = f32[3,32,128]{2,1,0:T(8,128)S(1)} collective-permute-done((f32[3,32,128]{2,1,0:T(8,128)S(1)}, f32[3,32,128]{2,1,0:T(8,128)S(1)}, u32[]{:S(2)}, u32[]{:S(2)}) %collective-permute-start.4) | collective-permute-done | bytes 49184 | tf_op jit(solution)/shard_map/ppermute | solution.py:19
  32.2 0.1 constant_dynamic-slice_fusion.1
  32.2 0.0 collective-permute-start.5
  32.3 0.0 copy-done.1
  32.3 0.6 fusion.39
  35.5 0.0 collective-permute-done.5
  35.5 0.1 fusion.36
  35.6 0.1 copy.18
  35.7 6.6 %all_gather.7 = f32[3,33,128]{1,0,2:T(4,128)S(1)} all-gather(f32[3,33,64]{1,0,2:T(4,128)S(1)} %copy.18), channel_id=1, replica_groups=mesh['blk'=16,'tile'=2] {'tile'}, dimensions={2}, use_global_device_ids=true | all-gather | bytes 76032 | tf_op jit(solution)/shard_map/all_gather | solution.py:62
  42.3 0.1 copy.21
  42.4 0.5 collective-permute-start.6
  42.9 3.7 %collective-permute-done.6 = f32[3,33,128]{2,1,0:T(8,128)S(1)} collective-permute-done((f32[3,33,128]{2,1,0:T(8,128)S(1)}, f32[3,33,128]{2,1,0:T(8,128)S(1)}, u32[]{:S(2)}, u32[]{:S(2)}) %collective-permute-start.6) | collective-permute-done | bytes 50720 | tf_op jit(solution)/shard_map/ppermute | solution.py:19
  46.7 1.9 %collective-permute-start.7 = (f32[3,33,256]{2,1,0:T(8,128)S(1)}, f32[3,33,256]{2,1,0:T(8,128)S(1)}, u32[]{:S(2)}, u32[]{:S(2)}) collective-permute-start(f32[3,33,256]{2,1,0:T(8,128)S(1)} %pad_maximum_fusion.3), channel_id=1, source_target_pairs={{0,16},{16,0},{2,18},{18,2},{4,20},{20,4},{6,22},{22,6},{8,24},{24... | collective-permute-start | bytes 304136 | tf_op jit(solution)/shard_map/ppermute | solution.py:19
  48.6 5.4 %collective-permute-done.7 = f32[3,33,256]{2,1,0:T(8,128)S(1)} collective-permute-done((f32[3,33,256]{2,1,0:T(8,128)S(1)}, f32[3,33,256]{2,1,0:T(8,128)S(1)}, u32[]{:S(2)}, u32[]{:S(2)}) %collective-permute-start.7) | collective-permute-done | bytes 101408 | tf_op jit(solution)/shard_map/ppermute | solution.py:19
  54.0 0.2 multiply_reduce_fusion
  54.2 0.4 fusion.28
  54.6 0.3 subtract_multiply_fusion
  55.0 4.6 %fusion.19 = f32[32,3,256]{2,0,1:T(8,128)S(1)} fusion(f32[3,256,512]{2,1,0:T(8,128)S(1)} %get-tuple-element.11, f32[3,256,512]{2,1,0:T(8,128)S(1)} %get-tuple-element.10, f32[256,512]{1,0:T(8,128)S(1)} %get-tuple-element.2, f32[3,3]{1,0:T(4,128)S(1)} %fusion.38, f32[3,33,512]{2,1,0:T(8,128)S(1)} %pad_maximum_fusion.1), kind=kOutput, calls=%fused_computation.21 | convolution fusion | flops 456523776 | bytes 3966976 | tf_op jit(solution)/shard_map/abij,bkj->aki/dot_general | solution.py:41
  59.5 1.3 %collective-permute-start.8 = (f32[3,32,128]{2,1,0:T(8,128)S(1)}, f32[3,32,128]{2,1,0:T(8,128)S(1)}, u32[]{:S(2)}, u32[]{:S(2)}) collective-permute-start(f32[3,32,128]{2,1,0:T(8,128)S(1)} %dynamic-slice_bitcast_fusion), channel_id=1, source_target_pairs={{0,4},{4,0},{2,6},{6,2},{8,12},{12,8},{10,14},{14,10},{16,20},{20,... | collective-permute-start | bytes 147464 | tf_op jit(solution)/shard_map/ppermute | solution.py:19
  60.8 2.9 %collective-permute-done.8 = f32[3,32,128]{2,1,0:T(8,128)S(1)} collective-permute-done((f32[3,32,128]{2,1,0:T(8,128)S(1)}, f32[3,32,128]{2,1,0:T(8,128)S(1)}, u32[]{:S(2)}, u32[]{:S(2)}) %collective-permute-start.8) | collective-permute-done | bytes 49184 | tf_op jit(solution)/shard_map/ppermute | solution.py:19
  63.7 0.1 constant_dynamic-slice_fusion
  63.8 0.0 collective-permute-start.9
  63.8 0.7 %multiply_reduce_fusion.2 = (f32[]{:T(128)}, f32[]{:T(128)}) fusion(f32[]{:T(128)} %bitcast.1, f32[]{:T(128)} %bitcast), kind=kLoop, calls=%fused_computation.73 | loop fusion | flops 286 | bytes 16 | tf_op jit(solution)/shard_map/reduce_sum | solution.py:51
  65.9 0.7 multiply_reduce_fusion.4
  67.2 0.0 collective-permute-done.9
  67.2 0.7 %fusion.37 = (f32[1,3,32,64]{3,2,1,0:T(8,128)S(1)}, f32[3,32,64]{2,1,0:T(8,128)}) fusion(f32[3,32,64]{2,1,0:T(8,128)S(1)} %collective-permute-done.9, f32[3,32,128]{2,1,0:T(8,128)S(1)} %bitcast_add_fusion, s32[]{:T(128)S(6)} %select_n.117, f32[3,32,64]{2,1,0:T(8,128)S(1)} %copy-done, f32[]{:T(128)} %bitcast.1, f32[3,32,64]{2,1,0:T(8,128)S(1)} %get-tuple-element.7, ...), kind=kLoop, calls=%fused_computation.62 | loop fusion | flops 67584 | bytes 147480 | tf_op jit(solution)/shard_map/stack | solution.py:101
  67.9 0.6 pad_maximum_fusion.4
  (16 shorter events, 0.1 us)
Async XLA Ops:
  0.6 11.5 %collective-permute-start.2 = (f32[3,64]{1,0:T(4,128)}, f32[3,64]{1,0:T(4,128)S(1)}, u32[]{:S(2)}, u32[]{:S(2)}) collective-permute-start(f32[3,64]{1,0:T(4,128)} %param.3), channel_id=1, source_target_pairs={{0,2},{2,0},{4,6},{6,4},{8,10},{10,8},{12,14},{14,12},{16,18},{18,... | collective-permute-start | bytes 2312 | tf_op jit(solution)/shard_map/ppermute | solution.py:19
  10.2 4.3 %collective-permute-start = (f32[3,33,128]{2,1,0:T(8,128)S(1)}, f32[3,33,128]{2,1,0:T(8,128)S(1)}, u32[]{:S(2)}, u32[]{:S(2)}) collective-permute-start(f32[3,33,128]{2,1,0:T(8,128)S(1)} %copy.17), channel_id=1, source_target_pairs={{0,8},{8,0},{2,10},{10,2},{4,12},{12,4},{6,14},{14,6},{16,24},{24,... | collective-permute-start | bytes 152072 | tf_op jit(solution)/shard_map/ppermute | solution.py:19
  13.0 4.5 %collective-permute-start.3 = (f32[3,128]{1,0:T(4,128)S(1)}, f32[3,128]{1,0:T(4,128)S(1)}, u32[]{:S(2)}, u32[]{:S(2)}) collective-permute-start(f32[3,128]{1,0:T(4,128)S(1)} %maximum_select_fusion.1), channel_id=1, source_target_pairs={{0,4},{4,0},{2,6},{6,2},{8,12},{12,8},{10,14},{14,10},{16,20},{20,... | collective-permute-start | bytes 4616 | tf_op jit(solution)/shard_map/ppermute | solution.py:19
  14.5 7.9 %collective-permute-start.1 = (f32[3,33,256]{2,1,0:T(8,128)S(1)}, f32[3,33,256]{2,1,0:T(8,128)S(1)}, u32[]{:S(2)}, u32[]{:S(2)}) collective-permute-start(f32[3,33,256]{2,1,0:T(8,128)S(1)} %pad_maximum_fusion.2), channel_id=1, source_target_pairs={{0,16},{16,0},{2,18},{18,2},{4,20},{20,4},{6,22},{22,6},{8,24},{24... | collective-permute-start | bytes 304136 | tf_op jit(solution)/shard_map/ppermute | solution.py:19
  23.4 8.9 %copy-start.1 = (f32[2]{0:T(128)S(1)}, f32[2]{0:T(128)}, u32[]{:S(2)}) copy-start(f32[2]{0:T(128)} %param.5) | copy-start | bytes 28
  23.4 12.1 %copy-start = (f32[3,32,64]{2,1,0:T(8,128)S(1)}, f32[3,32,64]{2,1,0:T(8,128)}, u32[]{:S(2)}) copy-start(f32[3,32,64]{2,1,0:T(8,128)} %param.4) | copy-start | bytes 73732
  28.0 4.2 %collective-permute-start.4 = (f32[3,32,128]{2,1,0:T(8,128)S(1)}, f32[3,32,128]{2,1,0:T(8,128)S(1)}, u32[]{:S(2)}, u32[]{:S(2)}) collective-permute-start(f32[3,32,128]{2,1,0:T(8,128)S(1)} %dynamic-slice_bitcast_fusion.1), channel_id=1, source_target_pairs={{0,4},{4,0},{2,6},{6,2},{8,12},{12,8},{10,14},{14,10},{16,20},{20,... | collective-permute-start | bytes 147464 | tf_op jit(solution)/shard_map/ppermute | solution.py:19
  32.2 3.2 %collective-permute-start.5 = (f32[3,32,64]{2,1,0:T(8,128)S(1)}, f32[3,32,64]{2,1,0:T(8,128)S(1)}, u32[]{:S(2)}, u32[]{:S(2)}) collective-permute-start(f32[3,32,64]{2,1,0:T(8,128)S(1)} %constant_dynamic-slice_fusion.1), channel_id=1, source_target_pairs={{0,2},{2,0},{4,6},{6,4},{8,10},{10,8},{12,14},{14,12},{16,18},{18,... | collective-permute-start | bytes 73736 | tf_op jit(solution)/shard_map/ppermute | solution.py:19
  42.4 4.3 %collective-permute-start.6 = (f32[3,33,128]{2,1,0:T(8,128)S(1)}, f32[3,33,128]{2,1,0:T(8,128)S(1)}, u32[]{:S(2)}, u32[]{:S(2)}) collective-permute-start(f32[3,33,128]{2,1,0:T(8,128)S(1)} %copy.21), channel_id=1, source_target_pairs={{0,8},{8,0},{2,10},{10,2},{4,12},{12,4},{6,14},{14,6},{16,24},{24,... | collective-permute-start | bytes 152072 | tf_op jit(solution)/shard_map/ppermute | solution.py:19
  46.7 7.3 %collective-permute-start.7 = (f32[3,33,256]{2,1,0:T(8,128)S(1)}, f32[3,33,256]{2,1,0:T(8,128)S(1)}, u32[]{:S(2)}, u32[]{:S(2)}) collective-permute-start(f32[3,33,256]{2,1,0:T(8,128)S(1)} %pad_maximum_fusion.3), channel_id=1, source_target_pairs={{0,16},{16,0},{2,18},{18,2},{4,20},{20,4},{6,22},{22,6},{8,24},{24... | collective-permute-start | bytes 304136 | tf_op jit(solution)/shard_map/ppermute | solution.py:19
  59.5 4.2 %collective-permute-start.8 = (f32[3,32,128]{2,1,0:T(8,128)S(1)}, f32[3,32,128]{2,1,0:T(8,128)S(1)}, u32[]{:S(2)}, u32[]{:S(2)}) collective-permute-start(f32[3,32,128]{2,1,0:T(8,128)S(1)} %dynamic-slice_bitcast_fusion), channel_id=1, source_target_pairs={{0,4},{4,0},{2,6},{6,2},{8,12},{12,8},{10,14},{14,10},{16,20},{20,... | collective-permute-start | bytes 147464 | tf_op jit(solution)/shard_map/ppermute | solution.py:19
  63.8 3.4 %collective-permute-start.9 = (f32[3,32,64]{2,1,0:T(8,128)S(1)}, f32[3,32,64]{2,1,0:T(8,128)S(1)}, u32[]{:S(2)}, u32[]{:S(2)}) collective-permute-start(f32[3,32,64]{2,1,0:T(8,128)S(1)} %constant_dynamic-slice_fusion), channel_id=1, source_target_pairs={{0,2},{2,0},{4,6},{6,4},{8,10},{10,8},{12,14},{14,12},{16,18},{18,... | collective-permute-start | bytes 73736 | tf_op jit(solution)/shard_map/ppermute | solution.py:19
where the time goes:
time: 68.9 us; the launch traced here: 68.6 us
  waiting for transfers between devices  19.9 us (29%)
  blocking collectives  13.9 us (20%)
  starting transfers between devices  11.9 us (17%)
  matrix products  9.13 us (13%)
  other arithmetic  6.44 us (9%)
  between operations  5.44 us (8%)
  local copies, waits for them, and re-layouts  1.92 us (3%)
    ppermute x10, waiting for transfers between devices, from_partner(): return lax.ppermute(block, axis, route)  19.9 us
    all_gather x2, blocking collectives, grid_product(): sources = lax.all_gather(packed, 'tile', axis=2, tiled=True)  13.9 us
    ppermute x10, starting transfers between devices, from_partner(): return lax.ppermute(block, axis, route)  11.9 us
    dot_general x2, matrix products, contract(): jnp.einsum('abij,bkj->aki', tensor, vectors, precision=lax.Precision.HIGH...  9.13 us
    another operation x3, other arithmetic, body(): return (displacement, jnp.stack([first_image, second_image]))  1.45 us
    reduce_sum x2, other arithmetic, weights_from(): jnp.sum(samples * jnp.cos(order * angles))  1.4 us
  transfers between devices with their start and end apart: 10, of which 5 were waited for; matrix products, arithmetic and copies ran while one was open for 7% of the time, Pallas kernels for 0%

commit v1 on v0

v1 whole, which is shorter than its diff:
```python
import math

import jax
import jax.numpy as jnp
import numpy as np
from jax import lax
from jax.experimental import pallas as pl
from jax.experimental.pallas import tpu as pltpu
from jax.sharding import PartitionSpec as P

soft_core = 1e-06
node_count = 32
axes = ("blk", "tile")
pairs = ((0, 0), (0, 1), (0, 2), (1, 1), (1, 2), (2, 2))
f32 = jnp.float32
bf16 = jnp.bfloat16


def exchange(block, mask):
    count = lax.axis_size("blk") * lax.axis_size("tile")
    return lax.ppermute(block, axes, [(i, i ^ mask) for i in range(count)])


def pack_kernel(noise, positions, message):
    half = noise.shape[0] // 2
    message[0:half, :] = jnp.concatenate([noise[0:half, :], noise[half:, :]], axis=1)
    spot = positions[...]
    pad = jnp.zeros((8 - spot.shape[0], spot.shape[1]), f32)
    spot = jnp.concatenate([spot, pad], axis=0)
    message[half:, :] = jnp.concatenate([spot, spot], axis=1)


def halves(value):
    high = value.astype(bf16)
    return high, (value - high.astype(f32)).astype(bf16)


def unpack_pair(first, second, half):
    width = first.shape[1] // 2
    left = lax.broadcasted_iota(jnp.int32, (1, 2 * width), 1) < width
    first_rolled = pltpu.roll(first, width, 1)
    second_rolled = pltpu.roll(second, width, 1)
    upper = jnp.where(left, first, second_rolled)
    lower = jnp.where(left, first_rolled, second)
    return upper[:half], lower[:half], upper[half:]


def build_tiles(columns, target_rows, high, low):
    source_count = columns.shape[1]
    tile_count = target_rows.shape[1] // 128
    chunk = 16

    def one_chunk(step, carry):
        start = pl.multiple_of(step * chunk, chunk)
        source = [columns[c, pl.ds(start, chunk), :] for c in range(3)]
        for tile in range(tile_count):
            lanes = slice(tile * 128, (tile + 1) * 128)
            offset = [source[c] - target_rows[c : c + 1, lanes] for c in range(3)]
            squared = offset[0] * offset[0] + offset[1] * offset[1] + offset[2] * offset[2]
            squared = squared + soft_core
            inverse = lax.rsqrt(squared)
            distance = squared * inverse
            inverse_squared = inverse * inverse
            cubed = inverse * inverse_squared
            near = distance < 2.0
            scalar = jnp.where(near, 1.0 - 0.28125 * distance, 0.75 * inverse + 0.5 * cubed)
            dyadic = jnp.where(near, 0.09375 * inverse, cubed * (0.75 - 1.5 * inverse_squared))
            scaled = [dyadic * offset[c] for c in range(3)]
            for number, (a, b) in enumerate(pairs):
                value = scaled[a] * offset[b]
                if a == b:
                    value = value + scalar
                top, rest = halves(value)
                high[number, pl.ds(start, chunk), lanes] = top
                low[number, pl.ds(start, chunk), lanes] = rest
        return carry

    lax.fori_loop(0, source_count // chunk, one_chunk, 0)


def fill_columns(columns, rows):
    for c in range(3):
        for tile in range(rows.shape[1] // 128):
            lanes = slice(tile * 128, (tile + 1) * 128)
            wide = jnp.broadcast_to(rows[c : c + 1, lanes], (128, 128))
            columns[c, lanes, :] = wide.T


def apply_tiles(field, high, low):
    count = field[0].shape[0]
    parts = [halves(value) for value in field]
    both = [jnp.concatenate(part, axis=0) for part in parts]
    result = [None, None, None]

    def add(component, value):
        result[component] = value if result[component] is None else result[component] + value

    def dot(left, right):
        return jnp.dot(left, right, preferred_element_type=f32)

    for number, (a, b) in enumerate(pairs):
        if a == b:
            product = dot(both[a], high[number])
            add(a, product[:count] + product[count:])
            add(a, dot(parts[a][0], low[number]))
        else:
            product = dot(jnp.concatenate([both[a], both[b]], axis=0), high[number])
            add(b, product[:count] + product[count : 2 * count])
            add(a, product[2 * count : 3 * count] + product[3 * count :])
            product = dot(jnp.concatenate([parts[a][0], parts[b][0]], axis=0), low[number])
            add(b, product[:count])
            add(a, product[count:])
    return result


def first_kernel(bounds, blocks, near_positions, noise, partial, message, columns, rows, high, low):
    half = noise.shape[0] // 2
    vectors = noise.shape[0] // 3
    width = noise.shape[1]
    count = blocks.shape[0]
    uppers, lowers = [], []
    for number in range(0, count, 2):
        upper, lower, spots = unpack_pair(blocks[number], blocks[number + 1], half)
        uppers.append(upper)
        lowers.append(lower)
        rows[:, number * width : (number + 2) * width] = spots
    fill_columns(columns, rows)
    build_tiles(columns, near_positions, high, low)
    field = jnp.concatenate([jnp.concatenate(uppers, axis=1), jnp.concatenate(lowers, axis=1)], axis=0)
    field = [field[c * vectors : (c + 1) * vectors] for c in range(3)]
    value = jnp.concatenate(apply_tiles(field, high, low), axis=0)
    partial[...] = value
    message[...] = value
    center = 0.5 * (bounds[1] + bounds[0])
    message[:, :width] = value[:, :width] - center * noise[...]


def second_kernel(near_positions, blocks, bounds, nodes, high, low, weights, columns, rows):
    half = blocks.shape[1] - 8
    width = blocks.shape[2] // 2
    for number in range(0, blocks.shape[0], 2):
        spots = unpack_pair(blocks[number], blocks[number + 1], half)[2]
        rows[:, number * width : (number + 2) * width] = spots
    fill_columns(columns, near_positions)
    build_tiles(columns, rows, high, low)
    center = 0.5 * (bounds[1] + bounds[0])
    spread = 0.5 * (bounds[1] - bounds[0])
    samples = jnp.sqrt(jnp.where(nodes[3:4, :] > 0.0, center + spread * nodes[1:2, :], 0.0))
    total = jnp.sum(samples * nodes[...], axis=1, keepdims=True)
    weights[...] = jnp.broadcast_to((2.0 / node_count) * total, weights.shape)


def swapped(value, offset, width):
    count = value.shape[1] // width
    if offset == 0:
        return value
    tiles = [value[:, 128 * t : 128 * (t + 1)] for t in range(count * width // 128)]
    per_tile = 128 // width
    inner, outer = offset % per_tile, offset // per_tile
    tiles = [tiles[t ^ outer] for t in range(len(tiles))]
    if inner:
        tiles = [pltpu.roll(tile, width, 1) for tile in tiles]
    return tiles[0] if len(tiles) == 1 else jnp.concatenate(tiles, axis=1)


def third_kernel(bounds, *refs):
    received = refs[:-7]
    partial, message, high, low, first_image, kept, sent = refs[-7:]
    rows_count = partial.shape[0]
    width = first_image.shape[1]
    vectors = rows_count // 3
    spread = 0.5 * (bounds[1] - bounds[0])
    total = message[...]
    own = partial[:, :width]
    for number, ref in enumerate(received):
        part = swapped(ref[...], number + 1, width)
        total = total + part
        own = own + part[:, :width]
    first_image[...] = own
    linear = total / spread
    field = [linear[c * vectors : (c + 1) * vectors] for c in range(3)]
    value = jnp.concatenate(apply_tiles(field, high, low), axis=0)
    middle = value.shape[1] // 2
    kept[...] = value[:, :middle]
    sent[...] = value[:, middle:]


def fourth_kernel(kept, arrived, own, *outgoing):
    half = kept.shape[0] // 2
    width = own.shape[1] // 2
    total = kept[...] + arrived[...]
    for number, ref in enumerate((own, *outgoing)):
        block = total[:, number * width : (number + 1) * width]
        ref[...] = jnp.concatenate([block[:half], block[half:]], axis=1)


def final_kernel(bounds, weights, noise, first_image, own, *refs):
    received, (displacement, images) = refs[:-2], refs[-2:]
    width = noise.shape[1]
    total = own[...]
    for ref in received:
        total = total + ref[...]
    second = jnp.concatenate([total[:, :width], total[:, width:]], axis=0)
    center = 0.5 * (bounds[1] + bounds[0])
    spread = 0.5 * (bounds[1] - bounds[0])
    vectors = noise[...]
    first = first_image[...]
    linear = (first - center * vectors) / spread
    quadratic = 2.0 * (second - center * linear) / spread - vectors
    displacement[...] = (
        0.5 * weights[0:1, :width] * vectors
        + weights[1:2, :width] * linear
        + weights[2:3, :width] * quadratic
    )
    images[0] = first
    images[1] = second


smem = pl.BlockSpec(memory_space=pltpu.SMEM)
vmem = pl.BlockSpec(memory_space=pltpu.VMEM)


def call(kernel, inputs, in_specs, outputs, scratch=()):
    return pl.pallas_call(
        kernel,
        in_specs=in_specs,
        out_shape=[jax.ShapeDtypeStruct(shape, dtype) for shape, dtype in outputs],
        out_specs=[vmem] * len(outputs),
        scratch_shapes=list(scratch),
    )(*inputs)


def node_table():
    angles = math.pi * (np.arange(node_count) + 0.5) / node_count
    table = np.zeros((8, 128), np.float32)
    for order in range(3):
        table[order, :node_count] = np.cos(order * angles)
    table[3, :node_count] = 1.0
    return table


def combinations(masks):
    result = [0]
    for mask in masks:
        result += [value ^ mask for value in result]
    return result


def body(positions, noise_vectors, spectrum_bounds):
    tiles = lax.axis_size("tile")
    bits = lax.axis_size("blk").bit_length() - 1
    half_bits = bits // 2
    core_mask = tiles
    far_masks = [tiles << bit for bit in reversed(range(half_bits, bits))]
    near_masks = [1 << bit for bit in range(tiles.bit_length() - 1)]
    near_masks += [tiles << bit for bit in range(1, half_bits)]
    components, vectors, width = noise_vectors.shape
    rows = components * vectors
    noise = noise_vectors.reshape(rows, width)
    bounds = spectrum_bounds

    (packed,) = call(
        pack_kernel, (noise, positions), [vmem, vmem], [((rows // 2 + 8, 2 * width), f32)]
    )
    far = packed[None]
    near = positions
    for mask in far_masks:
        far = jnp.concatenate([far, exchange(far, mask)], axis=0)
    for mask in near_masks:
        near = jnp.concatenate([near, exchange(near, mask)], axis=1)
    blocks = jnp.concatenate([far, exchange(far, core_mask)], axis=0)
    near_count, far_count = near.shape[1], blocks.shape[0] * width

    partial, message = call(
        first_kernel,
        (bounds, blocks, near, noise),
        [smem, vmem, vmem, vmem],
        [((rows, near_count), f32)] * 2,
        (
            pltpu.VMEM((3, far_count, 128), f32),
            pltpu.VMEM((8, far_count), f32),
            pltpu.VMEM((6, far_count, near_count), bf16),
            pltpu.VMEM((6, far_count, near_count), bf16),
        ),
    )
    high, low, weights = call(
        second_kernel,
        (near, blocks, bounds, jnp.asarray(node_table())),
        [vmem, vmem, smem, vmem],
        [((6, near_count, far_count), bf16)] * 2 + [((8, 128), f32)],
        (pltpu.VMEM((3, near_count, 128), f32), pltpu.VMEM((8, far_count), f32)),
    )
    received = [exchange(message, mask) for mask in combinations(near_masks)[1:]]
    first_image, kept, sent = call(
        third_kernel,
        (bounds, *received, partial, message, high, low),
        [smem] + [vmem] * (len(received) + 4),
        [((rows, width), f32), ((rows, far_count // 2), f32), ((rows, far_count // 2), f32)],
    )
    arrived = exchange(sent, core_mask)
    far_steps = combinations(far_masks)
    own, *outgoing = call(
        fourth_kernel,
        (kept, arrived),
        [vmem, vmem],
        [((rows // 2, 2 * width), f32)] * len(far_steps),
    )
    received = [exchange(block, mask) for block, mask in zip(outgoing, far_steps[1:])]
    displacement, images = call(
        final_kernel,
        (bounds, weights, noise, first_image, own, *received),
        [smem] + [vmem] * (4 + len(received)),
        [((rows, width), f32), ((2, rows, width), f32)],
    )
    shape = noise_vectors.shape
    return displacement.reshape(shape), images.reshape((2, *shape))


def solution(mesh):
    return jax.shard_map(
        body,
        mesh=mesh,
        in_specs=(P(None, axes), P(None, None, axes), P()),
        out_specs=(P(None, None, axes), P(None, None, None, axes)),
        check_vma=False,
    )
```

time: 68.9 us -> 55.2 us (0.80)
  Pallas kernels: 0 us -> 16.4 us
  blocking collectives: 13.9 us -> 0 us
  matrix products: 9.13 us -> 0 us
  waiting for transfers between devices: 19.9 us -> 13.7 us
  starting transfers between devices: 11.9 us -> 16.9 us
  between operations: 5.44 us -> 0.67 us
  other arithmetic: 6.44 us -> 5.06 us
    pallas_call x0 -> x6, Pallas kernels: none -> 16.4 us  [call(): pl.pallas_call(kernel, in_specs=in_specs, out_shape=[jax.ShapeDtypeStruct...]
    all_gather x2 -> x0, blocking collectives: 13.9 us -> none  [grid_product(): sources = lax.all_gather(packed, 'tile', axis=2, tiled=True)]
    dot_general x2 -> x0, matrix products: 9.13 us -> none  [contract(): jnp.einsum('abij,bkj->aki', tensor, vectors, precision=lax.Precision.HIGH...]
    ppermute x10 -> x12, waiting for transfers between devices: 19.9 us -> 13.7 us  [exchange(): return lax.ppermute(block, axes, [(i, i ^ mask) for i in range(count)])]
    ppermute x10 -> x12, starting transfers between devices: 11.9 us -> 16.9 us  [exchange(): return lax.ppermute(block, axes, [(i, i ^ mask) for i in range(count)])]
    concatenate x6 -> x5, other arithmetic: 0.89 us -> 5.06 us  [the longest x2 2.1 us: body(): near = jnp.concatenate([near, exchange(near, mask)], axis=1)]
    unnamed x6 -> x14, local copies, waits for them, and re-layouts: 0.02 us -> 1.89 us
    reduce_sum x4 -> x0, other arithmetic: 1.83 us -> none  [the longest x2 1.4 us: weights_from(): jnp.sum(samples * jnp.cos(order * angles))]
  transfers between devices with their start and end apart: 10 -> 12, of which waited for: 5 -> 9; matrix products, arithmetic and copies ran while one was open for 7% -> 5% of each run, Pallas kernels for 0% -> 8%
where the time goes in v1:
time: 55.2 us; the launch traced here: 54.6 us
  starting transfers between devices  16.9 us (31%)
  Pallas kernels  16.4 us (30%)
  waiting for transfers between devices  13.7 us (25%)
  other arithmetic  5.06 us (9%)
  local copies, waits for them, and re-layouts  1.89 us (3%)
  between operations  0.67 us (1%)
    ppermute x12, starting transfers between devices, exchange(): return lax.ppermute(block, axes, [(i, i ^ mask) for i in range(count)])  16.9 us
    pallas_call x6, Pallas kernels, call(): pl.pallas_call(kernel, in_specs=in_specs, out_shape=[jax.ShapeDtypeStruct...  16.4 us
    ppermute x12, waiting for transfers between devices, exchange(): return lax.ppermute(block, axes, [(i, i ^ mask) for i in range(count)])  13.7 us
    concatenate x2, other arithmetic, body(): near = jnp.concatenate([near, exchange(near, mask)], axis=1)  2.1 us
    unnamed x14, local copies, waits for them, and re-layouts  1.89 us
    concatenate x2, other arithmetic, body(): far = jnp.concatenate([far, exchange(far, mask)], axis=0)  1.51 us
    concatenate x1, other arithmetic, body(): blocks = jnp.concatenate([far, exchange(far, core_mask)], axis=0)  1.45 us
  transfers between devices with their start and end apart: 12, of which 9 were waited for; matrix products, arithmetic and copies ran while one was open for 5% of the time, Pallas kernels for 8%

profile of v1, /device:TPU:0, one launch (start us, length us, event | category | flops | bytes accessed | tf_op | source)
XLA Modules:
  0.0 54.6 jit_solution(17604167523730915367)
XLA Ops:
  0.6 1.5 %shard_map.59 = f32[56,128]{1,0:T(8,128)} custom-call(f32[96,64]{1,0:T(8,128)} %bitcast.8, f32[3,64]{1,0:T(4,128)} %positions.1), custom_call_target="tpu_custom_call" | custom-call | tf_op jit(solution)/shard_map/pallas_call | solution.py:224
  2.1 4.1 %collective-permute-start.2 = (f32[1,56,128]{2,1,0:T(8,128)}, f32[1,56,128]{2,1,0:T(8,128)S(1)}, u32[]{:S(2)}, u32[]{:S(2)}) collective-permute-start(f32[1,56,128]{2,1,0:T(8,128)} %bitcast.4), channel_id=1, source_target_pairs={{0,16},{1,17},{2,18},{3,19},{4,20},{5,21},{6,22},{7,23},{8,24},{9,... | collective-permute-start | bytes 86024 | tf_op jit(solution)/shard_map/ppermute | solution.py:21
  6.2 2.1 %collective-permute-done.2 = f32[1,56,128]{2,1,0:T(8,128)S(1)} collective-permute-done((f32[1,56,128]{2,1,0:T(8,128)}, f32[1,56,128]{2,1,0:T(8,128)S(1)}, u32[]{:S(2)}, u32[]{:S(2)}) %collective-permute-start.2) | collective-permute-done | bytes 28704 | tf_op jit(solution)/shard_map/ppermute | solution.py:21
  8.2 0.8 %pad_maximum_fusion.2 = f32[2,56,128]{2,1,0:T(8,128)S(1)} fusion(f32[1,56,128]{2,1,0:T(8,128)S(1)} %collective-permute-done.2, f32[1,56,128]{2,1,0:T(8,128)} %bitcast.5), kind=kLoop, calls=%fused_computation.2 | loop fusion | flops 14336 | bytes 114688 | tf_op jit(solution)/shard_map/concatenate | solution.py:268
  9.0 1.9 %collective-permute-start.3 = (f32[2,56,128]{2,1,0:T(8,128)S(1)}, f32[2,56,128]{2,1,0:T(8,128)S(1)}, u32[]{:S(2)}, u32[]{:S(2)}) collective-permute-start(f32[2,56,128]{2,1,0:T(8,128)S(1)} %pad_maximum_fusion.2), channel_id=1, source_target_pairs={{0,8},{1,9},{2,10},{3,11},{4,12},{5,13},{6,14},{7,15},{8,0},{9,1},... | collective-permute-start | bytes 172040 | tf_op jit(solution)/shard_map/ppermute | solution.py:21
  10.9 1.5 %collective-permute-start = (f32[3,64]{1,0:T(4,128)}, f32[3,64]{1,0:T(4,128)S(1)}, u32[]{:S(2)}, u32[]{:S(2)}) collective-permute-start(f32[3,64]{1,0:T(4,128)} %positions.1), channel_id=1, source_target_pairs={{0,1},{1,0},{2,3},{3,2},{4,5},{5,4},{6,7},{7,6},{8,9},{9,8},{10,11... | collective-permute-start | bytes 2312 | tf_op jit(solution)/shard_map/ppermute | solution.py:21
  12.4 0.8 %collective-permute-done.3 = f32[2,56,128]{2,1,0:T(8,128)S(1)} collective-permute-done((f32[2,56,128]{2,1,0:T(8,128)S(1)}, f32[2,56,128]{2,1,0:T(8,128)S(1)}, u32[]{:S(2)}, u32[]{:S(2)}) %collective-permute-start.3) | collective-permute-done | bytes 57376 | tf_op jit(solution)/shard_map/ppermute | solution.py:21
  13.2 0.8 %pad_maximum_fusion.1 = f32[4,56,128]{2,1,0:T(8,128)S(1)} fusion(f32[2,56,128]{2,1,0:T(8,128)S(1)} %collective-permute-done.3, f32[1,56,128]{2,1,0:T(8,128)S(1)} %collective-permute-done.2, f32[1,56,128]{2,1,0:T(8,128)} %bitcast.6), kind=kLoop, calls=%fused_computation.1 | loop fusion | flops 57344 | bytes 229376 | tf_op jit(solution)/shard_map/concatenate | solution.py:268
  13.9 0.1 collective-permute-start.4
  14.0 0.7 %collective-permute-done = f32[3,64]{1,0:T(4,128)S(1)} collective-permute-done((f32[3,64]{1,0:T(4,128)}, f32[3,64]{1,0:T(4,128)S(1)}, u32[]{:S(2)}, u32[]{:S(2)}) %collective-permute-start) | collective-permute-done | bytes 800 | tf_op jit(solution)/shard_map/ppermute | solution.py:21
  14.7 0.8 %pad_maximum_fusion.4 = f32[3,128]{1,0:T(4,128)S(1)} fusion(f32[3,64]{1,0:T(4,128)S(1)} %collective-permute-done, f32[3,64]{1,0:T(4,128)} %positions.1), kind=kLoop, calls=%fused_computation.4 | loop fusion | flops 384 | bytes 3072 | tf_op jit(solution)/shard_map/concatenate | solution.py:270
  15.5 1.5 %collective-permute-start.1 = (f32[3,128]{1,0:T(4,128)S(1)}, f32[3,128]{1,0:T(4,128)S(1)}, u32[]{:S(2)}, u32[]{:S(2)}) collective-permute-start(f32[3,128]{1,0:T(4,128)S(1)} %pad_maximum_fusion.4), channel_id=1, source_target_pairs={{0,4},{1,5},{2,6},{3,7},{4,0},{5,1},{6,2},{7,3},{8,12},{9,13},{10,... | collective-permute-start | bytes 4616 | tf_op jit(solution)/shard_map/ppermute | solution.py:21
  17.0 2.1 %collective-permute-done.1 = f32[3,128]{1,0:T(4,128)S(1)} collective-permute-done((f32[3,128]{1,0:T(4,128)S(1)}, f32[3,128]{1,0:T(4,128)S(1)}, u32[]{:S(2)}, u32[]{:S(2)}) %collective-permute-start.1) | collective-permute-done | bytes 1568 | tf_op jit(solution)/shard_map/ppermute | solution.py:21
  19.0 1.3 %pad_maximum_fusion.3.near_positions = f32[3,256]{1,0:T(4,128)} fusion(f32[3,128]{1,0:T(4,128)S(1)} %collective-permute-done.1, f32[3,64]{1,0:T(4,128)S(1)} %collective-permute-done, f32[3,64]{1,0:T(4,128)} %positions.1), kind=kLoop, calls=%fused_computation.3 | loop fusion | flops 1536 | bytes 6144 | tf_op jit(solution)/shard_map/concatenate | solution.py:270
  20.4 0.0 collective-permute-done.4
  20.4 1.5 %pad_maximum_fusion.blocks = f32[8,56,128]{2,1,0:T(8,128)} fusion(f32[4,56,128]{2,1,0:T(8,128)S(1)} %collective-permute-done.4, f32[2,56,128]{2,1,0:T(8,128)S(1)} %collective-permute-done.3, f32[1,56,128]{2,1,0:T(8,128)S(1)} %collective-permute-done.2, f32[1,56,128]{2,1,0:T(8,128)} %bitcast.7), kind=kLoop, calls=%fused_computation | loop fusion | flops 172032 | bytes 458752 | tf_op jit(solution)/shard_map/concatenate | solution.py:271
  21.8 4.1 %shard_map.61 = (f32[96,256]{1,0:T(8,128)}, f32[96,256]{1,0:T(8,128)}) custom-call(f32[2]{0:T(128)} %bounds.7, f32[8,56,128]{2,1,0:T(8,128)} %pad_maximum_fusion.blocks, f32[3,256]{1,0:T(4,128)} %pad_maximum_fusion.3.near_positions, f32[96,64]{1,0:T(8,128)} %bitcast.9), custom_call_target="tpu_custom_call" | custom-call | tf_op jit(solution)/shard_map/pallas_call | solution.py:224
  26.0 1.5 %collective-permute-start.5 = (f32[96,256]{1,0:T(8,128)}, f32[96,256]{1,0:T(8,128)S(1)}, u32[]{:S(2)}, u32[]{:S(2)}) collective-permute-start(f32[96,256]{1,0:T(8,128)} %get-tuple-element.17.refs_4_), channel_id=1, source_target_pairs={{0,1},{1,0},{2,3},{3,2},{4,5},{5,4},{6,7},{7,6},{8,9},{9,8},{10,11... | collective-permute-start | bytes 294920 | tf_op jit(solution)/shard_map/ppermute | solution.py:21
  27.5 1.5 %collective-permute-start.6 = (f32[96,256]{1,0:T(8,128)}, f32[96,256]{1,0:T(8,128)S(1)}, u32[]{:S(2)}, u32[]{:S(2)}) collective-permute-start(f32[96,256]{1,0:T(8,128)} %get-tuple-element.17.refs_4_), channel_id=1, source_target_pairs={{0,4},{1,5},{2,6},{3,7},{4,0},{5,1},{6,2},{7,3},{8,12},{9,13},{10,... | collective-permute-start | bytes 294920 | tf_op jit(solution)/shard_map/ppermute | solution.py:21
  29.0 0.5 collective-permute-start.7
  29.5 4.1 %shard_map.60 = (bf16[6,256,512]{2,1,0:T(8,128)(2,1)}, bf16[6,256,512]{2,1,0:T(8,128)(2,1)}, f32[8,128]{1,0:T(8,128)}) custom-call(f32[3,256]{1,0:T(4,128)} %pad_maximum_fusion.3.near_positions, f32[8,56,128]{2,1,0:T(8,128)} %pad_maximum_fusion.blocks, f32[2]{0:T(128)} %bounds.7, f32[8,128]{1,0:T(8,128)} %constant.2.clone.nodes), custom_call_target="tpu_custom_call" | custom-call | tf_op jit(solution)/shard_map/pallas_call | solution.py:224
  33.6 0.0 collective-permute-done.5.refs_0_
  33.6 0.0 copy-start.1
  33.6 0.0 collective-permute-done.6.refs_1_
  33.6 0.0 copy-start.2
  33.6 1.1 %collective-permute-done.7.refs_2_ = f32[96,256]{1,0:T(8,128)S(1)} collective-permute-done((f32[96,256]{1,0:T(8,128)}, f32[96,256]{1,0:T(8,128)S(1)}, u32[]{:S(2)}, u32[]{:S(2)}) %collective-permute-start.7) | collective-permute-done | bytes 98336 | tf_op jit(solution)/shard_map/ppermute | solution.py:21
  34.7 0.0 copy-done.1
  34.7 0.0 copy-done.2
  34.7 0.6 %copy-done.3 = f32[96,256]{1,0:T(8,128)} copy-done((f32[96,256]{1,0:T(8,128)}, f32[96,256]{1,0:T(8,128)S(1)}, u32[]{:S(2)}) %copy-start.3) | copy-done | bytes 98328
  35.3 3.4 %shard_map.62 = (f32[96,64]{1,0:T(8,128)}, f32[96,256]{1,0:T(8,128)}, f32[96,256]{1,0:T(8,128)}) custom-call(f32[2]{0:T(128)} %bounds.7, f32[96,256]{1,0:T(8,128)} %copy-done.1, f32[96,256]{1,0:T(8,128)} %copy-done.2, f32[96,256]{1,0:T(8,128)} %copy-done.3, f32[96,256]{1,0:T(8,128)} %get-tuple-element.18.refs_3_, f32[96,256]{1,0:T(8,128)} %get-tuple-element.17.refs_4_, ...), custom_call_target="tpu_custom_call" | custom-call | tf_op jit(solution)/shard_map/pallas_call | solution.py:224
  38.8 0.0 collective-permute-start.8
  38.8 1.5 %collective-permute-done.8.arrived = f32[96,256]{1,0:T(8,128)S(1)} collective-permute-done((f32[96,256]{1,0:T(8,128)}, f32[96,256]{1,0:T(8,128)S(1)}, u32[]{:S(2)}, u32[]{:S(2)}) %collective-permute-start.8) | collective-permute-done | bytes 98336 | tf_op jit(solution)/shard_map/ppermute | solution.py:21
  40.3 0.0 copy-start
  40.3 0.6 %copy-done = f32[96,256]{1,0:T(8,128)} copy-done((f32[96,256]{1,0:T(8,128)}, f32[96,256]{1,0:T(8,128)S(1)}, u32[]{:S(2)}) %copy-start) | copy-done | bytes 98328
  40.9 1.6 %shard_map.63 = (f32[48,128]{1,0:T(8,128)}, f32[48,128]{1,0:T(8,128)}, f32[48,128]{1,0:T(8,128)}, f32[48,128]{1,0:T(8,128)}) custom-call(f32[96,256]{1,0:T(8,128)} %get-tuple-element.22.kept, f32[96,256]{1,0:T(8,128)} %copy-done), custom_call_target="tpu_custom_call" | custom-call | tf_op jit(solution)/shard_map/pallas_call | solution.py:224
  42.6 2.8 %collective-permute-start.9 = (f32[48,128]{1,0:T(8,128)}, f32[48,128]{1,0:T(8,128)S(1)}, u32[]{:S(2)}, u32[]{:S(2)}) collective-permute-start(f32[48,128]{1,0:T(8,128)} %get-tuple-element.25), channel_id=1, source_target_pairs={{0,16},{1,17},{2,18},{3,19},{4,20},{5,21},{6,22},{7,23},{8,24},{9,... | collective-permute-start | bytes 73736 | tf_op jit(solution)/shard_map/ppermute | solution.py:21
  45.4 1.2 %collective-permute-start.10 = (f32[48,128]{1,0:T(8,128)}, f32[48,128]{1,0:T(8,128)S(1)}, u32[]{:S(2)}, u32[]{:S(2)}) collective-permute-start(f32[48,128]{1,0:T(8,128)} %get-tuple-element.26), channel_id=1, source_target_pairs={{0,8},{1,9},{2,10},{3,11},{4,12},{5,13},{6,14},{7,15},{8,0},{9,1},... | collective-permute-start | bytes 73736 | tf_op jit(solution)/shard_map/ppermute | solution.py:21
  46.6 0.4 collective-permute-start.11
  47.0 0.8 %collective-permute-done.9.refs_0_ = f32[48,128]{1,0:T(8,128)S(1)} collective-permute-done((f32[48,128]{1,0:T(8,128)}, f32[48,128]{1,0:T(8,128)S(1)}, u32[]{:S(2)}, u32[]{:S(2)}) %collective-permute-start.9) | collective-permute-done | bytes 24608 | tf_op jit(solution)/shard_map/ppermute | solution.py:21
  47.8 0.0 copy-start.4
  47.8 1.6 %collective-permute-done.10.refs_1_ = f32[48,128]{1,0:T(8,128)S(1)} collective-permute-done((f32[48,128]{1,0:T(8,128)}, f32[48,128]{1,0:T(8,128)S(1)}, u32[]{:S(2)}, u32[]{:S(2)}) %collective-permute-start.10) | collective-permute-done | bytes 24608 | tf_op jit(solution)/shard_map/ppermute | solution.py:21
  49.4 0.0 copy-start.5
  49.4 3.0 %collective-permute-done.11.refs_2_ = f32[48,128]{1,0:T(8,128)S(1)} collective-permute-done((f32[48,128]{1,0:T(8,128)}, f32[48,128]{1,0:T(8,128)S(1)}, u32[]{:S(2)}, u32[]{:S(2)}) %collective-permute-start.11) | collective-permute-done | bytes 24608 | tf_op jit(solution)/shard_map/ppermute | solution.py:21
  52.4 0.0 copy-start.6
  52.4 0.0 copy-done.4
  52.4 0.0 copy-done.5
  52.4 0.6 %copy-done.6 = f32[48,128]{1,0:T(8,128)} copy-done((f32[48,128]{1,0:T(8,128)}, f32[48,128]{1,0:T(8,128)S(1)}, u32[]{:S(2)}) %copy-start.6) | copy-done | bytes 24600
  53.0 1.6 %shard_map.64 = (f32[96,64]{1,0:T(8,128)}, f32[2,96,64]{2,1,0:T(8,128)}) custom-call(f32[2]{0:T(128)} %bounds.7, f32[8,128]{1,0:T(8,128)} %get-tuple-element.16.weights, f32[96,64]{1,0:T(8,128)} %bitcast.10, f32[96,64]{1,0:T(8,128)} %get-tuple-element.21.first_image, f32[48,128]{1,0:T(8,128)} %get-tuple-element.24.own, f32[48,128]{1,0:T(8,128)} %copy-done.4, ...), custom_call_target="tpu_custom_call" | custom-call | tf_op jit(solution)/shard_map/pallas_call | solution.py:224
  (1 shorter events, 0.0 us)
Async XLA Ops:
  2.1 6.1 %collective-permute-start.2 = (f32[1,56,128]{2,1,0:T(8,128)}, f32[1,56,128]{2,1,0:T(8,128)S(1)}, u32[]{:S(2)}, u32[]{:S(2)}) collective-permute-start(f32[1,56,128]{2,1,0:T(8,128)} %bitcast.4), channel_id=1, source_target_pairs={{0,16},{1,17},{2,18},{3,19},{4,20},{5,21},{6,22},{7,23},{8,24},{9,... | collective-permute-start | bytes 86024 | tf_op jit(solution)/shard_map/ppermute | solution.py:21
  9.0 4.2 %collective-permute-start.3 = (f32[2,56,128]{2,1,0:T(8,128)S(1)}, f32[2,56,128]{2,1,0:T(8,128)S(1)}, u32[]{:S(2)}, u32[]{:S(2)}) collective-permute-start(f32[2,56,128]{2,1,0:T(8,128)S(1)} %pad_maximum_fusion.2), channel_id=1, source_target_pairs={{0,8},{1,9},{2,10},{3,11},{4,12},{5,13},{6,14},{7,15},{8,0},{9,1},... | collective-permute-start | bytes 172040 | tf_op jit(solution)/shard_map/ppermute | solution.py:21
  10.9 3.8 %collective-permute-start = (f32[3,64]{1,0:T(4,128)}, f32[3,64]{1,0:T(4,128)S(1)}, u32[]{:S(2)}, u32[]{:S(2)}) collective-permute-start(f32[3,64]{1,0:T(4,128)} %positions.1), channel_id=1, source_target_pairs={{0,1},{1,0},{2,3},{3,2},{4,5},{5,4},{6,7},{7,6},{8,9},{9,8},{10,11... | collective-permute-start | bytes 2312 | tf_op jit(solution)/shard_map/ppermute | solution.py:21
  13.9 6.4 %collective-permute-start.4 = (f32[4,56,128]{2,1,0:T(8,128)S(1)}, f32[4,56,128]{2,1,0:T(8,128)S(1)}, u32[]{:S(2)}, u32[]{:S(2)}) collective-permute-start(f32[4,56,128]{2,1,0:T(8,128)S(1)} %pad_maximum_fusion.1), channel_id=1, source_target_pairs={{0,2},{1,3},{2,0},{3,1},{4,6},{5,7},{6,4},{7,5},{8,10},{9,11},{10,... | collective-permute-start | bytes 344072 | tf_op jit(solution)/shard_map/ppermute | solution.py:21
  15.5 3.6 %collective-permute-start.1 = (f32[3,128]{1,0:T(4,128)S(1)}, f32[3,128]{1,0:T(4,128)S(1)}, u32[]{:S(2)}, u32[]{:S(2)}) collective-permute-start(f32[3,128]{1,0:T(4,128)S(1)} %pad_maximum_fusion.4), channel_id=1, source_target_pairs={{0,4},{1,5},{2,6},{3,7},{4,0},{5,1},{6,2},{7,3},{8,12},{9,13},{10,... | collective-permute-start | bytes 4616 | tf_op jit(solution)/shard_map/ppermute | solution.py:21
  26.0 7.6 %collective-permute-start.5 = (f32[96,256]{1,0:T(8,128)}, f32[96,256]{1,0:T(8,128)S(1)}, u32[]{:S(2)}, u32[]{:S(2)}) collective-permute-start(f32[96,256]{1,0:T(8,128)} %get-tuple-element.17.refs_4_), channel_id=1, source_target_pairs={{0,1},{1,0},{2,3},{3,2},{4,5},{5,4},{6,7},{7,6},{8,9},{9,8},{10,11... | collective-permute-start | bytes 294920 | tf_op jit(solution)/shard_map/ppermute | solution.py:21
  27.5 6.1 %collective-permute-start.6 = (f32[96,256]{1,0:T(8,128)}, f32[96,256]{1,0:T(8,128)S(1)}, u32[]{:S(2)}, u32[]{:S(2)}) collective-permute-start(f32[96,256]{1,0:T(8,128)} %get-tuple-element.17.refs_4_), channel_id=1, source_target_pairs={{0,4},{1,5},{2,6},{3,7},{4,0},{5,1},{6,2},{7,3},{8,12},{9,13},{10,... | collective-permute-start | bytes 294920 | tf_op jit(solution)/shard_map/ppermute | solution.py:21
  29.0 5.7 %collective-permute-start.7 = (f32[96,256]{1,0:T(8,128)}, f32[96,256]{1,0:T(8,128)S(1)}, u32[]{:S(2)}, u32[]{:S(2)}) collective-permute-start(f32[96,256]{1,0:T(8,128)} %get-tuple-element.17.refs_4_), channel_id=1, source_target_pairs={{0,5},{1,4},{2,7},{3,6},{4,1},{5,0},{6,3},{7,2},{8,13},{9,12},{10,... | collective-permute-start | bytes 294920 | tf_op jit(solution)/shard_map/ppermute | solution.py:21
  33.6 1.1 %copy-start.1 = (f32[96,256]{1,0:T(8,128)}, f32[96,256]{1,0:T(8,128)S(1)}, u32[]{:S(2)}) copy-start(f32[96,256]{1,0:T(8,128)S(1)} %collective-permute-done.5.refs_0_) | copy-start | bytes 294916
  33.6 1.1 %copy-start.2 = (f32[96,256]{1,0:T(8,128)}, f32[96,256]{1,0:T(8,128)S(1)}, u32[]{:S(2)}) copy-start(f32[96,256]{1,0:T(8,128)S(1)} %collective-permute-done.6.refs_1_) | copy-start | bytes 294916
  34.7 0.6 %copy-start.3 = (f32[96,256]{1,0:T(8,128)}, f32[96,256]{1,0:T(8,128)S(1)}, u32[]{:S(2)}) copy-start(f32[96,256]{1,0:T(8,128)S(1)} %collective-permute-done.7.refs_2_) | copy-start | bytes 294916
  38.8 1.5 %collective-permute-start.8 = (f32[96,256]{1,0:T(8,128)}, f32[96,256]{1,0:T(8,128)S(1)}, u32[]{:S(2)}, u32[]{:S(2)}) collective-permute-start(f32[96,256]{1,0:T(8,128)} %get-tuple-element.23), channel_id=1, source_target_pairs={{0,2},{1,3},{2,0},{3,1},{4,6},{5,7},{6,4},{7,5},{8,10},{9,11},{10,... | collective-permute-start | bytes 294920 | tf_op jit(solution)/shard_map/ppermute | solution.py:21
  40.3 0.6 %copy-start = (f32[96,256]{1,0:T(8,128)}, f32[96,256]{1,0:T(8,128)S(1)}, u32[]{:S(2)}) copy-start(f32[96,256]{1,0:T(8,128)S(1)} %collective-permute-done.8.arrived) | copy-start | bytes 294916
  42.6 5.2 %collective-permute-start.9 = (f32[48,128]{1,0:T(8,128)}, f32[48,128]{1,0:T(8,128)S(1)}, u32[]{:S(2)}, u32[]{:S(2)}) collective-permute-start(f32[48,128]{1,0:T(8,128)} %get-tuple-element.25), channel_id=1, source_target_pairs={{0,16},{1,17},{2,18},{3,19},{4,20},{5,21},{6,22},{7,23},{8,24},{9,... | collective-permute-start | bytes 73736 | tf_op jit(solution)/shard_map/ppermute | solution.py:21
  45.4 4.0 %collective-permute-start.10 = (f32[48,128]{1,0:T(8,128)}, f32[48,128]{1,0:T(8,128)S(1)}, u32[]{:S(2)}, u32[]{:S(2)}) collective-permute-start(f32[48,128]{1,0:T(8,128)} %get-tuple-element.26), channel_id=1, source_target_pairs={{0,8},{1,9},{2,10},{3,11},{4,12},{5,13},{6,14},{7,15},{8,0},{9,1},... | collective-permute-start | bytes 73736 | tf_op jit(solution)/shard_map/ppermute | solution.py:21
  46.6 5.8 %collective-permute-start.11 = (f32[48,128]{1,0:T(8,128)}, f32[48,128]{1,0:T(8,128)S(1)}, u32[]{:S(2)}, u32[]{:S(2)}) collective-permute-start(f32[48,128]{1,0:T(8,128)} %get-tuple-element.27), channel_id=1, source_target_pairs={{0,24},{1,25},{2,26},{3,27},{4,28},{5,29},{6,30},{7,31},{8,16},{9,... | collective-permute-start | bytes 73736 | tf_op jit(solution)/shard_map/ppermute | solution.py:21
  47.8 4.7 %copy-start.4 = (f32[48,128]{1,0:T(8,128)}, f32[48,128]{1,0:T(8,128)S(1)}, u32[]{:S(2)}) copy-start(f32[48,128]{1,0:T(8,128)S(1)} %collective-permute-done.9.refs_0_) | copy-start | bytes 73732
  49.4 3.0 %copy-start.5 = (f32[48,128]{1,0:T(8,128)}, f32[48,128]{1,0:T(8,128)S(1)}, u32[]{:S(2)}) copy-start(f32[48,128]{1,0:T(8,128)S(1)} %collective-permute-done.10.refs_1_) | copy-start | bytes 73732
  52.4 0.6 %copy-start.6 = (f32[48,128]{1,0:T(8,128)}, f32[48,128]{1,0:T(8,128)S(1)}, u32[]{:S(2)}) copy-start(f32[48,128]{1,0:T(8,128)S(1)} %collective-permute-done.11.refs_2_) | copy-start | bytes 73732

commit v2 on v1

--- a/solution.py
+++ b/solution.py
@@ -10,6 +10,7 @@
 
 soft_core = 1e-06
 node_count = 32
+spare_bytes = 8 << 20
 axes = ("blk", "tile")
 pairs = ((0, 0), (0, 1), (0, 2), (1, 1), (1, 2), (2, 2))
 f32 = jnp.float32
@@ -135,7 +136,7 @@
     message[:, :width] = value[:, :width] - center * noise[...]
 
 
-def second_kernel(near_positions, blocks, bounds, nodes, high, low, weights, columns, rows):
+def second_kernel(bounds, near_positions, blocks, nodes, high, low, weights, columns, rows):
     half = blocks.shape[1] - 8
     width = blocks.shape[2] // 2
     for number in range(0, blocks.shape[0], 2):
@@ -220,14 +221,29 @@
 vmem = pl.BlockSpec(memory_space=pltpu.VMEM)
 
 
-def call(kernel, inputs, in_specs, outputs, scratch=()):
+def call(kernel, inputs, outputs, scratch=(), final=False):
+    specs, arrays = [], []
+    for value, place in inputs:
+        specs.append(smem if place == "smem" else vmem)
+        arrays.append(pltpu.with_memory_space_constraint(value, pltpu.VMEM) if place == "vmem" else value)
+    make = jax.ShapeDtypeStruct if final else pltpu.VMEM
+    sizes = [math.prod(ref.shape) * np.dtype(ref.dtype).itemsize for ref in scratch]
     return pl.pallas_call(
         kernel,
-        in_specs=in_specs,
-        out_shape=[jax.ShapeDtypeStruct(shape, dtype) for shape, dtype in outputs],
+        in_specs=specs,
+        out_shape=[make(shape, dtype) for shape, dtype in outputs],
         out_specs=[vmem] * len(outputs),
         scratch_shapes=list(scratch),
-    )(*inputs)
+        compiler_params=pltpu.CompilerParams(vmem_limit_bytes=sum(sizes) + spare_bytes),
+    )(*arrays)
+
+
+def held(*values):
+    return [(value, "vmem") for value in values]
+
+
+def given(*values):
+    return [(value, "") for value in values]
 
 
 def node_table():
@@ -259,9 +275,7 @@
     noise = noise_vectors.reshape(rows, width)
     bounds = spectrum_bounds
 
-    (packed,) = call(
-        pack_kernel, (noise, positions), [vmem, vmem], [((rows // 2 + 8, 2 * width), f32)]
-    )
+    (packed,) = call(pack_kernel, given(noise, positions), [((rows // 2 + 8, 2 * width), f32)])
     far = packed[None]
     near = positions
     for mask in far_masks:
@@ -270,11 +284,11 @@
         near = jnp.concatenate([near, exchange(near, mask)], axis=1)
     blocks = jnp.concatenate([far, exchange(far, core_mask)], axis=0)
     near_count, far_count = near.shape[1], blocks.shape[0] * width
+    scalars = [(bounds, "smem")]
 
     partial, message = call(
         first_kernel,
-        (bounds, blocks, near, noise),
-        [smem, vmem, vmem, vmem],
+        scalars + held(blocks, near) + given(noise),
         [((rows, near_count), f32)] * 2,
         (
             pltpu.VMEM((3, far_count, 128), f32),
@@ -285,32 +299,27 @@
     )
     high, low, weights = call(
         second_kernel,
-        (near, blocks, bounds, jnp.asarray(node_table())),
-        [vmem, vmem, smem, vmem],
+        scalars + held(near, blocks) + given(jnp.asarray(node_table())),
         [((6, near_count, far_count), bf16)] * 2 + [((8, 128), f32)],
         (pltpu.VMEM((3, near_count, 128), f32), pltpu.VMEM((8, far_count), f32)),
     )
     received = [exchange(message, mask) for mask in combinations(near_masks)[1:]]
     first_image, kept, sent = call(
         third_kernel,
-        (bounds, *received, partial, message, high, low),
-        [smem] + [vmem] * (len(received) + 4),
+        scalars + held(*received, partial, message, high, low),
         [((rows, width), f32), ((rows, far_count // 2), f32), ((rows, far_count // 2), f32)],
     )
     arrived = exchange(sent, core_mask)
     far_steps = combinations(far_masks)
     own, *outgoing = call(
-        fourth_kernel,
-        (kept, arrived),
-        [vmem, vmem],
-        [((rows // 2, 2 * width), f32)] * len(far_steps),
+        fourth_kernel, held(kept, arrived), [((rows // 2, 2 * width), f32)] * len(far_steps)
     )
     received = [exchange(block, mask) for block, mask in zip(outgoing, far_steps[1:])]
     displacement, images = call(
         final_kernel,
-        (bounds, weights, noise, first_image, own, *received),
-        [smem] + [vmem] * (4 + len(received)),
+        scalars + held(weights) + given(noise) + held(first_image, own, *received),
         [((rows, width), f32), ((2, rows, width), f32)],
+        final=True,
     )
     shape = noise_vectors.shape
     return displacement.reshape(shape), images.reshape((2, *shape))

time: 55.2 us -> 43.8 us (0.79)
  Pallas kernels: 16.4 us -> 7.83 us
  other arithmetic: 5.06 us -> 0.18 us
  local copies, waits for them, and re-layouts: 1.89 us -> 3.61 us
    pallas_call x6, Pallas kernels: 16.4 us -> 7.83 us  [call(): pl.pallas_call(kernel, in_specs=specs, out_shape=[make(shape, dtype) for...]
    concatenate x2, other arithmetic: 2.1 us -> 0.15 us  [body(): near = jnp.concatenate([near, exchange(near, mask)], axis=1)]
    unnamed x14 -> x10, local copies, waits for them, and re-layouts: 1.89 us -> 3.61 us
    concatenate x2, other arithmetic: 1.51 us -> 0.02 us  [body(): far = jnp.concatenate([far, exchange(far, mask)], axis=0)]
    concatenate x1, other arithmetic: 1.45 us -> 0.02 us  [body(): blocks = jnp.concatenate([far, exchange(far, core_mask)], axis=0)]
  transfers between devices with their start and end apart: 12 -> 12, of which waited for: 9 -> 10; matrix products, arithmetic and copies ran while one was open for 5% -> 0% of each run, Pallas kernels for 8% -> 5%
where the time goes in v2:
time: 43.8 us; the launch traced here: 43.5 us
  starting transfers between devices  17.1 us (39%)
  waiting for transfers between devices  14.1 us (32%)
  Pallas kernels  7.83 us (18%)
  local copies, waits for them, and re-layouts  3.61 us (8%)
  between operations  0.71 us (2%)
    ppermute x12, starting transfers between devices, exchange(): return lax.ppermute(block, axes, [(i, i ^ mask) for i in range(count)])  17.1 us
    ppermute x12, waiting for transfers between devices, exchange(): return lax.ppermute(block, axes, [(i, i ^ mask) for i in range(count)])  14.1 us
    pallas_call x6, Pallas kernels, call(): pl.pallas_call(kernel, in_specs=specs, out_shape=[make(shape, dtype) for...  7.83 us
    unnamed x10, local copies, waits for them, and re-layouts  3.61 us
  transfers between devices with their start and end apart: 12, of which 10 were waited for; matrix products, arithmetic and copies ran while one was open for 0% of the time, Pallas kernels for 5%

profile of v2, /device:TPU:0, one launch (start us, length us, event | category | flops | bytes accessed | tf_op | source)
XLA Modules:
  0.0 43.5 jit_solution(11722597550440894280)
XLA Ops:
  0.6 0.0 copy-start
  0.6 0.8 %copy-done = f32[3,32,64]{2,1,0:T(8,128)S(1)} copy-done((f32[3,32,64]{2,1,0:T(8,128)S(1)}, f32[3,32,64]{2,1,0:T(8,128)}, u32[]{:S(2)}) %copy-start) | copy-done | bytes 24600
  1.4 0.0 copy-start.2
  1.4 0.7 %copy-done.2 = f32[3,64]{1,0:T(4,128)S(1)} copy-done((f32[3,64]{1,0:T(4,128)S(1)}, f32[3,64]{1,0:T(4,128)}, u32[]{:S(2)}) %copy-start.2) | copy-done | bytes 792
  2.1 0.1 shard_map.59
  2.2 4.1 %collective-permute-start.2 = (f32[1,56,128]{2,1,0:T(8,128)S(1)}, f32[1,56,128]{2,1,0:T(8,128)S(1)}, u32[]{:S(2)}, u32[]{:S(2)}) collective-permute-start(f32[1,56,128]{2,1,0:T(8,128)S(1)} %bitcast.4), channel_id=1, source_target_pairs={{0,16},{1,17},{2,18},{3,19},{4,20},{5,21},{6,22},{7,23},{8,24},{9,... | collective-permute-start | bytes 86024 | tf_op jit(solution)/shard_map/ppermute | solution.py:22
  6.3 1.9 %collective-permute-done.2 = f32[1,56,128]{2,1,0:T(8,128)S(1)} collective-permute-done((f32[1,56,128]{2,1,0:T(8,128)S(1)}, f32[1,56,128]{2,1,0:T(8,128)S(1)}, u32[]{:S(2)}, u32[]{:S(2)}) %collective-permute-start.2) | collective-permute-done | bytes 28704 | tf_op jit(solution)/shard_map/ppermute | solution.py:22
  8.1 1.9 %collective-permute-start.3 = (f32[2,56,128]{2,1,0:T(8,128)S(1)}, f32[2,56,128]{2,1,0:T(8,128)S(1)}, u32[]{:S(2)}, u32[]{:S(2)}) collective-permute-start(f32[2,56,128]{2,1,0:T(8,128)S(1)} %pad_maximum_fusion.2), channel_id=1, source_target_pairs={{0,8},{1,9},{2,10},{3,11},{4,12},{5,13},{6,14},{7,15},{8,0},{9,1},... | collective-permute-start | bytes 172040 | tf_op jit(solution)/shard_map/ppermute | solution.py:22
  10.0 1.5 %collective-permute-start = (f32[3,64]{1,0:T(4,128)S(1)}, f32[3,64]{1,0:T(4,128)S(1)}, u32[]{:S(2)}, u32[]{:S(2)}) collective-permute-start(f32[3,64]{1,0:T(4,128)S(1)} %copy-done.2), channel_id=1, source_target_pairs={{0,1},{1,0},{2,3},{3,2},{4,5},{5,4},{6,7},{7,6},{8,9},{9,8},{10,11... | collective-permute-start | bytes 2312 | tf_op jit(solution)/shard_map/ppermute | solution.py:22
  11.5 0.8 %collective-permute-done.3 = f32[2,56,128]{2,1,0:T(8,128)S(1)} collective-permute-done((f32[2,56,128]{2,1,0:T(8,128)S(1)}, f32[2,56,128]{2,1,0:T(8,128)S(1)}, u32[]{:S(2)}, u32[]{:S(2)}) %collective-permute-start.3) | collective-permute-done | bytes 57376 | tf_op jit(solution)/shard_map/ppermute | solution.py:22
  12.3 0.1 collective-permute-start.4
  12.4 1.2 %collective-permute-done = f32[3,64]{1,0:T(4,128)S(1)} collective-permute-done((f32[3,64]{1,0:T(4,128)S(1)}, f32[3,64]{1,0:T(4,128)S(1)}, u32[]{:S(2)}, u32[]{:S(2)}) %collective-permute-start) | collective-permute-done | bytes 800 | tf_op jit(solution)/shard_map/ppermute | solution.py:22
  13.6 0.1 pad_maximum_fusion.4
  13.7 1.5 %collective-permute-start.1 = (f32[3,128]{1,0:T(4,128)S(1)}, f32[3,128]{1,0:T(4,128)S(1)}, u32[]{:S(2)}, u32[]{:S(2)}) collective-permute-start(f32[3,128]{1,0:T(4,128)S(1)} %pad_maximum_fusion.4), channel_id=1, source_target_pairs={{0,4},{1,5},{2,6},{3,7},{4,0},{5,1},{6,2},{7,3},{8,12},{9,13},{10,... | collective-permute-start | bytes 4616 | tf_op jit(solution)/shard_map/ppermute | solution.py:22
  15.2 2.1 %collective-permute-done.1 = f32[3,128]{1,0:T(4,128)S(1)} collective-permute-done((f32[3,128]{1,0:T(4,128)S(1)}, f32[3,128]{1,0:T(4,128)S(1)}, u32[]{:S(2)}, u32[]{:S(2)}) %collective-permute-start.1) | collective-permute-done | bytes 1568 | tf_op jit(solution)/shard_map/ppermute | solution.py:22
  17.3 0.1 pad_maximum_fusion.3.near_positions
  17.3 0.0 collective-permute-done.4
  17.4 0.0 copy-start.1
  17.4 0.8 %copy-done.1 = f32[3,32,64]{2,1,0:T(8,128)S(1)} copy-done((f32[3,32,64]{2,1,0:T(8,128)S(1)}, f32[3,32,64]{2,1,0:T(8,128)}, u32[]{:S(2)}) %copy-start.1) | copy-done | bytes 24600
  18.2 0.0 copy-start.3
  18.2 0.7 %copy-done.3 = f32[2]{0:T(128)S(1)} copy-done((f32[2]{0:T(128)S(1)}, f32[2]{0:T(128)}, u32[]{:S(2)}) %copy-start.3) | copy-done | bytes 32
  18.8 3.1 %shard_map.61 = (f32[96,256]{1,0:T(8,128)S(1)}, f32[96,256]{1,0:T(8,128)S(1)}) custom-call(f32[2]{0:T(128)S(1)} %copy-done.3, f32[8,56,128]{2,1,0:T(8,128)S(1)} %pad_maximum_fusion.blocks, f32[3,256]{1,0:T(4,128)S(1)} %pad_maximum_fusion.3.near_positions, f32[96,64]{1,0:T(8,128)S(1)} %bitcast.9), custom_call_target="tpu_custom_call" | custom-call | tf_op jit(solution)/shard_map/pallas_call | solution.py:231
  21.9 1.5 %collective-permute-start.5 = (f32[96,256]{1,0:T(8,128)S(1)}, f32[96,256]{1,0:T(8,128)S(1)}, u32[]{:S(2)}, u32[]{:S(2)}) collective-permute-start(f32[96,256]{1,0:T(8,128)S(1)} %get-tuple-element.17.refs_4_), channel_id=1, source_target_pairs={{0,1},{1,0},{2,3},{3,2},{4,5},{5,4},{6,7},{7,6},{8,9},{9,8},{10,11... | collective-permute-start | bytes 294920 | tf_op jit(solution)/shard_map/ppermute | solution.py:22
  23.4 1.5 %collective-permute-start.6 = (f32[96,256]{1,0:T(8,128)S(1)}, f32[96,256]{1,0:T(8,128)S(1)}, u32[]{:S(2)}, u32[]{:S(2)}) collective-permute-start(f32[96,256]{1,0:T(8,128)S(1)} %get-tuple-element.17.refs_4_), channel_id=1, source_target_pairs={{0,4},{1,5},{2,6},{3,7},{4,0},{5,1},{6,2},{7,3},{8,12},{9,13},{10,... | collective-permute-start | bytes 294920 | tf_op jit(solution)/shard_map/ppermute | solution.py:22
  25.0 0.5 %collective-permute-start.7 = (f32[96,256]{1,0:T(8,128)S(1)}, f32[96,256]{1,0:T(8,128)S(1)}, u32[]{:S(2)}, u32[]{:S(2)}) collective-permute-start(f32[96,256]{1,0:T(8,128)S(1)} %get-tuple-element.17.refs_4_), channel_id=1, source_target_pairs={{0,5},{1,4},{2,7},{3,6},{4,1},{5,0},{6,3},{7,2},{8,13},{9,12},{10,... | collective-permute-start | bytes 294920 | tf_op jit(solution)/shard_map/ppermute | solution.py:22
  25.4 0.0 copy-start.4
  25.4 0.7 %copy-done.4 = f32[8,128]{1,0:T(8,128)S(1)} copy-done((f32[8,128]{1,0:T(8,128)S(1)}, f32[8,128]{1,0:T(8,128)}, u32[]{:S(2)}) %copy-start.4) | copy-done | bytes 4120
  26.1 2.1 %shard_map.60 = (bf16[6,256,512]{2,1,0:T(8,128)(2,1)S(1)}, bf16[6,256,512]{2,1,0:T(8,128)(2,1)S(1)}, f32[8,128]{1,0:T(8,128)S(1)}) custom-call(f32[2]{0:T(128)S(1)} %copy-done.3, f32[3,256]{1,0:T(4,128)S(1)} %pad_maximum_fusion.3.near_positions, f32[8,56,128]{2,1,0:T(8,128)S(1)} %pad_maximum_fusion.blocks, f32[8,128]{1,0:T(8,128)S(1)} %copy-done.4), custom_call_target="tpu_custom_call" | custom-call | tf_op jit(solution)/shard_map/pallas_call | solution.py:231
  28.3 0.0 collective-permute-done.5.refs_0_
  28.3 0.6 %collective-permute-done.6.refs_1_ = f32[96,256]{1,0:T(8,128)S(1)} collective-permute-done((f32[96,256]{1,0:T(8,128)S(1)}, f32[96,256]{1,0:T(8,128)S(1)}, u32[]{:S(2)}, u32[]{:S(2)}) %collective-permute-start.6) | collective-permute-done | bytes 98336 | tf_op jit(solution)/shard_map/ppermute | solution.py:22
  28.9 1.6 %collective-permute-done.7.refs_2_ = f32[96,256]{1,0:T(8,128)S(1)} collective-permute-done((f32[96,256]{1,0:T(8,128)S(1)}, f32[96,256]{1,0:T(8,128)S(1)}, u32[]{:S(2)}, u32[]{:S(2)}) %collective-permute-start.7) | collective-permute-done | bytes 98336 | tf_op jit(solution)/shard_map/ppermute | solution.py:22
  30.5 1.2 %shard_map.62 = (f32[96,64]{1,0:T(8,128)S(1)}, f32[96,256]{1,0:T(8,128)S(1)}, f32[96,256]{1,0:T(8,128)S(1)}) custom-call(f32[2]{0:T(128)S(1)} %copy-done.3, f32[96,256]{1,0:T(8,128)S(1)} %collective-permute-done.5.refs_0_, f32[96,256]{1,0:T(8,128)S(1)} %collective-permute-done.6.refs_1_, f32[96,256]{1,0:T(8,128)S(1)} %collective-permute-done.7.refs_2_, ...), custom_call_target="tpu_custom_call" | custom-call | tf_op jit(solution)/shard_map/pallas_call | solution.py:231
  31.7 0.0 collective-permute-start.8
  31.7 1.3 %collective-permute-done.8.arrived = f32[96,256]{1,0:T(8,128)S(1)} collective-permute-done((f32[96,256]{1,0:T(8,128)S(1)}, f32[96,256]{1,0:T(8,128)S(1)}, u32[]{:S(2)}, u32[]{:S(2)}) %collective-permute-start.8) | collective-permute-done | bytes 98336 | tf_op jit(solution)/shard_map/ppermute | solution.py:22
  33.0 0.1 shard_map.63
  33.1 2.9 %collective-permute-start.9 = (f32[48,128]{1,0:T(8,128)S(1)}, f32[48,128]{1,0:T(8,128)S(1)}, u32[]{:S(2)}, u32[]{:S(2)}) collective-permute-start(f32[48,128]{1,0:T(8,128)S(1)} %get-tuple-element.25), channel_id=1, source_target_pairs={{0,16},{1,17},{2,18},{3,19},{4,20},{5,21},{6,22},{7,23},{8,24},{9,... | collective-permute-start | bytes 73736 | tf_op jit(solution)/shard_map/ppermute | solution.py:22
  35.9 0.7 %collective-permute-start.10 = (f32[48,128]{1,0:T(8,128)S(1)}, f32[48,128]{1,0:T(8,128)S(1)}, u32[]{:S(2)}, u32[]{:S(2)}) collective-permute-start(f32[48,128]{1,0:T(8,128)S(1)} %get-tuple-element.26), channel_id=1, source_target_pairs={{0,8},{1,9},{2,10},{3,11},{4,12},{5,13},{6,14},{7,15},{8,0},{9,1},... | collective-permute-start | bytes 73736 | tf_op jit(solution)/shard_map/ppermute | solution.py:22
  36.6 0.9 %collective-permute-start.11 = (f32[48,128]{1,0:T(8,128)S(1)}, f32[48,128]{1,0:T(8,128)S(1)}, u32[]{:S(2)}, u32[]{:S(2)}) collective-permute-start(f32[48,128]{1,0:T(8,128)S(1)} %get-tuple-element.27), channel_id=1, source_target_pairs={{0,24},{1,25},{2,26},{3,27},{4,28},{5,29},{6,30},{7,31},{8,16},{9,... | collective-permute-start | bytes 73736 | tf_op jit(solution)/shard_map/ppermute | solution.py:22
  37.5 0.6 %collective-permute-done.9.refs_0_ = f32[48,128]{1,0:T(8,128)S(1)} collective-permute-done((f32[48,128]{1,0:T(8,128)S(1)}, f32[48,128]{1,0:T(8,128)S(1)}, u32[]{:S(2)}, u32[]{:S(2)}) %collective-permute-start.9) | collective-permute-done | bytes 24608 | tf_op jit(solution)/shard_map/ppermute | solution.py:22
  38.1 1.6 %collective-permute-done.10.refs_1_ = f32[48,128]{1,0:T(8,128)S(1)} collective-permute-done((f32[48,128]{1,0:T(8,128)S(1)}, f32[48,128]{1,0:T(8,128)S(1)}, u32[]{:S(2)}, u32[]{:S(2)}) %collective-permute-start.10) | collective-permute-done | bytes 24608 | tf_op jit(solution)/shard_map/ppermute | solution.py:22
  39.8 2.5 %collective-permute-done.11.refs_2_ = f32[48,128]{1,0:T(8,128)S(1)} collective-permute-done((f32[48,128]{1,0:T(8,128)S(1)}, f32[48,128]{1,0:T(8,128)S(1)}, u32[]{:S(2)}, u32[]{:S(2)}) %collective-permute-start.11) | collective-permute-done | bytes 24608 | tf_op jit(solution)/shard_map/ppermute | solution.py:22
  42.3 1.3 %shard_map.64 = (f32[96,64]{1,0:T(8,128)}, f32[2,96,64]{2,1,0:T(8,128)}) custom-call(f32[2]{0:T(128)S(1)} %copy-done.3, f32[8,128]{1,0:T(8,128)S(1)} %get-tuple-element.16.weights, f32[96,64]{1,0:T(8,128)S(1)} %bitcast.10, f32[96,64]{1,0:T(8,128)S(1)} %get-tuple-element.21.first_image, f32[48,128]{1,0:T(8,128)S(1)} %get-tuple-element.24.own, ...), custom_call_target="tpu_custom_call" | custom-call | tf_op jit(solution)/shard_map/pallas_call | solution.py:231
  (3 shorter events, 0.0 us)
Async XLA Ops:
  0.6 0.8 %copy-start = (f32[3,32,64]{2,1,0:T(8,128)S(1)}, f32[3,32,64]{2,1,0:T(8,128)}, u32[]{:S(2)}) copy-start(f32[3,32,64]{2,1,0:T(8,128)} %param.5) | copy-start | bytes 73732
  1.4 0.7 %copy-start.2 = (f32[3,64]{1,0:T(4,128)S(1)}, f32[3,64]{1,0:T(4,128)}, u32[]{:S(2)}) copy-start(f32[3,64]{1,0:T(4,128)} %positions.1) | copy-start | bytes 2308
  2.2 5.9 %collective-permute-start.2 = (f32[1,56,128]{2,1,0:T(8,128)S(1)}, f32[1,56,128]{2,1,0:T(8,128)S(1)}, u32[]{:S(2)}, u32[]{:S(2)}) collective-permute-start(f32[1,56,128]{2,1,0:T(8,128)S(1)} %bitcast.4), channel_id=1, source_target_pairs={{0,16},{1,17},{2,18},{3,19},{4,20},{5,21},{6,22},{7,23},{8,24},{9,... | collective-permute-start | bytes 86024 | tf_op jit(solution)/shard_map/ppermute | solution.py:22
  8.1 4.2 %collective-permute-start.3 = (f32[2,56,128]{2,1,0:T(8,128)S(1)}, f32[2,56,128]{2,1,0:T(8,128)S(1)}, u32[]{:S(2)}, u32[]{:S(2)}) collective-permute-start(f32[2,56,128]{2,1,0:T(8,128)S(1)} %pad_maximum_fusion.2), channel_id=1, source_target_pairs={{0,8},{1,9},{2,10},{3,11},{4,12},{5,13},{6,14},{7,15},{8,0},{9,1},... | collective-permute-start | bytes 172040 | tf_op jit(solution)/shard_map/ppermute | solution.py:22
  10.0 3.6 %collective-permute-start = (f32[3,64]{1,0:T(4,128)S(1)}, f32[3,64]{1,0:T(4,128)S(1)}, u32[]{:S(2)}, u32[]{:S(2)}) collective-permute-start(f32[3,64]{1,0:T(4,128)S(1)} %copy-done.2), channel_id=1, source_target_pairs={{0,1},{1,0},{2,3},{3,2},{4,5},{5,4},{6,7},{7,6},{8,9},{9,8},{10,11... | collective-permute-start | bytes 2312 | tf_op jit(solution)/shard_map/ppermute | solution.py:22
  12.3 5.0 %collective-permute-start.4 = (f32[4,56,128]{2,1,0:T(8,128)S(1)}, f32[4,56,128]{2,1,0:T(8,128)S(1)}, u32[]{:S(2)}, u32[]{:S(2)}) collective-permute-start(f32[4,56,128]{2,1,0:T(8,128)S(1)} %pad_maximum_fusion.1), channel_id=1, source_target_pairs={{0,2},{1,3},{2,0},{3,1},{4,6},{5,7},{6,4},{7,5},{8,10},{9,11},{10,... | collective-permute-start | bytes 344072 | tf_op jit(solution)/shard_map/ppermute | solution.py:22
  13.7 3.6 %collective-permute-start.1 = (f32[3,128]{1,0:T(4,128)S(1)}, f32[3,128]{1,0:T(4,128)S(1)}, u32[]{:S(2)}, u32[]{:S(2)}) collective-permute-start(f32[3,128]{1,0:T(4,128)S(1)} %pad_maximum_fusion.4), channel_id=1, source_target_pairs={{0,4},{1,5},{2,6},{3,7},{4,0},{5,1},{6,2},{7,3},{8,12},{9,13},{10,... | collective-permute-start | bytes 4616 | tf_op jit(solution)/shard_map/ppermute | solution.py:22
  17.4 0.8 %copy-start.1 = (f32[3,32,64]{2,1,0:T(8,128)S(1)}, f32[3,32,64]{2,1,0:T(8,128)}, u32[]{:S(2)}) copy-start(f32[3,32,64]{2,1,0:T(8,128)} %param.5) | copy-start | bytes 73732
  18.2 0.7 %copy-start.3 = (f32[2]{0:T(128)S(1)}, f32[2]{0:T(128)}, u32[]{:S(2)}) copy-start(f32[2]{0:T(128)} %bounds.7) | copy-start | bytes 28
  21.9 6.4 %collective-permute-start.5 = (f32[96,256]{1,0:T(8,128)S(1)}, f32[96,256]{1,0:T(8,128)S(1)}, u32[]{:S(2)}, u32[]{:S(2)}) collective-permute-start(f32[96,256]{1,0:T(8,128)S(1)} %get-tuple-element.17.refs_4_), channel_id=1, source_target_pairs={{0,1},{1,0},{2,3},{3,2},{4,5},{5,4},{6,7},{7,6},{8,9},{9,8},{10,11... | collective-permute-start | bytes 294920 | tf_op jit(solution)/shard_map/ppermute | solution.py:22
  23.4 5.4 %collective-permute-start.6 = (f32[96,256]{1,0:T(8,128)S(1)}, f32[96,256]{1,0:T(8,128)S(1)}, u32[]{:S(2)}, u32[]{:S(2)}) collective-permute-start(f32[96,256]{1,0:T(8,128)S(1)} %get-tuple-element.17.refs_4_), channel_id=1, source_target_pairs={{0,4},{1,5},{2,6},{3,7},{4,0},{5,1},{6,2},{7,3},{8,12},{9,13},{10,... | collective-permute-start | bytes 294920 | tf_op jit(solution)/shard_map/ppermute | solution.py:22
  25.0 5.5 %collective-permute-start.7 = (f32[96,256]{1,0:T(8,128)S(1)}, f32[96,256]{1,0:T(8,128)S(1)}, u32[]{:S(2)}, u32[]{:S(2)}) collective-permute-start(f32[96,256]{1,0:T(8,128)S(1)} %get-tuple-element.17.refs_4_), channel_id=1, source_target_pairs={{0,5},{1,4},{2,7},{3,6},{4,1},{5,0},{6,3},{7,2},{8,13},{9,12},{10,... | collective-permute-start | bytes 294920 | tf_op jit(solution)/shard_map/ppermute | solution.py:22
  25.4 0.7 %copy-start.4 = (f32[8,128]{1,0:T(8,128)S(1)}, f32[8,128]{1,0:T(8,128)}, u32[]{:S(2)}) copy-start(f32[8,128]{1,0:T(8,128)} %constant.2.clone.nodes) | copy-start | bytes 12292
  31.7 1.3 %collective-permute-start.8 = (f32[96,256]{1,0:T(8,128)S(1)}, f32[96,256]{1,0:T(8,128)S(1)}, u32[]{:S(2)}, u32[]{:S(2)}) collective-permute-start(f32[96,256]{1,0:T(8,128)S(1)} %get-tuple-element.23), channel_id=1, source_target_pairs={{0,2},{1,3},{2,0},{3,1},{4,6},{5,7},{6,4},{7,5},{8,10},{9,11},{10,... | collective-permute-start | bytes 294920 | tf_op jit(solution)/shard_map/ppermute | solution.py:22
  33.1 5.1 %collective-permute-start.9 = (f32[48,128]{1,0:T(8,128)S(1)}, f32[48,128]{1,0:T(8,128)S(1)}, u32[]{:S(2)}, u32[]{:S(2)}) collective-permute-start(f32[48,128]{1,0:T(8,128)S(1)} %get-tuple-element.25), channel_id=1, source_target_pairs={{0,16},{1,17},{2,18},{3,19},{4,20},{5,21},{6,22},{7,23},{8,24},{9,... | collective-permute-start | bytes 73736 | tf_op jit(solution)/shard_map/ppermute | solution.py:22
  35.9 3.8 %collective-permute-start.10 = (f32[48,128]{1,0:T(8,128)S(1)}, f32[48,128]{1,0:T(8,128)S(1)}, u32[]{:S(2)}, u32[]{:S(2)}) collective-permute-start(f32[48,128]{1,0:T(8,128)S(1)} %get-tuple-element.26), channel_id=1, source_target_pairs={{0,8},{1,9},{2,10},{3,11},{4,12},{5,13},{6,14},{7,15},{8,0},{9,1},... | collective-permute-start | bytes 73736 | tf_op jit(solution)/shard_map/ppermute | solution.py:22
  36.6 5.6 %collective-permute-start.11 = (f32[48,128]{1,0:T(8,128)S(1)}, f32[48,128]{1,0:T(8,128)S(1)}, u32[]{:S(2)}, u32[]{:S(2)}) collective-permute-start(f32[48,128]{1,0:T(8,128)S(1)} %get-tuple-element.27), channel_id=1, source_target_pairs={{0,24},{1,25},{2,26},{3,27},{4,28},{5,29},{6,30},{7,31},{8,16},{9,... | collective-permute-start | bytes 73736 | tf_op jit(solution)/shard_map/ppermute | solution.py:22

commit v3 on v2

--- a/solution.py
+++ b/solution.py
@@ -22,13 +22,29 @@
     return lax.ppermute(block, axes, [(i, i ^ mask) for i in range(count)])
 
 
-def pack_kernel(noise, positions, message):
+def open_kernel(
+    noise_in, positions_in, bounds_in, nodes_in, message, noise, positions, scalars, nodes, bounds, sems
+):
+    moves = (
+        (noise_in, noise),
+        (positions_in, positions),
+        (bounds_in, bounds),
+        (nodes_in, nodes),
+    )
+    copies = [pltpu.make_async_copy(*move, sems.at[n]) for n, move in enumerate(moves)]
+    for copy in copies:
+        copy.start()
+    for copy in copies:
+        copy.wait()
     half = noise.shape[0] // 2
     message[0:half, :] = jnp.concatenate([noise[0:half, :], noise[half:, :]], axis=1)
     spot = positions[...]
     pad = jnp.zeros((8 - spot.shape[0], spot.shape[1]), f32)
     spot = jnp.concatenate([spot, pad], axis=0)
     message[half:, :] = jnp.concatenate([spot, spot], axis=1)
+    highest, lowest = bounds[1], bounds[0]
+    scalars[0:4, :] = jnp.full((4, 128), 0.5 * (highest + lowest), f32)
+    scalars[4:8, :] = jnp.full((4, 128), 0.5 * (highest - lowest), f32)
 
 
 def halves(value):
@@ -114,39 +130,61 @@
     return result
 
 
-def first_kernel(bounds, blocks, near_positions, noise, partial, message, columns, rows, high, low):
-    half = noise.shape[0] // 2
-    vectors = noise.shape[0] // 3
-    width = noise.shape[1]
-    count = blocks.shape[0]
+def gather_rows(pieces, rows, half):
     uppers, lowers = [], []
-    for number in range(0, count, 2):
-        upper, lower, spots = unpack_pair(blocks[number], blocks[number + 1], half)
-        uppers.append(upper)
-        lowers.append(lower)
-        rows[:, number * width : (number + 2) * width] = spots
+    start = 0
+    for piece in pieces:
+        for number in range(0, piece.shape[0], 2):
+            upper, lower, spots = unpack_pair(piece[number], piece[number + 1], half)
+            uppers.append(upper)
+            lowers.append(lower)
+            rows[:, start : start + spots.shape[1]] = spots
+            start += spots.shape[1]
+    return uppers, lowers
+
+
+def side_by_side(values):
+    return values[0] if len(values) == 1 else jnp.concatenate(values, axis=1)
+
+
+def product_of(pieces, near_positions, scratch):
+    columns, rows, high, low = scratch
+    half = pieces[0].shape[1] - 8
+    vectors = 2 * half // 3
+    uppers, lowers = gather_rows(pieces, rows, half)
     fill_columns(columns, rows)
     build_tiles(columns, near_positions, high, low)
-    field = jnp.concatenate([jnp.concatenate(uppers, axis=1), jnp.concatenate(lowers, axis=1)], axis=0)
+    field = jnp.concatenate([side_by_side(uppers), side_by_side(lowers)], axis=0)
     field = [field[c * vectors : (c + 1) * vectors] for c in range(3)]
-    value = jnp.concatenate(apply_tiles(field, high, low), axis=0)
+    return jnp.concatenate(apply_tiles(field, high, low), axis=0)
+
+
+def opening_part(near_positions, *refs):
+    pieces, total, scratch = refs[:-5], refs[-5], refs[-4:]
+    total[...] = product_of(pieces, near_positions, scratch)
+
+
+def middle_part(near_positions, before, *refs):
+    pieces, total, scratch = refs[:-5], refs[-5], refs[-4:]
+    total[...] = before[...] + product_of(pieces, near_positions, scratch)
+
+
+def closing_part(scalars, noise, near_positions, before, *refs):
+    pieces, (partial, message), scratch = refs[:-6], refs[-6:-4], refs[-4:]
+    width = noise.shape[1]
+    value = before[...] + product_of(pieces, near_positions, scratch)
     partial[...] = value
     message[...] = value
-    center = 0.5 * (bounds[1] + bounds[0])
-    message[:, :width] = value[:, :width] - center * noise[...]
-
-
-def second_kernel(bounds, near_positions, blocks, nodes, high, low, weights, columns, rows):
-    half = blocks.shape[1] - 8
-    width = blocks.shape[2] // 2
-    for number in range(0, blocks.shape[0], 2):
-        spots = unpack_pair(blocks[number], blocks[number + 1], half)[2]
-        rows[:, number * width : (number + 2) * width] = spots
+    message[:, :width] = value[:, :width] - scalars[0:1, :width] * noise[...]
+
+
+def second_kernel(scalars, nodes, near_positions, *refs):
+    pieces, (high, low, weights, columns, rows) = refs[:-5], refs[-5:]
+    gather_rows(pieces, rows, pieces[0].shape[1] - 8)
     fill_columns(columns, near_positions)
     build_tiles(columns, rows, high, low)
-    center = 0.5 * (bounds[1] + bounds[0])
-    spread = 0.5 * (bounds[1] - bounds[0])
-    samples = jnp.sqrt(jnp.where(nodes[3:4, :] > 0.0, center + spread * nodes[1:2, :], 0.0))
+    samples = scalars[0:1, :] + scalars[4:5, :] * nodes[1:2, :]
+    samples = jnp.sqrt(jnp.where(nodes[3:4, :] > 0.0, samples, 0.0))
     total = jnp.sum(samples * nodes[...], axis=1, keepdims=True)
     weights[...] = jnp.broadcast_to((2.0 / node_count) * total, weights.shape)
 
@@ -164,13 +202,10 @@
     return tiles[0] if len(tiles) == 1 else jnp.concatenate(tiles, axis=1)
 
 
-def third_kernel(bounds, *refs):
+def third_kernel(scalars, *refs):
     received = refs[:-7]
-    partial, message, high, low, first_image, kept, sent = refs[-7:]
-    rows_count = partial.shape[0]
+    partial, message, high, low, first_image, linear, sent = refs[-7:]
     width = first_image.shape[1]
-    vectors = rows_count // 3
-    spread = 0.5 * (bounds[1] - bounds[0])
     total = message[...]
     own = partial[:, :width]
     for number, ref in enumerate(received):
@@ -178,12 +213,21 @@
         total = total + part
         own = own + part[:, :width]
     first_image[...] = own
-    linear = total / spread
-    field = [linear[c * vectors : (c + 1) * vectors] for c in range(3)]
-    value = jnp.concatenate(apply_tiles(field, high, low), axis=0)
-    middle = value.shape[1] // 2
-    kept[...] = value[:, :middle]
-    sent[...] = value[:, middle:]
+    linear[...] = total / scalars[4:5, 0:1]
+    half_product(linear, high, low, sent, 1)
+
+
+def half_product(linear, high, low, out, side):
+    vectors = linear.shape[0] // 3
+    middle = high.shape[2] // 2
+    lanes = slice(side * middle, (side + 1) * middle)
+    field = [linear[c * vectors : (c + 1) * vectors, :] for c in range(3)]
+    value = apply_tiles(field, high.at[:, :, lanes], low.at[:, :, lanes])
+    out[...] = jnp.concatenate(value, axis=0)
+
+
+def kept_kernel(linear, high, low, kept):
+    half_product(linear, high, low, kept, 0)
 
 
 def fourth_kernel(kept, arrived, own, *outgoing):
@@ -195,15 +239,15 @@
         ref[...] = jnp.concatenate([block[:half], block[half:]], axis=1)
 
 
-def final_kernel(bounds, weights, noise, first_image, own, *refs):
+def final_kernel(scalars, weights, noise, first_image, own, *refs):
     received, (displacement, images) = refs[:-2], refs[-2:]
     width = noise.shape[1]
     total = own[...]
     for ref in received:
         total = total + ref[...]
     second = jnp.concatenate([total[:, :width], total[:, width:]], axis=0)
-    center = 0.5 * (bounds[1] + bounds[0])
-    spread = 0.5 * (bounds[1] - bounds[0])
+    center = scalars[0:1, :width]
+    spread = scalars[4:5, :width]
     vectors = noise[...]
     first = first_image[...]
     linear = (first - center * vectors) / spread
@@ -217,33 +261,25 @@
     images[1] = second
 
 
-smem = pl.BlockSpec(memory_space=pltpu.SMEM)
 vmem = pl.BlockSpec(memory_space=pltpu.VMEM)
 
 
-def call(kernel, inputs, outputs, scratch=(), final=False):
-    specs, arrays = [], []
-    for value, place in inputs:
-        specs.append(smem if place == "smem" else vmem)
-        arrays.append(pltpu.with_memory_space_constraint(value, pltpu.VMEM) if place == "vmem" else value)
+def call(kernel, inputs, outputs, scratch=(), final=False, opening=False):
+    space = pltpu.HBM if opening else pltpu.VMEM
     make = jax.ShapeDtypeStruct if final else pltpu.VMEM
-    sizes = [math.prod(ref.shape) * np.dtype(ref.dtype).itemsize for ref in scratch]
+    sizes = [
+        math.prod(ref.shape) * np.dtype(ref.dtype).itemsize
+        for ref in scratch
+        if ref.memory_space == pltpu.VMEM
+    ]
     return pl.pallas_call(
         kernel,
-        in_specs=specs,
+        in_specs=[pl.BlockSpec(memory_space=space)] * len(inputs),
         out_shape=[make(shape, dtype) for shape, dtype in outputs],
         out_specs=[vmem] * len(outputs),
         scratch_shapes=list(scratch),
         compiler_params=pltpu.CompilerParams(vmem_limit_bytes=sum(sizes) + spare_bytes),
-    )(*arrays)
-
-
-def held(*values):
-    return [(value, "vmem") for value in values]
-
-
-def given(*values):
-    return [(value, "") for value in values]
+    )(*[pltpu.with_memory_space_constraint(value, space) for value in inputs])
 
 
 def node_table():
@@ -262,7 +298,7 @@
     return result
 
 
-def body(positions, noise_vectors, spectrum_bounds):
+def body(positions_in, noise_vectors, spectrum_bounds):
     tiles = lax.axis_size("tile")
     bits = lax.axis_size("blk").bit_length() - 1
     half_bits = bits // 2
@@ -272,52 +308,77 @@
     near_masks += [tiles << bit for bit in range(1, half_bits)]
     components, vectors, width = noise_vectors.shape
     rows = components * vectors
-    noise = noise_vectors.reshape(rows, width)
-    bounds = spectrum_bounds
-
-    (packed,) = call(pack_kernel, given(noise, positions), [((rows // 2 + 8, 2 * width), f32)])
-    far = packed[None]
+    last = len(far_masks) - 1
+    block = ((rows // 2, 2 * width), f32)
+
+    message, noise, positions, scalars, nodes = call(
+        open_kernel,
+        (
+            noise_vectors.reshape(rows, width),
+            positions_in,
+            spectrum_bounds,
+            jnp.asarray(node_table()),
+        ),
+        [
+            ((rows // 2 + 8, 2 * width), f32),
+            ((rows, width), f32),
+            (positions_in.shape, f32),
+            ((8, 128), f32),
+            ((8, 128), f32),
+        ],
+        (pltpu.SMEM((2,), f32), pltpu.SemaphoreType.DMA((4,))),
+        opening=True,
+    )
     near = positions
-    for mask in far_masks:
-        far = jnp.concatenate([far, exchange(far, mask)], axis=0)
+    far = message[None]
     for mask in near_masks:
         near = jnp.concatenate([near, exchange(near, mask)], axis=1)
-    blocks = jnp.concatenate([far, exchange(far, core_mask)], axis=0)
-    near_count, far_count = near.shape[1], blocks.shape[0] * width
-    scalars = [(bounds, "smem")]
-
+    for mask in far_masks[:last]:
+        far = jnp.concatenate([far, exchange(far, mask)], axis=0)
+    across = exchange(far, core_mask)
+    late = exchange(far, far_masks[last])
+    late_across = exchange(late, core_mask)
+    near_count, piece_count = near.shape[1], far.shape[0] * width
+    far_count = 4 * piece_count
+
+    def tiles_for(count):
+        return (
+            pltpu.VMEM((3, count, 128), f32),
+            pltpu.VMEM((8, count), f32),
+            pltpu.VMEM((6, count, near_count), bf16),
+            pltpu.VMEM((6, count, near_count), bf16),
+        )
+
+    whole = ((rows, near_count), f32)
+    (total,) = call(opening_part, (near, far, across), [whole], tiles_for(2 * piece_count))
+    (total,) = call(middle_part, (near, total, late), [whole], tiles_for(piece_count))
     partial, message = call(
-        first_kernel,
-        scalars + held(blocks, near) + given(noise),
-        [((rows, near_count), f32)] * 2,
-        (
-            pltpu.VMEM((3, far_count, 128), f32),
-            pltpu.VMEM((8, far_count), f32),
-            pltpu.VMEM((6, far_count, near_count), bf16),
-            pltpu.VMEM((6, far_count, near_count), bf16),
-        ),
+        closing_part,
+        (scalars, noise, near, total, late_across),
+        [whole, whole],
+        tiles_for(piece_count),
     )
     high, low, weights = call(
         second_kernel,
-        scalars + held(near, blocks) + given(jnp.asarray(node_table())),
+        (scalars, nodes, near, far, late, across, late_across),
         [((6, near_count, far_count), bf16)] * 2 + [((8, 128), f32)],
         (pltpu.VMEM((3, near_count, 128), f32), pltpu.VMEM((8, far_count), f32)),
     )
-    received = [exchange(message, mask) for mask in combinations(near_masks)[1:]]
-    first_image, kept, sent = call(
+    near_steps = combinations(near_masks)
+    received = [exchange(message, mask) for mask in near_steps[1:]]
+    first_image, linear, sent = call(
         third_kernel,
-        scalars + held(*received, partial, message, high, low),
-        [((rows, width), f32), ((rows, far_count // 2), f32), ((rows, far_count // 2), f32)],
+        (scalars, *received, partial, message, high, low),
+        [((rows, width), f32), whole, ((rows, far_count // 2), f32)],
     )
     arrived = exchange(sent, core_mask)
+    (kept,) = call(kept_kernel, (linear, high, low), [((rows, far_count // 2), f32)])
     far_steps = combinations(far_masks)
-    own, *outgoing = call(
-        fourth_kernel, held(kept, arrived), [((rows // 2, 2 * width), f32)] * len(far_steps)
-    )
-    received = [exchange(block, mask) for block, mask in zip(outgoing, far_steps[1:])]
+    own, *outgoing = call(fourth_kernel, (kept, arrived), [block] * len(far_steps))
+    received = [exchange(value, mask) for value, mask in zip(outgoing, far_steps[1:])]
     displacement, images = call(
         final_kernel,
-        scalars + held(weights) + given(noise) + held(first_image, own, *received),
+        (scalars, weights, noise, first_image, own, *received),
         [((rows, width), f32), ((2, rows, width), f32)],
         final=True,
     )

time: 43.8 us -> 36.8 us (0.84)
  local copies, waits for them, and re-layouts: 3.61 us -> 0 us
  waiting for transfers between devices: 14.1 us -> 11.4 us
  Pallas kernels: 7.83 us -> 7.26 us
    unnamed x10 -> x0, local copies, waits for them, and re-layouts: 3.61 us -> none
    ppermute x12 -> x13, waiting for transfers between devices: 14.1 us -> 11.4 us  [exchange(): return lax.ppermute(block, axes, [(i, i ^ mask) for i in range(count)])]
    pallas_call x6 -> x9, Pallas kernels: 7.83 us -> 7.26 us  [call(): pl.pallas_call(kernel, in_specs=[pl.BlockSpec(memory_space=space)] * len(...]
    ppermute x12 -> x13, starting transfers between devices: 17.1 us -> 17.1 us  [exchange(): return lax.ppermute(block, axes, [(i, i ^ mask) for i in range(count)])]
  transfers between devices with their start and end apart: 12 -> 13, of which waited for: 10 -> 9; matrix products, arithmetic and copies ran while one was open for 0% -> 0% of each run, Pallas kernels for 5% -> 12%
where the time goes in v3:
time: 36.8 us; the launch traced here: 36.6 us
  starting transfers between devices  17.1 us (46%)
  waiting for transfers between devices  11.4 us (31%)
  Pallas kernels  7.26 us (20%)
  between operations  0.72 us (2%)
    ppermute x13, starting transfers between devices, exchange(): return lax.ppermute(block, axes, [(i, i ^ mask) for i in range(count)])  17.1 us
    ppermute x13, waiting for transfers between devices, exchange(): return lax.ppermute(block, axes, [(i, i ^ mask) for i in range(count)])  11.4 us
    pallas_call x9, Pallas kernels, call(): pl.pallas_call(kernel, in_specs=[pl.BlockSpec(memory_space=space)] * len(...  7.26 us
  transfers between devices with their start and end apart: 13, of which 9 were waited for; matrix products, arithmetic and copies ran while one was open for 0% of the time, Pallas kernels for 12%

profile of v3, /device:TPU:0, one launch (start us, length us, event | category | flops | bytes accessed | tf_op | source)
XLA Modules:
  0.0 36.6 jit_solution(1576219278554228795)
XLA Ops:
  0.6 0.9 %shard_map.59 = (f32[56,128]{1,0:T(8,128)S(1)}, f32[96,64]{1,0:T(8,128)S(1)}, f32[3,64]{1,0:T(4,128)S(1)}, f32[8,128]{1,0:T(8,128)S(1)}, f32[8,128]{1,0:T(8,128)S(1)}) custom-call(f32[96,64]{1,0:T(8,128)} %bitcast.6, f32[3,64]{1,0:T(4,128)} %positions_in.1, f32[2]{0:T(128)} %bounds_in.1, f32[8,128]{1,0:T(8,128)} %constant.2.clone.nodes_in), custom_call_target="tpu_custom_call" | custom-call | tf_op jit(solution)/shard_map/pallas_call | solution.py:275
  1.6 4.1 %collective-permute-start.2 = (f32[1,56,128]{2,1,0:T(8,128)S(1)}, f32[1,56,128]{2,1,0:T(8,128)S(1)}, u32[]{:S(2)}, u32[]{:S(2)}) collective-permute-start(f32[1,56,128]{2,1,0:T(8,128)S(1)} %bitcast.4), channel_id=1, source_target_pairs={{0,16},{1,17},{2,18},{3,19},{4,20},{5,21},{6,22},{7,23},{8,24},{9,... | collective-permute-start | bytes 86024 | tf_op jit(solution)/shard_map/ppermute | solution.py:22
  5.7 1.5 %collective-permute-start = (f32[3,64]{1,0:T(4,128)S(1)}, f32[3,64]{1,0:T(4,128)S(1)}, u32[]{:S(2)}, u32[]{:S(2)}) collective-permute-start(f32[3,64]{1,0:T(4,128)S(1)} %get-tuple-element.23), channel_id=1, source_target_pairs={{0,1},{1,0},{2,3},{3,2},{4,5},{5,4},{6,7},{7,6},{8,9},{9,8},{10,11... | collective-permute-start | bytes 2312 | tf_op jit(solution)/shard_map/ppermute | solution.py:22
  7.2 0.4 %collective-permute-done.2 = f32[1,56,128]{2,1,0:T(8,128)S(1)} collective-permute-done((f32[1,56,128]{2,1,0:T(8,128)S(1)}, f32[1,56,128]{2,1,0:T(8,128)S(1)}, u32[]{:S(2)}, u32[]{:S(2)}) %collective-permute-start.2) | collective-permute-done | bytes 28704 | tf_op jit(solution)/shard_map/ppermute | solution.py:22
  7.6 1.9 %collective-permute-start.3 = (f32[2,56,128]{2,1,0:T(8,128)S(1)}, f32[2,56,128]{2,1,0:T(8,128)S(1)}, u32[]{:S(2)}, u32[]{:S(2)}) collective-permute-start(f32[2,56,128]{2,1,0:T(8,128)S(1)} %pad_maximum_fusion.refs_0_), channel_id=1, source_target_pairs={{0,8},{1,9},{2,10},{3,11},{4,12},{5,13},{6,14},{7,15},{8,0},{9,1},... | collective-permute-start | bytes 172040 | tf_op jit(solution)/shard_map/ppermute | solution.py:22
  9.5 0.0 collective-permute-done
  9.5 0.1 pad_maximum_fusion.2
  9.5 1.5 %collective-permute-start.1 = (f32[3,128]{1,0:T(4,128)S(1)}, f32[3,128]{1,0:T(4,128)S(1)}, u32[]{:S(2)}, u32[]{:S(2)}) collective-permute-start(f32[3,128]{1,0:T(4,128)S(1)} %pad_maximum_fusion.2), channel_id=1, source_target_pairs={{0,4},{1,5},{2,6},{3,7},{4,0},{5,1},{6,2},{7,3},{8,12},{9,13},{10,... | collective-permute-start | bytes 4616 | tf_op jit(solution)/shard_map/ppermute | solution.py:22
  11.1 0.0 collective-permute-start.4
  11.1 0.7 %collective-permute-done.3.refs_1_.refs_0_ = f32[2,56,128]{2,1,0:T(8,128)S(1)} collective-permute-done((f32[2,56,128]{2,1,0:T(8,128)S(1)}, f32[2,56,128]{2,1,0:T(8,128)S(1)}, u32[]{:S(2)}, u32[]{:S(2)}) %collective-permute-start.3) | collective-permute-done | bytes 57376 | tf_op jit(solution)/shard_map/ppermute | solution.py:22
  11.7 0.0 collective-permute-start.5
  11.7 1.4 %collective-permute-done.1 = f32[3,128]{1,0:T(4,128)S(1)} collective-permute-done((f32[3,128]{1,0:T(4,128)S(1)}, f32[3,128]{1,0:T(4,128)S(1)}, u32[]{:S(2)}, u32[]{:S(2)}) %collective-permute-start.1) | collective-permute-done | bytes 1568 | tf_op jit(solution)/shard_map/ppermute | solution.py:22
  13.1 0.1 pad_maximum_fusion.1.near_positions
  13.2 0.0 collective-permute-done.4.refs_2_.refs_1_
  13.2 1.4 %shard_map.61.before = f32[96,256]{1,0:T(8,128)S(1)} custom-call(f32[3,256]{1,0:T(4,128)S(1)} %pad_maximum_fusion.1.near_positions, f32[2,56,128]{2,1,0:T(8,128)S(1)} %pad_maximum_fusion.refs_0_, f32[2,56,128]{2,1,0:T(8,128)S(1)} %collective-permute-done.4.refs_2_.refs_1_), custom_call_target="tpu_custom_call" | custom-call | tf_op jit(solution)/shard_map/pallas_call | solution.py:275
  14.6 0.9 %shard_map.62.before = f32[96,256]{1,0:T(8,128)S(1)} custom-call(f32[3,256]{1,0:T(4,128)S(1)} %pad_maximum_fusion.1.near_positions, f32[96,256]{1,0:T(8,128)S(1)} %shard_map.61.before, f32[2,56,128]{2,1,0:T(8,128)S(1)} %collective-permute-done.3.refs_1_.refs_0_), custom_call_target="tpu_custom_call" | custom-call | tf_op jit(solution)/shard_map/pallas_call | solution.py:275
  15.5 0.0 collective-permute-done.5.refs_3_.refs_0_
  15.5 0.9 %shard_map.63 = (f32[96,256]{1,0:T(8,128)S(1)}, f32[96,256]{1,0:T(8,128)S(1)}) custom-call(f32[8,128]{1,0:T(8,128)S(1)} %get-tuple-element.21.scalars, f32[96,64]{1,0:T(8,128)S(1)} %get-tuple-element.26.noise, f32[3,256]{1,0:T(4,128)S(1)} %pad_maximum_fusion.1.near_positions, f32[96,256]{1,0:T(8,128)S(1)} %shard_map.62.before, ...), custom_call_target="tpu_custom_call" | custom-call | tf_op jit(solution)/shard_map/pallas_call | solution.py:275
  16.4 1.6 %collective-permute-start.6 = (f32[96,256]{1,0:T(8,128)S(1)}, f32[96,256]{1,0:T(8,128)S(1)}, u32[]{:S(2)}, u32[]{:S(2)}) collective-permute-start(f32[96,256]{1,0:T(8,128)S(1)} %get-tuple-element.27.refs_4_), channel_id=1, source_target_pairs={{0,1},{1,0},{2,3},{3,2},{4,5},{5,4},{6,7},{7,6},{8,9},{9,8},{10,11... | collective-permute-start | bytes 294920 | tf_op jit(solution)/shard_map/ppermute | solution.py:22
  17.9 1.5 %collective-permute-start.7 = (f32[96,256]{1,0:T(8,128)S(1)}, f32[96,256]{1,0:T(8,128)S(1)}, u32[]{:S(2)}, u32[]{:S(2)}) collective-permute-start(f32[96,256]{1,0:T(8,128)S(1)} %get-tuple-element.27.refs_4_), channel_id=1, source_target_pairs={{0,4},{1,5},{2,6},{3,7},{4,0},{5,1},{6,2},{7,3},{8,12},{9,13},{10,... | collective-permute-start | bytes 294920 | tf_op jit(solution)/shard_map/ppermute | solution.py:22
  19.4 0.5 %collective-permute-start.8 = (f32[96,256]{1,0:T(8,128)S(1)}, f32[96,256]{1,0:T(8,128)S(1)}, u32[]{:S(2)}, u32[]{:S(2)}) collective-permute-start(f32[96,256]{1,0:T(8,128)S(1)} %get-tuple-element.27.refs_4_), channel_id=1, source_target_pairs={{0,5},{1,4},{2,7},{3,6},{4,1},{5,0},{6,3},{7,2},{8,13},{9,12},{10,... | collective-permute-start | bytes 294920 | tf_op jit(solution)/shard_map/ppermute | solution.py:22
  19.9 1.6 %shard_map.60 = (bf16[6,256,512]{2,1,0:T(8,128)(2,1)S(1)}, bf16[6,256,512]{2,1,0:T(8,128)(2,1)S(1)}, f32[8,128]{1,0:T(8,128)S(1)}) custom-call(f32[8,128]{1,0:T(8,128)S(1)} %get-tuple-element.21.scalars, f32[8,128]{1,0:T(8,128)S(1)} %get-tuple-element.22.nodes, f32[3,256]{1,0:T(4,128)S(1)} %pad_maximum_fusion.1.near_positions, ...), custom_call_target="tpu_custom_call" | custom-call | tf_op jit(solution)/shard_map/pallas_call | solution.py:275
  21.5 0.0 collective-permute-done.6.refs_0_
  21.5 2.1 %collective-permute-done.7.refs_1_ = f32[96,256]{1,0:T(8,128)S(1)} collective-permute-done((f32[96,256]{1,0:T(8,128)S(1)}, f32[96,256]{1,0:T(8,128)S(1)}, u32[]{:S(2)}, u32[]{:S(2)}) %collective-permute-start.7) | collective-permute-done | bytes 98336 | tf_op jit(solution)/shard_map/ppermute | solution.py:22
  23.6 1.4 %collective-permute-done.8.refs_2_ = f32[96,256]{1,0:T(8,128)S(1)} collective-permute-done((f32[96,256]{1,0:T(8,128)S(1)}, f32[96,256]{1,0:T(8,128)S(1)}, u32[]{:S(2)}, u32[]{:S(2)}) %collective-permute-start.8) | collective-permute-done | bytes 98336 | tf_op jit(solution)/shard_map/ppermute | solution.py:22
  25.0 0.4 %shard_map.64 = (f32[96,64]{1,0:T(8,128)S(1)}, f32[96,256]{1,0:T(8,128)S(1)}, f32[96,256]{1,0:T(8,128)S(1)}) custom-call(f32[8,128]{1,0:T(8,128)S(1)} %get-tuple-element.21.scalars, f32[96,256]{1,0:T(8,128)S(1)} %collective-permute-done.6.refs_0_, f32[96,256]{1,0:T(8,128)S(1)} %collective-permute-done.7.refs_1_, ...), custom_call_target="tpu_custom_call" | custom-call | tf_op jit(solution)/shard_map/pallas_call | solution.py:275
  25.4 0.1 collective-permute-start.9
  25.5 0.4 %shard_map.65.kept = f32[96,256]{1,0:T(8,128)S(1)} custom-call(f32[96,256]{1,0:T(8,128)S(1)} %get-tuple-element.32.linear, bf16[6,256,512]{2,1,0:T(8,128)(2,1)S(1)} %get-tuple-element.29.refs_5_.high, bf16[6,256,512]{2,1,0:T(8,128)(2,1)S(1)} %get-tuple-element.30.refs_6_.low), custom_call_target="tpu_custom_call" | custom-call | tf_op jit(solution)/shard_map/pallas_call | solution.py:275
  25.8 0.9 %collective-permute-done.9.arrived = f32[96,256]{1,0:T(8,128)S(1)} collective-permute-done((f32[96,256]{1,0:T(8,128)S(1)}, f32[96,256]{1,0:T(8,128)S(1)}, u32[]{:S(2)}, u32[]{:S(2)}) %collective-permute-start.9) | collective-permute-done | bytes 98336 | tf_op jit(solution)/shard_map/ppermute | solution.py:22
  26.7 0.1 shard_map.66
  26.8 2.8 %collective-permute-start.10 = (f32[48,128]{1,0:T(8,128)S(1)}, f32[48,128]{1,0:T(8,128)S(1)}, u32[]{:S(2)}, u32[]{:S(2)}) collective-permute-start(f32[48,128]{1,0:T(8,128)S(1)} %get-tuple-element.35), channel_id=1, source_target_pairs={{0,16},{1,17},{2,18},{3,19},{4,20},{5,21},{6,22},{7,23},{8,24},{9,... | collective-permute-start | bytes 73736 | tf_op jit(solution)/shard_map/ppermute | solution.py:22
  29.7 0.6 %collective-permute-start.11 = (f32[48,128]{1,0:T(8,128)S(1)}, f32[48,128]{1,0:T(8,128)S(1)}, u32[]{:S(2)}, u32[]{:S(2)}) collective-permute-start(f32[48,128]{1,0:T(8,128)S(1)} %get-tuple-element.36), channel_id=1, source_target_pairs={{0,8},{1,9},{2,10},{3,11},{4,12},{5,13},{6,14},{7,15},{8,0},{9,1},... | collective-permute-start | bytes 73736 | tf_op jit(solution)/shard_map/ppermute | solution.py:22
  30.2 1.1 %collective-permute-start.12 = (f32[48,128]{1,0:T(8,128)S(1)}, f32[48,128]{1,0:T(8,128)S(1)}, u32[]{:S(2)}, u32[]{:S(2)}) collective-permute-start(f32[48,128]{1,0:T(8,128)S(1)} %get-tuple-element.37), channel_id=1, source_target_pairs={{0,24},{1,25},{2,26},{3,27},{4,28},{5,29},{6,30},{7,31},{8,16},{9,... | collective-permute-start | bytes 73736 | tf_op jit(solution)/shard_map/ppermute | solution.py:22
  31.3 0.6 %collective-permute-done.10.refs_0_ = f32[48,128]{1,0:T(8,128)S(1)} collective-permute-done((f32[48,128]{1,0:T(8,128)S(1)}, f32[48,128]{1,0:T(8,128)S(1)}, u32[]{:S(2)}, u32[]{:S(2)}) %collective-permute-start.10) | collective-permute-done | bytes 24608 | tf_op jit(solution)/shard_map/ppermute | solution.py:22
  31.9 1.6 %collective-permute-done.11.refs_1_ = f32[48,128]{1,0:T(8,128)S(1)} collective-permute-done((f32[48,128]{1,0:T(8,128)S(1)}, f32[48,128]{1,0:T(8,128)S(1)}, u32[]{:S(2)}, u32[]{:S(2)}) %collective-permute-start.11) | collective-permute-done | bytes 24608 | tf_op jit(solution)/shard_map/ppermute | solution.py:22
  33.5 2.4 %collective-permute-done.12.refs_2_ = f32[48,128]{1,0:T(8,128)S(1)} collective-permute-done((f32[48,128]{1,0:T(8,128)S(1)}, f32[48,128]{1,0:T(8,128)S(1)}, u32[]{:S(2)}, u32[]{:S(2)}) %collective-permute-start.12) | collective-permute-done | bytes 24608 | tf_op jit(solution)/shard_map/ppermute | solution.py:22
  35.9 0.7 %shard_map.67 = (f32[96,64]{1,0:T(8,128)}, f32[2,96,64]{2,1,0:T(8,128)}) custom-call(f32[8,128]{1,0:T(8,128)S(1)} %get-tuple-element.21.scalars, f32[8,128]{1,0:T(8,128)S(1)} %get-tuple-element.25.weights, f32[96,64]{1,0:T(8,128)S(1)} %get-tuple-element.26.noise, f32[96,64]{1,0:T(8,128)S(1)} %get-tuple-element.31.first_image, ...), custom_call_target="tpu_custom_call" | custom-call | tf_op jit(solution)/shard_map/pallas_call | solution.py:275
  (1 shorter events, 0.0 us)
Async XLA Ops:
  1.6 6.0 %collective-permute-start.2 = (f32[1,56,128]{2,1,0:T(8,128)S(1)}, f32[1,56,128]{2,1,0:T(8,128)S(1)}, u32[]{:S(2)}, u32[]{:S(2)}) collective-permute-start(f32[1,56,128]{2,1,0:T(8,128)S(1)} %bitcast.4), channel_id=1, source_target_pairs={{0,16},{1,17},{2,18},{3,19},{4,20},{5,21},{6,22},{7,23},{8,24},{9,... | collective-permute-start | bytes 86024 | tf_op jit(solution)/shard_map/ppermute | solution.py:22
  5.7 3.8 %collective-permute-start = (f32[3,64]{1,0:T(4,128)S(1)}, f32[3,64]{1,0:T(4,128)S(1)}, u32[]{:S(2)}, u32[]{:S(2)}) collective-permute-start(f32[3,64]{1,0:T(4,128)S(1)} %get-tuple-element.23), channel_id=1, source_target_pairs={{0,1},{1,0},{2,3},{3,2},{4,5},{5,4},{6,7},{7,6},{8,9},{9,8},{10,11... | collective-permute-start | bytes 2312 | tf_op jit(solution)/shard_map/ppermute | solution.py:22
  7.6 4.2 %collective-permute-start.3 = (f32[2,56,128]{2,1,0:T(8,128)S(1)}, f32[2,56,128]{2,1,0:T(8,128)S(1)}, u32[]{:S(2)}, u32[]{:S(2)}) collective-permute-start(f32[2,56,128]{2,1,0:T(8,128)S(1)} %pad_maximum_fusion.refs_0_), channel_id=1, source_target_pairs={{0,8},{1,9},{2,10},{3,11},{4,12},{5,13},{6,14},{7,15},{8,0},{9,1},... | collective-permute-start | bytes 172040 | tf_op jit(solution)/shard_map/ppermute | solution.py:22
  9.5 3.6 %collective-permute-start.1 = (f32[3,128]{1,0:T(4,128)S(1)}, f32[3,128]{1,0:T(4,128)S(1)}, u32[]{:S(2)}, u32[]{:S(2)}) collective-permute-start(f32[3,128]{1,0:T(4,128)S(1)} %pad_maximum_fusion.2), channel_id=1, source_target_pairs={{0,4},{1,5},{2,6},{3,7},{4,0},{5,1},{6,2},{7,3},{8,12},{9,13},{10,... | collective-permute-start | bytes 4616 | tf_op jit(solution)/shard_map/ppermute | solution.py:22
  11.1 2.1 %collective-permute-start.4 = (f32[2,56,128]{2,1,0:T(8,128)S(1)}, f32[2,56,128]{2,1,0:T(8,128)S(1)}, u32[]{:S(2)}, u32[]{:S(2)}) collective-permute-start(f32[2,56,128]{2,1,0:T(8,128)S(1)} %pad_maximum_fusion.refs_0_), channel_id=1, source_target_pairs={{0,2},{1,3},{2,0},{3,1},{4,6},{5,7},{6,4},{7,5},{8,10},{9,11},{10,... | collective-permute-start | bytes 172040 | tf_op jit(solution)/shard_map/ppermute | solution.py:22
  11.7 3.7 %collective-permute-start.5 = (f32[2,56,128]{2,1,0:T(8,128)S(1)}, f32[2,56,128]{2,1,0:T(8,128)S(1)}, u32[]{:S(2)}, u32[]{:S(2)}) collective-permute-start(f32[2,56,128]{2,1,0:T(8,128)S(1)} %collective-permute-done.3.refs_1_.refs_0_), channel_id=1, source_target_pairs={{0,2},{1,3},{2,0},{3,1},{4,6},{5,7},{6,4},{7,5},{8,10},{9,11},{10,... | collective-permute-start | bytes 172040 | tf_op jit(solution)/shard_map/ppermute | solution.py:22
  16.4 5.2 %collective-permute-start.6 = (f32[96,256]{1,0:T(8,128)S(1)}, f32[96,256]{1,0:T(8,128)S(1)}, u32[]{:S(2)}, u32[]{:S(2)}) collective-permute-start(f32[96,256]{1,0:T(8,128)S(1)} %get-tuple-element.27.refs_4_), channel_id=1, source_target_pairs={{0,1},{1,0},{2,3},{3,2},{4,5},{5,4},{6,7},{7,6},{8,9},{9,8},{10,11... | collective-permute-start | bytes 294920 | tf_op jit(solution)/shard_map/ppermute | solution.py:22
  17.9 5.7 %collective-permute-start.7 = (f32[96,256]{1,0:T(8,128)S(1)}, f32[96,256]{1,0:T(8,128)S(1)}, u32[]{:S(2)}, u32[]{:S(2)}) collective-permute-start(f32[96,256]{1,0:T(8,128)S(1)} %get-tuple-element.27.refs_4_), channel_id=1, source_target_pairs={{0,4},{1,5},{2,6},{3,7},{4,0},{5,1},{6,2},{7,3},{8,12},{9,13},{10,... | collective-permute-start | bytes 294920 | tf_op jit(solution)/shard_map/ppermute | solution.py:22
  19.4 5.5 %collective-permute-start.8 = (f32[96,256]{1,0:T(8,128)S(1)}, f32[96,256]{1,0:T(8,128)S(1)}, u32[]{:S(2)}, u32[]{:S(2)}) collective-permute-start(f32[96,256]{1,0:T(8,128)S(1)} %get-tuple-element.27.refs_4_), channel_id=1, source_target_pairs={{0,5},{1,4},{2,7},{3,6},{4,1},{5,0},{6,3},{7,2},{8,13},{9,12},{10,... | collective-permute-start | bytes 294920 | tf_op jit(solution)/shard_map/ppermute | solution.py:22
  25.4 1.4 %collective-permute-start.9 = (f32[96,256]{1,0:T(8,128)S(1)}, f32[96,256]{1,0:T(8,128)S(1)}, u32[]{:S(2)}, u32[]{:S(2)}) collective-permute-start(f32[96,256]{1,0:T(8,128)S(1)} %get-tuple-element.33), channel_id=1, source_target_pairs={{0,2},{1,3},{2,0},{3,1},{4,6},{5,7},{6,4},{7,5},{8,10},{9,11},{10,... | collective-permute-start | bytes 294920 | tf_op jit(solution)/shard_map/ppermute | solution.py:22
  26.8 5.1 %collective-permute-start.10 = (f32[48,128]{1,0:T(8,128)S(1)}, f32[48,128]{1,0:T(8,128)S(1)}, u32[]{:S(2)}, u32[]{:S(2)}) collective-permute-start(f32[48,128]{1,0:T(8,128)S(1)} %get-tuple-element.35), channel_id=1, source_target_pairs={{0,16},{1,17},{2,18},{3,19},{4,20},{5,21},{6,22},{7,23},{8,24},{9,... | collective-permute-start | bytes 73736 | tf_op jit(solution)/shard_map/ppermute | solution.py:22
  29.7 3.8 %collective-permute-start.11 = (f32[48,128]{1,0:T(8,128)S(1)}, f32[48,128]{1,0:T(8,128)S(1)}, u32[]{:S(2)}, u32[]{:S(2)}) collective-permute-start(f32[48,128]{1,0:T(8,128)S(1)} %get-tuple-element.36), channel_id=1, source_target_pairs={{0,8},{1,9},{2,10},{3,11},{4,12},{5,13},{6,14},{7,15},{8,0},{9,1},... | collective-permute-start | bytes 73736 | tf_op jit(solution)/shard_map/ppermute | solution.py:22
  30.2 5.6 %collective-permute-start.12 = (f32[48,128]{1,0:T(8,128)S(1)}, f32[48,128]{1,0:T(8,128)S(1)}, u32[]{:S(2)}, u32[]{:S(2)}) collective-permute-start(f32[48,128]{1,0:T(8,128)S(1)} %get-tuple-element.37), channel_id=1, source_target_pairs={{0,24},{1,25},{2,26},{3,27},{4,28},{5,29},{6,30},{7,31},{8,16},{9,... | collective-permute-start | bytes 73736 | tf_op jit(solution)/shard_map/ppermute | solution.py:22

commit v4 on v3

--- a/solution.py
+++ b/solution.py
@@ -65,7 +65,7 @@
 def build_tiles(columns, target_rows, high, low):
     source_count = columns.shape[1]
     tile_count = target_rows.shape[1] // 128
-    chunk = 16
+    chunk = 32
 
     def one_chunk(step, carry):
         start = pl.multiple_of(step * chunk, chunk)
@@ -202,10 +202,17 @@
     return tiles[0] if len(tiles) == 1 else jnp.concatenate(tiles, axis=1)
 
 
+def packed_block(value, number, width):
+    half = value.shape[0] // 2
+    block = value[:, number * width : (number + 1) * width]
+    return jnp.concatenate([block[:half], block[half:]], axis=1)
+
+
 def third_kernel(scalars, *refs):
-    received = refs[:-7]
-    partial, message, high, low, first_image, linear, sent = refs[-7:]
+    received = refs[:-9]
+    partial, message, high, low, first_image, last, kept, sent, linear = refs[-9:]
     width = first_image.shape[1]
+    vectors = message.shape[0] // 3
     total = message[...]
     own = partial[:, :width]
     for number, ref in enumerate(received):
@@ -214,35 +221,25 @@
         own = own + part[:, :width]
     first_image[...] = own
     linear[...] = total / scalars[4:5, 0:1]
-    half_product(linear, high, low, sent, 1)
-
-
-def half_product(linear, high, low, out, side):
-    vectors = linear.shape[0] // 3
-    middle = high.shape[2] // 2
-    lanes = slice(side * middle, (side + 1) * middle)
     field = [linear[c * vectors : (c + 1) * vectors, :] for c in range(3)]
-    value = apply_tiles(field, high.at[:, :, lanes], low.at[:, :, lanes])
-    out[...] = jnp.concatenate(value, axis=0)
-
-
-def kept_kernel(linear, high, low, kept):
-    half_product(linear, high, low, kept, 0)
-
-
-def fourth_kernel(kept, arrived, own, *outgoing):
-    half = kept.shape[0] // 2
-    width = own.shape[1] // 2
-    total = kept[...] + arrived[...]
-    for number, ref in enumerate((own, *outgoing)):
-        block = total[:, number * width : (number + 1) * width]
-        ref[...] = jnp.concatenate([block[:half], block[half:]], axis=1)
-
-
-def final_kernel(scalars, weights, noise, first_image, own, *refs):
+    value = jnp.concatenate(apply_tiles(field, high, low), axis=0)
+    count = value.shape[1] // width // 2
+    for number in range(count - 1):
+        kept[number] = packed_block(value, number, width)
+        sent[number] = packed_block(value, count + number, width)
+    last[0] = packed_block(value, count - 1, width)
+    last[1] = packed_block(value, 2 * count - 1, width)
+
+
+def fourth_kernel(kept, arrived, *outgoing):
+    for number, ref in enumerate(outgoing):
+        ref[...] = kept[number] + arrived[number]
+
+
+def final_kernel(scalars, weights, noise, first_image, own, last, last_across, *refs):
     received, (displacement, images) = refs[:-2], refs[-2:]
     width = noise.shape[1]
-    total = own[...]
+    total = own[...] + last[0] + last_across[0]
     for ref in received:
         total = total + ref[...]
     second = jnp.concatenate([total[:, :width], total[:, width:]], axis=0)
@@ -298,14 +295,17 @@
     return result
 
 
-def body(positions_in, noise_vectors, spectrum_bounds):
-    tiles = lax.axis_size("tile")
-    bits = lax.axis_size("blk").bit_length() - 1
+def masks_for(blocks, tiles):
+    bits = blocks.bit_length() - 1
     half_bits = bits // 2
-    core_mask = tiles
     far_masks = [tiles << bit for bit in reversed(range(half_bits, bits))]
     near_masks = [1 << bit for bit in range(tiles.bit_length() - 1)]
     near_masks += [tiles << bit for bit in range(1, half_bits)]
+    return tiles, far_masks, near_masks
+
+
+def body(positions_in, noise_vectors, spectrum_bounds):
+    core_mask, far_masks, near_masks = masks_for(lax.axis_size("blk"), lax.axis_size("tile"))
     components, vectors, width = noise_vectors.shape
     rows = components * vectors
     last = len(far_masks) - 1
@@ -331,8 +331,11 @@
     )
     near = positions
     far = message[None]
-    for mask in near_masks:
-        near = jnp.concatenate([near, exchange(near, mask)], axis=1)
+    near = [positions]
+    near_steps = combinations(near_masks)[1:]
+    for mask in near_steps:
+        near.append(exchange(positions, mask))
+    near = jnp.concatenate(near, axis=1)
     for mask in far_masks[:last]:
         far = jnp.concatenate([far, exchange(far, mask)], axis=0)
     across = exchange(far, core_mask)
@@ -364,21 +367,23 @@
         [((6, near_count, far_count), bf16)] * 2 + [((8, 128), f32)],
         (pltpu.VMEM((3, near_count, 128), f32), pltpu.VMEM((8, far_count), f32)),
     )
-    near_steps = combinations(near_masks)
-    received = [exchange(message, mask) for mask in near_steps[1:]]
-    first_image, linear, sent = call(
+    received = [exchange(message, mask) for mask in near_steps]
+    far_steps = combinations(far_masks)[1:]
+    several = ((len(far_steps), rows // 2, 2 * width), f32)
+    first_image, last_part, kept, sent = call(
         third_kernel,
         (scalars, *received, partial, message, high, low),
-        [((rows, width), f32), whole, ((rows, far_count // 2), f32)],
+        [((rows, width), f32), ((2, rows // 2, 2 * width), f32), several, several],
+        (pltpu.VMEM((rows, near_count), f32),),
     )
     arrived = exchange(sent, core_mask)
-    (kept,) = call(kept_kernel, (linear, high, low), [((rows, far_count // 2), f32)])
-    far_steps = combinations(far_masks)
+    last_part = exchange(last_part, far_steps[-1])
     own, *outgoing = call(fourth_kernel, (kept, arrived), [block] * len(far_steps))
-    received = [exchange(value, mask) for value, mask in zip(outgoing, far_steps[1:])]
+    received = [exchange(value, mask) for value, mask in zip(outgoing, far_steps)]
+    last_across = exchange(last_part[1:], core_mask)
     displacement, images = call(
         final_kernel,
-        (scalars, weights, noise, first_image, own, *received),
+        (scalars, weights, noise, first_image, own, last_part, last_across, *received),
         [((rows, width), f32), ((2, rows, width), f32)],
         final=True,
     )

time: 36.8 us -> 40.3 us (1.095)
  starting transfers between devices: 17.1 us -> 19.3 us
  waiting for transfers between devices: 11.4 us -> 13.2 us
  Pallas kernels: 7.26 us -> 6.78 us
    ppermute x13 -> x15, starting transfers between devices: 17.1 us -> 19.3 us  [exchange(): return lax.ppermute(block, axes, [(i, i ^ mask) for i in range(count)])]
    ppermute x13 -> x15, waiting for transfers between devices: 11.4 us -> 13.2 us  [exchange(): return lax.ppermute(block, axes, [(i, i ^ mask) for i in range(count)])]
    pallas_call x9 -> x8, Pallas kernels: 7.26 us -> 6.78 us  [call(): pl.pallas_call(kernel, in_specs=[pl.BlockSpec(memory_space=space)] * len(...]
  transfers between devices with their start and end apart: 13 -> 15, of which waited for: 9 -> 10; matrix products, arithmetic and copies ran while one was open for 0% -> 0% of each run, Pallas kernels for 12% -> 9%
where the time goes in v4:
time: 40.3 us; the launch traced here: 40.1 us
  starting transfers between devices  19.3 us (48%)
  waiting for transfers between devices  13.2 us (33%)
  Pallas kernels  6.78 us (17%)
  between operations  0.71 us (2%)
    ppermute x15, starting transfers between devices, exchange(): return lax.ppermute(block, axes, [(i, i ^ mask) for i in range(count)])  19.3 us
    ppermute x15, waiting for transfers between devices, exchange(): return lax.ppermute(block, axes, [(i, i ^ mask) for i in range(count)])  13.2 us
    pallas_call x8, Pallas kernels, call(): pl.pallas_call(kernel, in_specs=[pl.BlockSpec(memory_space=space)] * len(...  6.78 us
  transfers between devices with their start and end apart: 15, of which 10 were waited for; matrix products, arithmetic and copies ran while one was open for 0% of the time, Pallas kernels for 9%

profile of v4, /device:TPU:0, one launch (start us, length us, event | category | flops | bytes accessed | tf_op | source)
XLA Modules:
  0.0 40.1 jit_solution(17723813996915396990)
XLA Ops:
  0.6 0.9 %shard_map.59 = (f32[56,128]{1,0:T(8,128)S(1)}, f32[96,64]{1,0:T(8,128)S(1)}, f32[3,64]{1,0:T(4,128)S(1)}, f32[8,128]{1,0:T(8,128)S(1)}, f32[8,128]{1,0:T(8,128)S(1)}) custom-call(f32[96,64]{1,0:T(8,128)} %bitcast.6, f32[3,64]{1,0:T(4,128)} %positions_in.1, f32[2]{0:T(128)} %bounds_in.1, f32[8,128]{1,0:T(8,128)} %constant.2.clone.nodes_in), custom_call_target="tpu_custom_call" | custom-call | tf_op jit(solution)/shard_map/pallas_call | solution.py:272
  1.6 4.1 %collective-permute-start.3 = (f32[1,56,128]{2,1,0:T(8,128)S(1)}, f32[1,56,128]{2,1,0:T(8,128)S(1)}, u32[]{:S(2)}, u32[]{:S(2)}) collective-permute-start(f32[1,56,128]{2,1,0:T(8,128)S(1)} %bitcast.4), channel_id=1, source_target_pairs={{0,16},{1,17},{2,18},{3,19},{4,20},{5,21},{6,22},{7,23},{8,24},{9,... | collective-permute-start | bytes 86024 | tf_op jit(solution)/shard_map/ppermute | solution.py:22
  5.7 1.9 %collective-permute-done.3 = f32[1,56,128]{2,1,0:T(8,128)S(1)} collective-permute-done((f32[1,56,128]{2,1,0:T(8,128)S(1)}, f32[1,56,128]{2,1,0:T(8,128)S(1)}, u32[]{:S(2)}, u32[]{:S(2)}) %collective-permute-start.3) | collective-permute-done | bytes 28704 | tf_op jit(solution)/shard_map/ppermute | solution.py:22
  7.6 1.9 %collective-permute-start.4 = (f32[2,56,128]{2,1,0:T(8,128)S(1)}, f32[2,56,128]{2,1,0:T(8,128)S(1)}, u32[]{:S(2)}, u32[]{:S(2)}) collective-permute-start(f32[2,56,128]{2,1,0:T(8,128)S(1)} %pad_maximum_fusion.refs_0_), channel_id=1, source_target_pairs={{0,8},{1,9},{2,10},{3,11},{4,12},{5,13},{6,14},{7,15},{8,0},{9,1},... | collective-permute-start | bytes 172040 | tf_op jit(solution)/shard_map/ppermute | solution.py:22
  9.5 2.4 %collective-permute-start.2 = (f32[3,64]{1,0:T(4,128)S(1)}, f32[3,64]{1,0:T(4,128)S(1)}, u32[]{:S(2)}, u32[]{:S(2)}) collective-permute-start(f32[3,64]{1,0:T(4,128)S(1)} %get-tuple-element.23), channel_id=1, source_target_pairs={{0,5},{1,4},{2,7},{3,6},{4,1},{5,0},{6,3},{7,2},{8,13},{9,12},{10,... | collective-permute-start | bytes 2312 | tf_op jit(solution)/shard_map/ppermute | solution.py:22
  11.9 0.5 %collective-permute-start.1 = (f32[3,64]{1,0:T(4,128)S(1)}, f32[3,64]{1,0:T(4,128)S(1)}, u32[]{:S(2)}, u32[]{:S(2)}) collective-permute-start(f32[3,64]{1,0:T(4,128)S(1)} %get-tuple-element.23), channel_id=1, source_target_pairs={{0,4},{1,5},{2,6},{3,7},{4,0},{5,1},{6,2},{7,3},{8,12},{9,13},{10,... | collective-permute-start | bytes 2312 | tf_op jit(solution)/shard_map/ppermute | solution.py:22
  12.4 0.5 %collective-permute-start = (f32[3,64]{1,0:T(4,128)S(1)}, f32[3,64]{1,0:T(4,128)S(1)}, u32[]{:S(2)}, u32[]{:S(2)}) collective-permute-start(f32[3,64]{1,0:T(4,128)S(1)} %get-tuple-element.23), channel_id=1, source_target_pairs={{0,1},{1,0},{2,3},{3,2},{4,5},{5,4},{6,7},{7,6},{8,9},{9,8},{10,11... | collective-permute-start | bytes 2312 | tf_op jit(solution)/shard_map/ppermute | solution.py:22
  12.9 0.0 collective-permute-start.5
  12.9 0.0 collective-permute-done.4.refs_1_.refs_0_
  13.0 0.5 %collective-permute-start.6 = (f32[2,56,128]{2,1,0:T(8,128)S(1)}, f32[2,56,128]{2,1,0:T(8,128)S(1)}, u32[]{:S(2)}, u32[]{:S(2)}) collective-permute-start(f32[2,56,128]{2,1,0:T(8,128)S(1)} %collective-permute-done.4.refs_1_.refs_0_), channel_id=1, source_target_pairs={{0,2},{1,3},{2,0},{3,1},{4,6},{5,7},{6,4},{7,5},{8,10},{9,11},{10,... | collective-permute-start | bytes 172040 | tf_op jit(solution)/shard_map/ppermute | solution.py:22
  13.5 0.5 %collective-permute-done.2 = f32[3,64]{1,0:T(4,128)S(1)} collective-permute-done((f32[3,64]{1,0:T(4,128)S(1)}, f32[3,64]{1,0:T(4,128)S(1)}, u32[]{:S(2)}, u32[]{:S(2)}) %collective-permute-start.2) | collective-permute-done | bytes 800 | tf_op jit(solution)/shard_map/ppermute | solution.py:22
  13.9 1.5 %collective-permute-done.1 = f32[3,64]{1,0:T(4,128)S(1)} collective-permute-done((f32[3,64]{1,0:T(4,128)S(1)}, f32[3,64]{1,0:T(4,128)S(1)}, u32[]{:S(2)}, u32[]{:S(2)}) %collective-permute-start.1) | collective-permute-done | bytes 800 | tf_op jit(solution)/shard_map/ppermute | solution.py:22
  15.5 0.5 %collective-permute-done = f32[3,64]{1,0:T(4,128)S(1)} collective-permute-done((f32[3,64]{1,0:T(4,128)S(1)}, f32[3,64]{1,0:T(4,128)S(1)}, u32[]{:S(2)}, u32[]{:S(2)}) %collective-permute-start) | collective-permute-done | bytes 800 | tf_op jit(solution)/shard_map/ppermute | solution.py:22
  16.0 0.1 pad_maximum_fusion.1.near_positions
  16.1 0.0 collective-permute-done.5.refs_2_.refs_1_
  16.1 1.3 %shard_map.61.before = f32[96,256]{1,0:T(8,128)S(1)} custom-call(f32[3,256]{1,0:T(4,128)S(1)} %pad_maximum_fusion.1.near_positions, f32[2,56,128]{2,1,0:T(8,128)S(1)} %pad_maximum_fusion.refs_0_, f32[2,56,128]{2,1,0:T(8,128)S(1)} %collective-permute-done.5.refs_2_.refs_1_), custom_call_target="tpu_custom_call" | custom-call | tf_op jit(solution)/shard_map/pallas_call | solution.py:272
  17.4 0.8 %shard_map.62.before = f32[96,256]{1,0:T(8,128)S(1)} custom-call(f32[3,256]{1,0:T(4,128)S(1)} %pad_maximum_fusion.1.near_positions, f32[96,256]{1,0:T(8,128)S(1)} %shard_map.61.before, f32[2,56,128]{2,1,0:T(8,128)S(1)} %collective-permute-done.4.refs_1_.refs_0_), custom_call_target="tpu_custom_call" | custom-call | tf_op jit(solution)/shard_map/pallas_call | solution.py:272
  18.2 0.0 collective-permute-done.6.refs_3_.refs_0_
  18.2 0.8 %shard_map.63 = (f32[96,256]{1,0:T(8,128)S(1)}, f32[96,256]{1,0:T(8,128)S(1)}) custom-call(f32[8,128]{1,0:T(8,128)S(1)} %get-tuple-element.21.scalars, f32[96,64]{1,0:T(8,128)S(1)} %get-tuple-element.26.noise, f32[3,256]{1,0:T(4,128)S(1)} %pad_maximum_fusion.1.near_positions, f32[96,256]{1,0:T(8,128)S(1)} %shard_map.62.before, ...), custom_call_target="tpu_custom_call" | custom-call | tf_op jit(solution)/shard_map/pallas_call | solution.py:272
  19.0 0.6 %collective-permute-start.7 = (f32[96,256]{1,0:T(8,128)S(1)}, f32[96,256]{1,0:T(8,128)S(1)}, u32[]{:S(2)}, u32[]{:S(2)}) collective-permute-start(f32[96,256]{1,0:T(8,128)S(1)} %get-tuple-element.27.refs_4_), channel_id=1, source_target_pairs={{0,1},{1,0},{2,3},{3,2},{4,5},{5,4},{6,7},{7,6},{8,9},{9,8},{10,11... | collective-permute-start | bytes 294920 | tf_op jit(solution)/shard_map/ppermute | solution.py:22
  19.6 1.5 %collective-permute-start.8 = (f32[96,256]{1,0:T(8,128)S(1)}, f32[96,256]{1,0:T(8,128)S(1)}, u32[]{:S(2)}, u32[]{:S(2)}) collective-permute-start(f32[96,256]{1,0:T(8,128)S(1)} %get-tuple-element.27.refs_4_), channel_id=1, source_target_pairs={{0,4},{1,5},{2,6},{3,7},{4,0},{5,1},{6,2},{7,3},{8,12},{9,13},{10,... | collective-permute-start | bytes 294920 | tf_op jit(solution)/shard_map/ppermute | solution.py:22
  21.1 1.4 %collective-permute-start.9 = (f32[96,256]{1,0:T(8,128)S(1)}, f32[96,256]{1,0:T(8,128)S(1)}, u32[]{:S(2)}, u32[]{:S(2)}) collective-permute-start(f32[96,256]{1,0:T(8,128)S(1)} %get-tuple-element.27.refs_4_), channel_id=1, source_target_pairs={{0,5},{1,4},{2,7},{3,6},{4,1},{5,0},{6,3},{7,2},{8,13},{9,12},{10,... | collective-permute-start | bytes 294920 | tf_op jit(solution)/shard_map/ppermute | solution.py:22
  22.5 1.5 %shard_map.60 = (bf16[6,256,512]{2,1,0:T(8,128)(2,1)S(1)}, bf16[6,256,512]{2,1,0:T(8,128)(2,1)S(1)}, f32[8,128]{1,0:T(8,128)S(1)}) custom-call(f32[8,128]{1,0:T(8,128)S(1)} %get-tuple-element.21.scalars, f32[8,128]{1,0:T(8,128)S(1)} %get-tuple-element.22.nodes, f32[3,256]{1,0:T(4,128)S(1)} %pad_maximum_fusion.1.near_positions, ...), custom_call_target="tpu_custom_call" | custom-call | tf_op jit(solution)/shard_map/pallas_call | solution.py:272
  24.0 0.4 %collective-permute-done.7.refs_0_ = f32[96,256]{1,0:T(8,128)S(1)} collective-permute-done((f32[96,256]{1,0:T(8,128)S(1)}, f32[96,256]{1,0:T(8,128)S(1)}, u32[]{:S(2)}, u32[]{:S(2)}) %collective-permute-start.7) | collective-permute-done | bytes 98336 | tf_op jit(solution)/shard_map/ppermute | solution.py:22
  24.4 0.8 %collective-permute-done.8.refs_1_ = f32[96,256]{1,0:T(8,128)S(1)} collective-permute-done((f32[96,256]{1,0:T(8,128)S(1)}, f32[96,256]{1,0:T(8,128)S(1)}, u32[]{:S(2)}, u32[]{:S(2)}) %collective-permute-start.8) | collective-permute-done | bytes 98336 | tf_op jit(solution)/shard_map/ppermute | solution.py:22
  25.3 1.4 %collective-permute-done.9.refs_2_ = f32[96,256]{1,0:T(8,128)S(1)} collective-permute-done((f32[96,256]{1,0:T(8,128)S(1)}, f32[96,256]{1,0:T(8,128)S(1)}, u32[]{:S(2)}, u32[]{:S(2)}) %collective-permute-start.9) | collective-permute-done | bytes 98336 | tf_op jit(solution)/shard_map/ppermute | solution.py:22
  26.6 0.8 %shard_map.64 = (f32[96,64]{1,0:T(8,128)S(1)}, f32[2,48,128]{2,1,0:T(8,128)S(1)}, f32[3,48,128]{2,1,0:T(8,128)S(1)}, f32[3,48,128]{2,1,0:T(8,128)S(1)}) custom-call(f32[8,128]{1,0:T(8,128)S(1)} %get-tuple-element.21.scalars, f32[96,256]{1,0:T(8,128)S(1)} %collective-permute-done.7.refs_0_, f32[96,256]{1,0:T(8,128)S(1)} %collective-permute-done.8.refs_1_, ...), custom_call_target="tpu_custom_call" | custom-call | tf_op jit(solution)/shard_map/pallas_call | solution.py:272
  27.4 0.1 collective-permute-start.10
  27.5 2.6 %collective-permute-start.11 = (f32[2,48,128]{2,1,0:T(8,128)S(1)}, f32[2,48,128]{2,1,0:T(8,128)S(1)}, u32[]{:S(2)}, u32[]{:S(2)}) collective-permute-start(f32[2,48,128]{2,1,0:T(8,128)S(1)} %get-tuple-element.35), channel_id=1, source_target_pairs={{0,24},{1,25},{2,26},{3,27},{4,28},{5,29},{6,30},{7,31},{8,16},{9,... | collective-permute-start | bytes 147464 | tf_op jit(solution)/shard_map/ppermute | solution.py:22
  30.0 3.5 %collective-permute-done.11.last = f32[2,48,128]{2,1,0:T(8,128)S(1)} collective-permute-done((f32[2,48,128]{2,1,0:T(8,128)S(1)}, f32[2,48,128]{2,1,0:T(8,128)S(1)}, u32[]{:S(2)}, u32[]{:S(2)}) %collective-permute-start.11) | collective-permute-done | bytes 49184 | tf_op jit(solution)/shard_map/ppermute | solution.py:22
  33.5 0.0 collective-permute-start.12
  33.5 0.0 collective-permute-done.10.arrived
  33.5 2.0 %collective-permute-start.13 = (f32[48,128]{1,0:T(8,128)S(1)}, f32[48,128]{1,0:T(8,128)S(1)}, u32[]{:S(2)}, u32[]{:S(2)}) collective-permute-start(f32[48,128]{1,0:T(8,128)S(1)} %get-tuple-element.36), channel_id=1, source_target_pairs={{0,16},{1,17},{2,18},{3,19},{4,20},{5,21},{6,22},{7,23},{8,24},{9,... | collective-permute-start | bytes 73736 | tf_op jit(solution)/shard_map/ppermute | solution.py:22
  35.6 1.1 %collective-permute-start.14 = (f32[48,128]{1,0:T(8,128)S(1)}, f32[48,128]{1,0:T(8,128)S(1)}, u32[]{:S(2)}, u32[]{:S(2)}) collective-permute-start(f32[48,128]{1,0:T(8,128)S(1)} %get-tuple-element.37), channel_id=1, source_target_pairs={{0,8},{1,9},{2,10},{3,11},{4,12},{5,13},{6,14},{7,15},{8,0},{9,1},... | collective-permute-start | bytes 73736 | tf_op jit(solution)/shard_map/ppermute | solution.py:22
  36.7 0.0 collective-permute-done.12.last_across
  36.7 2.1 %collective-permute-done.13.refs_0_ = f32[48,128]{1,0:T(8,128)S(1)} collective-permute-done((f32[48,128]{1,0:T(8,128)S(1)}, f32[48,128]{1,0:T(8,128)S(1)}, u32[]{:S(2)}, u32[]{:S(2)}) %collective-permute-start.13) | collective-permute-done | bytes 24608 | tf_op jit(solution)/shard_map/ppermute | solution.py:22
  38.7 0.6 %collective-permute-done.14.refs_1_ = f32[48,128]{1,0:T(8,128)S(1)} collective-permute-done((f32[48,128]{1,0:T(8,128)S(1)}, f32[48,128]{1,0:T(8,128)S(1)}, u32[]{:S(2)}, u32[]{:S(2)}) %collective-permute-start.14) | collective-permute-done | bytes 24608 | tf_op jit(solution)/shard_map/ppermute | solution.py:22
  39.4 0.7 %shard_map.66 = (f32[96,64]{1,0:T(8,128)}, f32[2,96,64]{2,1,0:T(8,128)}) custom-call(f32[8,128]{1,0:T(8,128)S(1)} %get-tuple-element.21.scalars, f32[8,128]{1,0:T(8,128)S(1)} %get-tuple-element.25.weights, f32[96,64]{1,0:T(8,128)S(1)} %get-tuple-element.26.noise, f32[96,64]{1,0:T(8,128)S(1)} %get-tuple-element.31.first_image, ...), custom_call_target="tpu_custom_call" | custom-call | tf_op jit(solution)/shard_map/pallas_call | solution.py:272
  (3 shorter events, 0.0 us)
Async XLA Ops:
  1.6 6.0 %collective-permute-start.3 = (f32[1,56,128]{2,1,0:T(8,128)S(1)}, f32[1,56,128]{2,1,0:T(8,128)S(1)}, u32[]{:S(2)}, u32[]{:S(2)}) collective-permute-start(f32[1,56,128]{2,1,0:T(8,128)S(1)} %bitcast.4), channel_id=1, source_target_pairs={{0,16},{1,17},{2,18},{3,19},{4,20},{5,21},{6,22},{7,23},{8,24},{9,... | collective-permute-start | bytes 86024 | tf_op jit(solution)/shard_map/ppermute | solution.py:22
  7.6 5.4 %collective-permute-start.4 = (f32[2,56,128]{2,1,0:T(8,128)S(1)}, f32[2,56,128]{2,1,0:T(8,128)S(1)}, u32[]{:S(2)}, u32[]{:S(2)}) collective-permute-start(f32[2,56,128]{2,1,0:T(8,128)S(1)} %pad_maximum_fusion.refs_0_), channel_id=1, source_target_pairs={{0,8},{1,9},{2,10},{3,11},{4,12},{5,13},{6,14},{7,15},{8,0},{9,1},... | collective-permute-start | bytes 172040 | tf_op jit(solution)/shard_map/ppermute | solution.py:22
  9.5 4.5 %collective-permute-start.2 = (f32[3,64]{1,0:T(4,128)S(1)}, f32[3,64]{1,0:T(4,128)S(1)}, u32[]{:S(2)}, u32[]{:S(2)}) collective-permute-start(f32[3,64]{1,0:T(4,128)S(1)} %get-tuple-element.23), channel_id=1, source_target_pairs={{0,5},{1,4},{2,7},{3,6},{4,1},{5,0},{6,3},{7,2},{8,13},{9,12},{10,... | collective-permute-start | bytes 2312 | tf_op jit(solution)/shard_map/ppermute | solution.py:22
  11.9 3.6 %collective-permute-start.1 = (f32[3,64]{1,0:T(4,128)S(1)}, f32[3,64]{1,0:T(4,128)S(1)}, u32[]{:S(2)}, u32[]{:S(2)}) collective-permute-start(f32[3,64]{1,0:T(4,128)S(1)} %get-tuple-element.23), channel_id=1, source_target_pairs={{0,4},{1,5},{2,6},{3,7},{4,0},{5,1},{6,2},{7,3},{8,12},{9,13},{10,... | collective-permute-start | bytes 2312 | tf_op jit(solution)/shard_map/ppermute | solution.py:22
  12.4 3.6 %collective-permute-start = (f32[3,64]{1,0:T(4,128)S(1)}, f32[3,64]{1,0:T(4,128)S(1)}, u32[]{:S(2)}, u32[]{:S(2)}) collective-permute-start(f32[3,64]{1,0:T(4,128)S(1)} %get-tuple-element.23), channel_id=1, source_target_pairs={{0,1},{1,0},{2,3},{3,2},{4,5},{5,4},{6,7},{7,6},{8,9},{9,8},{10,11... | collective-permute-start | bytes 2312 | tf_op jit(solution)/shard_map/ppermute | solution.py:22
  12.9 3.1 %collective-permute-start.5 = (f32[2,56,128]{2,1,0:T(8,128)S(1)}, f32[2,56,128]{2,1,0:T(8,128)S(1)}, u32[]{:S(2)}, u32[]{:S(2)}) collective-permute-start(f32[2,56,128]{2,1,0:T(8,128)S(1)} %pad_maximum_fusion.refs_0_), channel_id=1, source_target_pairs={{0,2},{1,3},{2,0},{3,1},{4,6},{5,7},{6,4},{7,5},{8,10},{9,11},{10,... | collective-permute-start | bytes 172040 | tf_op jit(solution)/shard_map/ppermute | solution.py:22
  13.0 5.2 %collective-permute-start.6 = (f32[2,56,128]{2,1,0:T(8,128)S(1)}, f32[2,56,128]{2,1,0:T(8,128)S(1)}, u32[]{:S(2)}, u32[]{:S(2)}) collective-permute-start(f32[2,56,128]{2,1,0:T(8,128)S(1)} %collective-permute-done.4.refs_1_.refs_0_), channel_id=1, source_target_pairs={{0,2},{1,3},{2,0},{3,1},{4,6},{5,7},{6,4},{7,5},{8,10},{9,11},{10,... | collective-permute-start | bytes 172040 | tf_op jit(solution)/shard_map/ppermute | solution.py:22
  19.0 5.4 %collective-permute-start.7 = (f32[96,256]{1,0:T(8,128)S(1)}, f32[96,256]{1,0:T(8,128)S(1)}, u32[]{:S(2)}, u32[]{:S(2)}) collective-permute-start(f32[96,256]{1,0:T(8,128)S(1)} %get-tuple-element.27.refs_4_), channel_id=1, source_target_pairs={{0,1},{1,0},{2,3},{3,2},{4,5},{5,4},{6,7},{7,6},{8,9},{9,8},{10,11... | collective-permute-start | bytes 294920 | tf_op jit(solution)/shard_map/ppermute | solution.py:22
  19.6 5.7 %collective-permute-start.8 = (f32[96,256]{1,0:T(8,128)S(1)}, f32[96,256]{1,0:T(8,128)S(1)}, u32[]{:S(2)}, u32[]{:S(2)}) collective-permute-start(f32[96,256]{1,0:T(8,128)S(1)} %get-tuple-element.27.refs_4_), channel_id=1, source_target_pairs={{0,4},{1,5},{2,6},{3,7},{4,0},{5,1},{6,2},{7,3},{8,12},{9,13},{10,... | collective-permute-start | bytes 294920 | tf_op jit(solution)/shard_map/ppermute | solution.py:22
  21.1 5.5 %collective-permute-start.9 = (f32[96,256]{1,0:T(8,128)S(1)}, f32[96,256]{1,0:T(8,128)S(1)}, u32[]{:S(2)}, u32[]{:S(2)}) collective-permute-start(f32[96,256]{1,0:T(8,128)S(1)} %get-tuple-element.27.refs_4_), channel_id=1, source_target_pairs={{0,5},{1,4},{2,7},{3,6},{4,1},{5,0},{6,3},{7,2},{8,13},{9,12},{10,... | collective-permute-start | bytes 294920 | tf_op jit(solution)/shard_map/ppermute | solution.py:22
  27.4 6.1 %collective-permute-start.10 = (f32[3,48,128]{2,1,0:T(8,128)S(1)}, f32[3,48,128]{2,1,0:T(8,128)S(1)}, u32[]{:S(2)}, u32[]{:S(2)}) collective-permute-start(f32[3,48,128]{2,1,0:T(8,128)S(1)} %get-tuple-element.33), channel_id=1, source_target_pairs={{0,2},{1,3},{2,0},{3,1},{4,6},{5,7},{6,4},{7,5},{8,10},{9,11},{10,... | collective-permute-start | bytes 221192 | tf_op jit(solution)/shard_map/ppermute | solution.py:22
  27.5 6.0 %collective-permute-start.11 = (f32[2,48,128]{2,1,0:T(8,128)S(1)}, f32[2,48,128]{2,1,0:T(8,128)S(1)}, u32[]{:S(2)}, u32[]{:S(2)}) collective-permute-start(f32[2,48,128]{2,1,0:T(8,128)S(1)} %get-tuple-element.35), channel_id=1, source_target_pairs={{0,24},{1,25},{2,26},{3,27},{4,28},{5,29},{6,30},{7,31},{8,16},{9,... | collective-permute-start | bytes 147464 | tf_op jit(solution)/shard_map/ppermute | solution.py:22
  33.5 3.2 %collective-permute-start.12 = (f32[1,48,128]{2,1,0:T(8,128)S(1)}, f32[1,48,128]{2,1,0:T(8,128)S(1)}, u32[]{:S(2)}, u32[]{:S(2)}) collective-permute-start(f32[1,48,128]{2,1,0:T(8,128)S(1)} %slice.4), channel_id=1, source_target_pairs={{0,2},{1,3},{2,0},{3,1},{4,6},{5,7},{6,4},{7,5},{8,10},{9,11},{10,... | collective-permute-start | bytes 73736 | tf_op jit(solution)/shard_map/ppermute | solution.py:22
  33.5 5.2 %collective-permute-start.13 = (f32[48,128]{1,0:T(8,128)S(1)}, f32[48,128]{1,0:T(8,128)S(1)}, u32[]{:S(2)}, u32[]{:S(2)}) collective-permute-start(f32[48,128]{1,0:T(8,128)S(1)} %get-tuple-element.36), channel_id=1, source_target_pairs={{0,16},{1,17},{2,18},{3,19},{4,20},{5,21},{6,22},{7,23},{8,24},{9,... | collective-permute-start | bytes 73736 | tf_op jit(solution)/shard_map/ppermute | solution.py:22
  35.6 3.8 %collective-permute-start.14 = (f32[48,128]{1,0:T(8,128)S(1)}, f32[48,128]{1,0:T(8,128)S(1)}, u32[]{:S(2)}, u32[]{:S(2)}) collective-permute-start(f32[48,128]{1,0:T(8,128)S(1)} %get-tuple-element.37), channel_id=1, source_target_pairs={{0,8},{1,9},{2,10},{3,11},{4,12},{5,13},{6,14},{7,15},{8,0},{9,1},... | collective-permute-start | bytes 73736 | tf_op jit(solution)/shard_map/ppermute | solution.py:22

commit v5 on v4

--- a/solution.py
+++ b/solution.py
@@ -55,11 +55,11 @@
 def unpack_pair(first, second, half):
     width = first.shape[1] // 2
     left = lax.broadcasted_iota(jnp.int32, (1, 2 * width), 1) < width
-    first_rolled = pltpu.roll(first, width, 1)
-    second_rolled = pltpu.roll(second, width, 1)
-    upper = jnp.where(left, first, second_rolled)
-    lower = jnp.where(left, first_rolled, second)
-    return upper[:half], lower[:half], upper[half:]
+    spots = jnp.where(left, first[half:], second[half:])
+    first, second = first[:half], second[:half]
+    upper = jnp.where(left, first, pltpu.roll(second, width, 1))
+    lower = jnp.where(left, pltpu.roll(first, width, 1), second)
+    return upper, lower, spots
 
 
 def build_tiles(columns, target_rows, high, low):
@@ -78,10 +78,9 @@
             inverse = lax.rsqrt(squared)
             distance = squared * inverse
             inverse_squared = inverse * inverse
-            cubed = inverse * inverse_squared
             near = distance < 2.0
-            scalar = jnp.where(near, 1.0 - 0.28125 * distance, 0.75 * inverse + 0.5 * cubed)
-            dyadic = jnp.where(near, 0.09375 * inverse, cubed * (0.75 - 1.5 * inverse_squared))
+            scalar = jnp.where(near, 1.0 - 0.28125 * distance, inverse * (0.75 + 0.5 * inverse_squared))
+            dyadic = inverse * jnp.where(near, 0.09375, inverse_squared * (0.75 - 1.5 * inverse_squared))
             scaled = [dyadic * offset[c] for c in range(3)]
             for number, (a, b) in enumerate(pairs):
                 value = scaled[a] * offset[b]
@@ -301,7 +300,7 @@
     far_masks = [tiles << bit for bit in reversed(range(half_bits, bits))]
     near_masks = [1 << bit for bit in range(tiles.bit_length() - 1)]
     near_masks += [tiles << bit for bit in range(1, half_bits)]
-    return tiles, far_masks, near_masks
+    return tiles, [mask ^ tiles for mask in far_masks], [mask ^ tiles for mask in near_masks]
 
 
 def body(positions_in, noise_vectors, spectrum_bounds):

time: 40.3 us -> 39.2 us (0.973)
  starting transfers between devices: 19.3 us -> 18.6 us
    ppermute x15, starting transfers between devices: 19.3 us -> 18.6 us  [exchange(): return lax.ppermute(block, axes, [(i, i ^ mask) for i in range(count)])]
  transfers between devices with their start and end apart: 15 -> 15, of which waited for: 10 -> 9; matrix products, arithmetic and copies ran while one was open for 0% -> 0% of each run, Pallas kernels for 9% -> 9%
where the time goes in v5:
time: 39.2 us; the launch traced here: 39 us
  starting transfers between devices  18.6 us (47%)
  waiting for transfers between devices  13.1 us (33%)
  Pallas kernels  6.58 us (17%)
  between operations  0.71 us (2%)
    ppermute x15, starting transfers between devices, exchange(): return lax.ppermute(block, axes, [(i, i ^ mask) for i in range(count)])  18.6 us
    ppermute x15, waiting for transfers between devices, exchange(): return lax.ppermute(block, axes, [(i, i ^ mask) for i in range(count)])  13.1 us
    pallas_call x8, Pallas kernels, call(): pl.pallas_call(kernel, in_specs=[pl.BlockSpec(memory_space=space)] * len(...  6.58 us
  transfers between devices with their start and end apart: 15, of which 9 were waited for; matrix products, arithmetic and copies ran while one was open for 0% of the time, Pallas kernels for 9%

profile of v5, /device:TPU:0, one launch (start us, length us, event | category | flops | bytes accessed | tf_op | source)
XLA Modules:
  0.0 39.0 jit_solution(16640867959499883089)
XLA Ops:
  0.6 0.9 %shard_map.59 = (f32[56,128]{1,0:T(8,128)S(1)}, f32[96,64]{1,0:T(8,128)S(1)}, f32[3,64]{1,0:T(4,128)S(1)}, f32[8,128]{1,0:T(8,128)S(1)}, f32[8,128]{1,0:T(8,128)S(1)}) custom-call(f32[96,64]{1,0:T(8,128)} %bitcast.6, f32[3,64]{1,0:T(4,128)} %positions_in.1, f32[2]{0:T(128)} %bounds_in.1, f32[8,128]{1,0:T(8,128)} %constant.2.clone.nodes_in), custom_call_target="tpu_custom_call" | custom-call | tf_op jit(solution)/shard_map/pallas_call | solution.py:271
  1.6 3.6 %collective-permute-start.3 = (f32[1,56,128]{2,1,0:T(8,128)S(1)}, f32[1,56,128]{2,1,0:T(8,128)S(1)}, u32[]{:S(2)}, u32[]{:S(2)}) collective-permute-start(f32[1,56,128]{2,1,0:T(8,128)S(1)} %bitcast.4), channel_id=1, source_target_pairs={{0,18},{1,19},{2,16},{3,17},{4,22},{5,23},{6,20},{7,21},{8,26},{9,... | collective-permute-start | bytes 86024 | tf_op jit(solution)/shard_map/ppermute | solution.py:22
  5.1 1.7 %collective-permute-done.3 = f32[1,56,128]{2,1,0:T(8,128)S(1)} collective-permute-done((f32[1,56,128]{2,1,0:T(8,128)S(1)}, f32[1,56,128]{2,1,0:T(8,128)S(1)}, u32[]{:S(2)}, u32[]{:S(2)}) %collective-permute-start.3) | collective-permute-done | bytes 28704 | tf_op jit(solution)/shard_map/ppermute | solution.py:22
  6.8 1.8 %collective-permute-start.4 = (f32[2,56,128]{2,1,0:T(8,128)S(1)}, f32[2,56,128]{2,1,0:T(8,128)S(1)}, u32[]{:S(2)}, u32[]{:S(2)}) collective-permute-start(f32[2,56,128]{2,1,0:T(8,128)S(1)} %pad_maximum_fusion.refs_0_), channel_id=1, source_target_pairs={{0,10},{1,11},{2,8},{3,9},{4,14},{5,15},{6,12},{7,13},{8,2},{9,3},... | collective-permute-start | bytes 172040 | tf_op jit(solution)/shard_map/ppermute | solution.py:22
  8.7 2.4 %collective-permute-start.2 = (f32[3,64]{1,0:T(4,128)S(1)}, f32[3,64]{1,0:T(4,128)S(1)}, u32[]{:S(2)}, u32[]{:S(2)}) collective-permute-start(f32[3,64]{1,0:T(4,128)S(1)} %get-tuple-element.23), channel_id=1, source_target_pairs={{0,5},{1,4},{2,7},{3,6},{4,1},{5,0},{6,3},{7,2},{8,13},{9,12},{10,... | collective-permute-start | bytes 2312 | tf_op jit(solution)/shard_map/ppermute | solution.py:22
  11.1 0.2 collective-permute-start.1
  11.3 0.5 %collective-permute-start = (f32[3,64]{1,0:T(4,128)S(1)}, f32[3,64]{1,0:T(4,128)S(1)}, u32[]{:S(2)}, u32[]{:S(2)}) collective-permute-start(f32[3,64]{1,0:T(4,128)S(1)} %get-tuple-element.23), channel_id=1, source_target_pairs={{0,3},{1,2},{2,1},{3,0},{4,7},{5,6},{6,5},{7,4},{8,11},{9,10},{10,... | collective-permute-start | bytes 2312 | tf_op jit(solution)/shard_map/ppermute | solution.py:22
  11.9 0.1 collective-permute-start.5
  12.0 0.0 collective-permute-done.4.refs_1_.refs_0_
  12.0 0.4 %collective-permute-start.6 = (f32[2,56,128]{2,1,0:T(8,128)S(1)}, f32[2,56,128]{2,1,0:T(8,128)S(1)}, u32[]{:S(2)}, u32[]{:S(2)}) collective-permute-start(f32[2,56,128]{2,1,0:T(8,128)S(1)} %collective-permute-done.4.refs_1_.refs_0_), channel_id=1, source_target_pairs={{0,2},{1,3},{2,0},{3,1},{4,6},{5,7},{6,4},{7,5},{8,10},{9,11},{10,... | collective-permute-start | bytes 172040 | tf_op jit(solution)/shard_map/ppermute | solution.py:22
  12.4 0.8 %collective-permute-done.2 = f32[3,64]{1,0:T(4,128)S(1)} collective-permute-done((f32[3,64]{1,0:T(4,128)S(1)}, f32[3,64]{1,0:T(4,128)S(1)}, u32[]{:S(2)}, u32[]{:S(2)}) %collective-permute-start.2) | collective-permute-done | bytes 800 | tf_op jit(solution)/shard_map/ppermute | solution.py:22
  13.1 1.0 %collective-permute-done.1 = f32[3,64]{1,0:T(4,128)S(1)} collective-permute-done((f32[3,64]{1,0:T(4,128)S(1)}, f32[3,64]{1,0:T(4,128)S(1)}, u32[]{:S(2)}, u32[]{:S(2)}) %collective-permute-start.1) | collective-permute-done | bytes 800 | tf_op jit(solution)/shard_map/ppermute | solution.py:22
  14.1 0.2 collective-permute-done
  14.3 0.1 pad_maximum_fusion.1.near_positions
  14.4 0.0 collective-permute-done.5.refs_2_.refs_1_
  14.4 1.2 %shard_map.61.before = f32[96,256]{1,0:T(8,128)S(1)} custom-call(f32[3,256]{1,0:T(4,128)S(1)} %pad_maximum_fusion.1.near_positions, f32[2,56,128]{2,1,0:T(8,128)S(1)} %pad_maximum_fusion.refs_0_, f32[2,56,128]{2,1,0:T(8,128)S(1)} %collective-permute-done.5.refs_2_.refs_1_), custom_call_target="tpu_custom_call" | custom-call | tf_op jit(solution)/shard_map/pallas_call | solution.py:271
  15.6 0.8 %shard_map.62.before = f32[96,256]{1,0:T(8,128)S(1)} custom-call(f32[3,256]{1,0:T(4,128)S(1)} %pad_maximum_fusion.1.near_positions, f32[96,256]{1,0:T(8,128)S(1)} %shard_map.61.before, f32[2,56,128]{2,1,0:T(8,128)S(1)} %collective-permute-done.4.refs_1_.refs_0_), custom_call_target="tpu_custom_call" | custom-call | tf_op jit(solution)/shard_map/pallas_call | solution.py:271
  16.4 0.0 collective-permute-done.6.refs_3_.refs_0_
  16.4 0.8 %shard_map.63 = (f32[96,256]{1,0:T(8,128)S(1)}, f32[96,256]{1,0:T(8,128)S(1)}) custom-call(f32[8,128]{1,0:T(8,128)S(1)} %get-tuple-element.21.scalars, f32[96,64]{1,0:T(8,128)S(1)} %get-tuple-element.26.noise, f32[3,256]{1,0:T(4,128)S(1)} %pad_maximum_fusion.1.near_positions, f32[96,256]{1,0:T(8,128)S(1)} %shard_map.62.before, ...), custom_call_target="tpu_custom_call" | custom-call | tf_op jit(solution)/shard_map/pallas_call | solution.py:271
  17.2 0.6 %collective-permute-start.7 = (f32[96,256]{1,0:T(8,128)S(1)}, f32[96,256]{1,0:T(8,128)S(1)}, u32[]{:S(2)}, u32[]{:S(2)}) collective-permute-start(f32[96,256]{1,0:T(8,128)S(1)} %get-tuple-element.27.refs_4_), channel_id=1, source_target_pairs={{0,3},{1,2},{2,1},{3,0},{4,7},{5,6},{6,5},{7,4},{8,11},{9,10},{10,... | collective-permute-start | bytes 294920 | tf_op jit(solution)/shard_map/ppermute | solution.py:22
  17.8 1.2 %collective-permute-start.8 = (f32[96,256]{1,0:T(8,128)S(1)}, f32[96,256]{1,0:T(8,128)S(1)}, u32[]{:S(2)}, u32[]{:S(2)}) collective-permute-start(f32[96,256]{1,0:T(8,128)S(1)} %get-tuple-element.27.refs_4_), channel_id=1, source_target_pairs={{0,6},{1,7},{2,4},{3,5},{4,2},{5,3},{6,0},{7,1},{8,14},{9,15},{10,... | collective-permute-start | bytes 294920 | tf_op jit(solution)/shard_map/ppermute | solution.py:22
  19.0 1.4 %collective-permute-start.9 = (f32[96,256]{1,0:T(8,128)S(1)}, f32[96,256]{1,0:T(8,128)S(1)}, u32[]{:S(2)}, u32[]{:S(2)}) collective-permute-start(f32[96,256]{1,0:T(8,128)S(1)} %get-tuple-element.27.refs_4_), channel_id=1, source_target_pairs={{0,5},{1,4},{2,7},{3,6},{4,1},{5,0},{6,3},{7,2},{8,13},{9,12},{10,... | collective-permute-start | bytes 294920 | tf_op jit(solution)/shard_map/ppermute | solution.py:22
  20.4 1.4 %shard_map.60 = (bf16[6,256,512]{2,1,0:T(8,128)(2,1)S(1)}, bf16[6,256,512]{2,1,0:T(8,128)(2,1)S(1)}, f32[8,128]{1,0:T(8,128)S(1)}) custom-call(f32[8,128]{1,0:T(8,128)S(1)} %get-tuple-element.21.scalars, f32[8,128]{1,0:T(8,128)S(1)} %get-tuple-element.22.nodes, f32[3,256]{1,0:T(4,128)S(1)} %pad_maximum_fusion.1.near_positions, ...), custom_call_target="tpu_custom_call" | custom-call | tf_op jit(solution)/shard_map/pallas_call | solution.py:271
  21.9 0.0 collective-permute-done.7.refs_0_
  21.9 2.2 %collective-permute-done.8.refs_1_ = f32[96,256]{1,0:T(8,128)S(1)} collective-permute-done((f32[96,256]{1,0:T(8,128)S(1)}, f32[96,256]{1,0:T(8,128)S(1)}, u32[]{:S(2)}, u32[]{:S(2)}) %collective-permute-start.8) | collective-permute-done | bytes 98336 | tf_op jit(solution)/shard_map/ppermute | solution.py:22
  24.0 1.4 %collective-permute-done.9.refs_2_ = f32[96,256]{1,0:T(8,128)S(1)} collective-permute-done((f32[96,256]{1,0:T(8,128)S(1)}, f32[96,256]{1,0:T(8,128)S(1)}, u32[]{:S(2)}, u32[]{:S(2)}) %collective-permute-start.9) | collective-permute-done | bytes 98336 | tf_op jit(solution)/shard_map/ppermute | solution.py:22
  25.4 0.8 %shard_map.64 = (f32[96,64]{1,0:T(8,128)S(1)}, f32[2,48,128]{2,1,0:T(8,128)S(1)}, f32[3,48,128]{2,1,0:T(8,128)S(1)}, f32[3,48,128]{2,1,0:T(8,128)S(1)}) custom-call(f32[8,128]{1,0:T(8,128)S(1)} %get-tuple-element.21.scalars, f32[96,256]{1,0:T(8,128)S(1)} %collective-permute-done.7.refs_0_, f32[96,256]{1,0:T(8,128)S(1)} %collective-permute-done.8.refs_1_, ...), custom_call_target="tpu_custom_call" | custom-call | tf_op jit(solution)/shard_map/pallas_call | solution.py:271
  26.2 0.1 collective-permute-start.10
  26.2 2.9 %collective-permute-start.11 = (f32[2,48,128]{2,1,0:T(8,128)S(1)}, f32[2,48,128]{2,1,0:T(8,128)S(1)}, u32[]{:S(2)}, u32[]{:S(2)}) collective-permute-start(f32[2,48,128]{2,1,0:T(8,128)S(1)} %get-tuple-element.35), channel_id=1, source_target_pairs={{0,24},{1,25},{2,26},{3,27},{4,28},{5,29},{6,30},{7,31},{8,16},{9,... | collective-permute-start | bytes 147464 | tf_op jit(solution)/shard_map/ppermute | solution.py:22
  29.1 3.1 %collective-permute-done.11.last = f32[2,48,128]{2,1,0:T(8,128)S(1)} collective-permute-done((f32[2,48,128]{2,1,0:T(8,128)S(1)}, f32[2,48,128]{2,1,0:T(8,128)S(1)}, u32[]{:S(2)}, u32[]{:S(2)}) %collective-permute-start.11) | collective-permute-done | bytes 49184 | tf_op jit(solution)/shard_map/ppermute | solution.py:22
  32.3 0.0 collective-permute-start.12
  32.3 0.0 collective-permute-done.10.arrived
  32.3 2.7 %collective-permute-start.13 = (f32[48,128]{1,0:T(8,128)S(1)}, f32[48,128]{1,0:T(8,128)S(1)}, u32[]{:S(2)}, u32[]{:S(2)}) collective-permute-start(f32[48,128]{1,0:T(8,128)S(1)} %get-tuple-element.36), channel_id=1, source_target_pairs={{0,18},{1,19},{2,16},{3,17},{4,22},{5,23},{6,20},{7,21},{8,26},{9,... | collective-permute-start | bytes 73736 | tf_op jit(solution)/shard_map/ppermute | solution.py:22
  35.0 0.5 %collective-permute-start.14 = (f32[48,128]{1,0:T(8,128)S(1)}, f32[48,128]{1,0:T(8,128)S(1)}, u32[]{:S(2)}, u32[]{:S(2)}) collective-permute-start(f32[48,128]{1,0:T(8,128)S(1)} %get-tuple-element.37), channel_id=1, source_target_pairs={{0,10},{1,11},{2,8},{3,9},{4,14},{5,15},{6,12},{7,13},{8,2},{9,3},... | collective-permute-start | bytes 73736 | tf_op jit(solution)/shard_map/ppermute | solution.py:22
  35.5 0.0 collective-permute-done.12.last_across
  35.5 1.0 %collective-permute-done.13.refs_0_ = f32[48,128]{1,0:T(8,128)S(1)} collective-permute-done((f32[48,128]{1,0:T(8,128)S(1)}, f32[48,128]{1,0:T(8,128)S(1)}, u32[]{:S(2)}, u32[]{:S(2)}) %collective-permute-start.13) | collective-permute-done | bytes 24608 | tf_op jit(solution)/shard_map/ppermute | solution.py:22
  36.5 1.8 %collective-permute-done.14.refs_1_ = f32[48,128]{1,0:T(8,128)S(1)} collective-permute-done((f32[48,128]{1,0:T(8,128)S(1)}, f32[48,128]{1,0:T(8,128)S(1)}, u32[]{:S(2)}, u32[]{:S(2)}) %collective-permute-start.14) | collective-permute-done | bytes 24608 | tf_op jit(solution)/shard_map/ppermute | solution.py:22
  38.3 0.7 %shard_map.66 = (f32[96,64]{1,0:T(8,128)}, f32[2,96,64]{2,1,0:T(8,128)}) custom-call(f32[8,128]{1,0:T(8,128)S(1)} %get-tuple-element.21.scalars, f32[8,128]{1,0:T(8,128)S(1)} %get-tuple-element.25.weights, f32[96,64]{1,0:T(8,128)S(1)} %get-tuple-element.26.noise, f32[96,64]{1,0:T(8,128)S(1)} %get-tuple-element.31.first_image, ...), custom_call_target="tpu_custom_call" | custom-call | tf_op jit(solution)/shard_map/pallas_call | solution.py:271
  (3 shorter events, 0.0 us)
Async XLA Ops:
  1.6 5.3 %collective-permute-start.3 = (f32[1,56,128]{2,1,0:T(8,128)S(1)}, f32[1,56,128]{2,1,0:T(8,128)S(1)}, u32[]{:S(2)}, u32[]{:S(2)}) collective-permute-start(f32[1,56,128]{2,1,0:T(8,128)S(1)} %bitcast.4), channel_id=1, source_target_pairs={{0,18},{1,19},{2,16},{3,17},{4,22},{5,23},{6,20},{7,21},{8,26},{9,... | collective-permute-start | bytes 86024 | tf_op jit(solution)/shard_map/ppermute | solution.py:22
  6.8 5.2 %collective-permute-start.4 = (f32[2,56,128]{2,1,0:T(8,128)S(1)}, f32[2,56,128]{2,1,0:T(8,128)S(1)}, u32[]{:S(2)}, u32[]{:S(2)}) collective-permute-start(f32[2,56,128]{2,1,0:T(8,128)S(1)} %pad_maximum_fusion.refs_0_), channel_id=1, source_target_pairs={{0,10},{1,11},{2,8},{3,9},{4,14},{5,15},{6,12},{7,13},{8,2},{9,3},... | collective-permute-start | bytes 172040 | tf_op jit(solution)/shard_map/ppermute | solution.py:22
  8.7 4.5 %collective-permute-start.2 = (f32[3,64]{1,0:T(4,128)S(1)}, f32[3,64]{1,0:T(4,128)S(1)}, u32[]{:S(2)}, u32[]{:S(2)}) collective-permute-start(f32[3,64]{1,0:T(4,128)S(1)} %get-tuple-element.23), channel_id=1, source_target_pairs={{0,5},{1,4},{2,7},{3,6},{4,1},{5,0},{6,3},{7,2},{8,13},{9,12},{10,... | collective-permute-start | bytes 2312 | tf_op jit(solution)/shard_map/ppermute | solution.py:22
  11.1 3.0 %collective-permute-start.1 = (f32[3,64]{1,0:T(4,128)S(1)}, f32[3,64]{1,0:T(4,128)S(1)}, u32[]{:S(2)}, u32[]{:S(2)}) collective-permute-start(f32[3,64]{1,0:T(4,128)S(1)} %get-tuple-element.23), channel_id=1, source_target_pairs={{0,6},{1,7},{2,4},{3,5},{4,2},{5,3},{6,0},{7,1},{8,14},{9,15},{10,... | collective-permute-start | bytes 2312 | tf_op jit(solution)/shard_map/ppermute | solution.py:22
  11.3 3.0 %collective-permute-start = (f32[3,64]{1,0:T(4,128)S(1)}, f32[3,64]{1,0:T(4,128)S(1)}, u32[]{:S(2)}, u32[]{:S(2)}) collective-permute-start(f32[3,64]{1,0:T(4,128)S(1)} %get-tuple-element.23), channel_id=1, source_target_pairs={{0,3},{1,2},{2,1},{3,0},{4,7},{5,6},{6,5},{7,4},{8,11},{9,10},{10,... | collective-permute-start | bytes 2312 | tf_op jit(solution)/shard_map/ppermute | solution.py:22
  11.9 2.6 %collective-permute-start.5 = (f32[2,56,128]{2,1,0:T(8,128)S(1)}, f32[2,56,128]{2,1,0:T(8,128)S(1)}, u32[]{:S(2)}, u32[]{:S(2)}) collective-permute-start(f32[2,56,128]{2,1,0:T(8,128)S(1)} %pad_maximum_fusion.refs_0_), channel_id=1, source_target_pairs={{0,2},{1,3},{2,0},{3,1},{4,6},{5,7},{6,4},{7,5},{8,10},{9,11},{10,... | collective-permute-start | bytes 172040 | tf_op jit(solution)/shard_map/ppermute | solution.py:22
  12.0 4.4 %collective-permute-start.6 = (f32[2,56,128]{2,1,0:T(8,128)S(1)}, f32[2,56,128]{2,1,0:T(8,128)S(1)}, u32[]{:S(2)}, u32[]{:S(2)}) collective-permute-start(f32[2,56,128]{2,1,0:T(8,128)S(1)} %collective-permute-done.4.refs_1_.refs_0_), channel_id=1, source_target_pairs={{0,2},{1,3},{2,0},{3,1},{4,6},{5,7},{6,4},{7,5},{8,10},{9,11},{10,... | collective-permute-start | bytes 172040 | tf_op jit(solution)/shard_map/ppermute | solution.py:22
  17.2 4.7 %collective-permute-start.7 = (f32[96,256]{1,0:T(8,128)S(1)}, f32[96,256]{1,0:T(8,128)S(1)}, u32[]{:S(2)}, u32[]{:S(2)}) collective-permute-start(f32[96,256]{1,0:T(8,128)S(1)} %get-tuple-element.27.refs_4_), channel_id=1, source_target_pairs={{0,3},{1,2},{2,1},{3,0},{4,7},{5,6},{6,5},{7,4},{8,11},{9,10},{10,... | collective-permute-start | bytes 294920 | tf_op jit(solution)/shard_map/ppermute | solution.py:22
  17.8 6.3 %collective-permute-start.8 = (f32[96,256]{1,0:T(8,128)S(1)}, f32[96,256]{1,0:T(8,128)S(1)}, u32[]{:S(2)}, u32[]{:S(2)}) collective-permute-start(f32[96,256]{1,0:T(8,128)S(1)} %get-tuple-element.27.refs_4_), channel_id=1, source_target_pairs={{0,6},{1,7},{2,4},{3,5},{4,2},{5,3},{6,0},{7,1},{8,14},{9,15},{10,... | collective-permute-start | bytes 294920 | tf_op jit(solution)/shard_map/ppermute | solution.py:22
  19.0 6.4 %collective-permute-start.9 = (f32[96,256]{1,0:T(8,128)S(1)}, f32[96,256]{1,0:T(8,128)S(1)}, u32[]{:S(2)}, u32[]{:S(2)}) collective-permute-start(f32[96,256]{1,0:T(8,128)S(1)} %get-tuple-element.27.refs_4_), channel_id=1, source_target_pairs={{0,5},{1,4},{2,7},{3,6},{4,1},{5,0},{6,3},{7,2},{8,13},{9,12},{10,... | collective-permute-start | bytes 294920 | tf_op jit(solution)/shard_map/ppermute | solution.py:22
  26.2 6.1 %collective-permute-start.10 = (f32[3,48,128]{2,1,0:T(8,128)S(1)}, f32[3,48,128]{2,1,0:T(8,128)S(1)}, u32[]{:S(2)}, u32[]{:S(2)}) collective-permute-start(f32[3,48,128]{2,1,0:T(8,128)S(1)} %get-tuple-element.33), channel_id=1, source_target_pairs={{0,2},{1,3},{2,0},{3,1},{4,6},{5,7},{6,4},{7,5},{8,10},{9,11},{10,... | collective-permute-start | bytes 221192 | tf_op jit(solution)/shard_map/ppermute | solution.py:22
  26.2 6.0 %collective-permute-start.11 = (f32[2,48,128]{2,1,0:T(8,128)S(1)}, f32[2,48,128]{2,1,0:T(8,128)S(1)}, u32[]{:S(2)}, u32[]{:S(2)}) collective-permute-start(f32[2,48,128]{2,1,0:T(8,128)S(1)} %get-tuple-element.35), channel_id=1, source_target_pairs={{0,24},{1,25},{2,26},{3,27},{4,28},{5,29},{6,30},{7,31},{8,16},{9,... | collective-permute-start | bytes 147464 | tf_op jit(solution)/shard_map/ppermute | solution.py:22
  32.3 3.2 %collective-permute-start.12 = (f32[1,48,128]{2,1,0:T(8,128)S(1)}, f32[1,48,128]{2,1,0:T(8,128)S(1)}, u32[]{:S(2)}, u32[]{:S(2)}) collective-permute-start(f32[1,48,128]{2,1,0:T(8,128)S(1)} %slice.4), channel_id=1, source_target_pairs={{0,2},{1,3},{2,0},{3,1},{4,6},{5,7},{6,4},{7,5},{8,10},{9,11},{10,... | collective-permute-start | bytes 73736 | tf_op jit(solution)/shard_map/ppermute | solution.py:22
  32.3 4.2 %collective-permute-start.13 = (f32[48,128]{1,0:T(8,128)S(1)}, f32[48,128]{1,0:T(8,128)S(1)}, u32[]{:S(2)}, u32[]{:S(2)}) collective-permute-start(f32[48,128]{1,0:T(8,128)S(1)} %get-tuple-element.36), channel_id=1, source_target_pairs={{0,18},{1,19},{2,16},{3,17},{4,22},{5,23},{6,20},{7,21},{8,26},{9,... | collective-permute-start | bytes 73736 | tf_op jit(solution)/shard_map/ppermute | solution.py:22
  35.0 3.3 %collective-permute-start.14 = (f32[48,128]{1,0:T(8,128)S(1)}, f32[48,128]{1,0:T(8,128)S(1)}, u32[]{:S(2)}, u32[]{:S(2)}) collective-permute-start(f32[48,128]{1,0:T(8,128)S(1)} %get-tuple-element.37), channel_id=1, source_target_pairs={{0,10},{1,11},{2,8},{3,9},{4,14},{5,15},{6,12},{7,13},{8,2},{9,3},... | collective-permute-start | bytes 73736 | tf_op jit(solution)/shard_map/ppermute | solution.py:22

commit v6 on v5

--- a/solution.py
+++ b/solution.py
@@ -1,3 +1,4 @@
+import functools
 import math
 
 import jax
@@ -34,14 +35,16 @@
     copies = [pltpu.make_async_copy(*move, sems.at[n]) for n, move in enumerate(moves)]
     for copy in copies:
         copy.start()
-    for copy in copies:
-        copy.wait()
+    copies[0].wait()
+    copies[1].wait()
     half = noise.shape[0] // 2
     message[0:half, :] = jnp.concatenate([noise[0:half, :], noise[half:, :]], axis=1)
     spot = positions[...]
     pad = jnp.zeros((8 - spot.shape[0], spot.shape[1]), f32)
     spot = jnp.concatenate([spot, pad], axis=0)
     message[half:, :] = jnp.concatenate([spot, spot], axis=1)
+    copies[2].wait()
+    copies[3].wait()
     highest, lowest = bounds[1], bounds[0]
     scalars[0:4, :] = jnp.full((4, 128), 0.5 * (highest + lowest), f32)
     scalars[4:8, :] = jnp.full((4, 128), 0.5 * (highest - lowest), f32)
@@ -65,7 +68,7 @@
 def build_tiles(columns, target_rows, high, low):
     source_count = columns.shape[1]
     tile_count = target_rows.shape[1] // 128
-    chunk = 32
+    chunk = 64
 
     def one_chunk(step, carry):
         start = pl.multiple_of(step * chunk, chunk)
@@ -235,10 +238,10 @@
         ref[...] = kept[number] + arrived[number]
 
 
-def final_kernel(scalars, weights, noise, first_image, own, last, last_across, *refs):
+def final_kernel(mine, scalars, weights, noise, first_image, own, last, last_across, *refs):
     received, (displacement, images) = refs[:-2], refs[-2:]
     width = noise.shape[1]
-    total = own[...] + last[0] + last_across[0]
+    total = own[...] + last[mine] + last_across[1 - mine]
     for ref in received:
         total = total + ref[...]
     second = jnp.concatenate([total[:, :width], total[:, width:]], axis=0)
@@ -376,12 +379,13 @@
         (pltpu.VMEM((rows, near_count), f32),),
     )
     arrived = exchange(sent, core_mask)
-    last_part = exchange(last_part, far_steps[-1])
+    straight = int(far_steps[-1] & core_mask == 0)
+    last_part = exchange(last_part, far_steps[-1] ^ straight * core_mask)
     own, *outgoing = call(fourth_kernel, (kept, arrived), [block] * len(far_steps))
     received = [exchange(value, mask) for value, mask in zip(outgoing, far_steps)]
-    last_across = exchange(last_part[1:], core_mask)
+    last_across = exchange(last_part, core_mask)
     displacement, images = call(
-        final_kernel,
+        functools.partial(final_kernel, straight),
         (scalars, weights, noise, first_image, own, last_part, last_across, *received),
         [((rows, width), f32), ((2, rows, width), f32)],
         final=True,

time: 39.2 us -> 38.5 us (0.982)
  waiting for transfers between devices: 13.1 us -> 12.2 us
    ppermute x15, waiting for transfers between devices: 13.1 us -> 12.2 us  [exchange(): return lax.ppermute(block, axes, [(i, i ^ mask) for i in range(count)])]
where the time goes in v6:
time: 38.5 us; the launch traced here: 38.4 us
  starting transfers between devices  18.9 us (49%)
  waiting for transfers between devices  12.2 us (32%)
  Pallas kernels  6.45 us (17%)
  between operations  0.71 us (2%)
    ppermute x15, starting transfers between devices, exchange(): return lax.ppermute(block, axes, [(i, i ^ mask) for i in range(count)])  18.9 us
    ppermute x15, waiting for transfers between devices, exchange(): return lax.ppermute(block, axes, [(i, i ^ mask) for i in range(count)])  12.2 us
    pallas_call x8, Pallas kernels, call(): pl.pallas_call(kernel, in_specs=[pl.BlockSpec(memory_space=space)] * len(...  6.45 us
  transfers between devices with their start and end apart: 15, of which 9 were waited for; matrix products, arithmetic and copies ran while one was open for 0% of the time, Pallas kernels for 9%

profile of v6, /device:TPU:0, one launch (start us, length us, event | category | flops | bytes accessed | tf_op | source)
XLA Modules:
  0.0 38.4 jit_solution(11129004726881514563)
XLA Ops:
  0.6 0.9 %shard_map.59 = (f32[56,128]{1,0:T(8,128)S(1)}, f32[96,64]{1,0:T(8,128)S(1)}, f32[3,64]{1,0:T(4,128)S(1)}, f32[8,128]{1,0:T(8,128)S(1)}, f32[8,128]{1,0:T(8,128)S(1)}) custom-call(f32[96,64]{1,0:T(8,128)} %bitcast.6, f32[3,64]{1,0:T(4,128)} %positions_in.1, f32[2]{0:T(128)} %bounds_in.1, f32[8,128]{1,0:T(8,128)} %constant.2.clone.nodes_in), custom_call_target="tpu_custom_call" | custom-call | tf_op jit(solution)/shard_map/pallas_call | solution.py:274
  1.6 3.6 %collective-permute-start.3 = (f32[1,56,128]{2,1,0:T(8,128)S(1)}, f32[1,56,128]{2,1,0:T(8,128)S(1)}, u32[]{:S(2)}, u32[]{:S(2)}) collective-permute-start(f32[1,56,128]{2,1,0:T(8,128)S(1)} %bitcast.4), channel_id=1, source_target_pairs={{0,18},{1,19},{2,16},{3,17},{4,22},{5,23},{6,20},{7,21},{8,26},{9,... | collective-permute-start | bytes 86024 | tf_op jit(solution)/shard_map/ppermute | solution.py:23
  5.1 1.7 %collective-permute-done.3 = f32[1,56,128]{2,1,0:T(8,128)S(1)} collective-permute-done((f32[1,56,128]{2,1,0:T(8,128)S(1)}, f32[1,56,128]{2,1,0:T(8,128)S(1)}, u32[]{:S(2)}, u32[]{:S(2)}) %collective-permute-start.3) | collective-permute-done | bytes 28704 | tf_op jit(solution)/shard_map/ppermute | solution.py:23
  6.8 1.8 %collective-permute-start.4 = (f32[2,56,128]{2,1,0:T(8,128)S(1)}, f32[2,56,128]{2,1,0:T(8,128)S(1)}, u32[]{:S(2)}, u32[]{:S(2)}) collective-permute-start(f32[2,56,128]{2,1,0:T(8,128)S(1)} %pad_maximum_fusion.refs_0_), channel_id=1, source_target_pairs={{0,10},{1,11},{2,8},{3,9},{4,14},{5,15},{6,12},{7,13},{8,2},{9,3},... | collective-permute-start | bytes 172040 | tf_op jit(solution)/shard_map/ppermute | solution.py:23
  8.7 2.4 %collective-permute-start.2 = (f32[3,64]{1,0:T(4,128)S(1)}, f32[3,64]{1,0:T(4,128)S(1)}, u32[]{:S(2)}, u32[]{:S(2)}) collective-permute-start(f32[3,64]{1,0:T(4,128)S(1)} %get-tuple-element.23), channel_id=1, source_target_pairs={{0,5},{1,4},{2,7},{3,6},{4,1},{5,0},{6,3},{7,2},{8,13},{9,12},{10,... | collective-permute-start | bytes 2312 | tf_op jit(solution)/shard_map/ppermute | solution.py:23
  11.1 0.2 collective-permute-start.1
  11.3 0.5 %collective-permute-start = (f32[3,64]{1,0:T(4,128)S(1)}, f32[3,64]{1,0:T(4,128)S(1)}, u32[]{:S(2)}, u32[]{:S(2)}) collective-permute-start(f32[3,64]{1,0:T(4,128)S(1)} %get-tuple-element.23), channel_id=1, source_target_pairs={{0,3},{1,2},{2,1},{3,0},{4,7},{5,6},{6,5},{7,4},{8,11},{9,10},{10,... | collective-permute-start | bytes 2312 | tf_op jit(solution)/shard_map/ppermute | solution.py:23
  11.9 0.1 collective-permute-start.5
  12.0 0.0 collective-permute-done.4.refs_1_.refs_0_
  12.0 0.4 %collective-permute-start.6 = (f32[2,56,128]{2,1,0:T(8,128)S(1)}, f32[2,56,128]{2,1,0:T(8,128)S(1)}, u32[]{:S(2)}, u32[]{:S(2)}) collective-permute-start(f32[2,56,128]{2,1,0:T(8,128)S(1)} %collective-permute-done.4.refs_1_.refs_0_), channel_id=1, source_target_pairs={{0,2},{1,3},{2,0},{3,1},{4,6},{5,7},{6,4},{7,5},{8,10},{9,11},{10,... | collective-permute-start | bytes 172040 | tf_op jit(solution)/shard_map/ppermute | solution.py:23
  12.4 0.8 %collective-permute-done.2 = f32[3,64]{1,0:T(4,128)S(1)} collective-permute-done((f32[3,64]{1,0:T(4,128)S(1)}, f32[3,64]{1,0:T(4,128)S(1)}, u32[]{:S(2)}, u32[]{:S(2)}) %collective-permute-start.2) | collective-permute-done | bytes 800 | tf_op jit(solution)/shard_map/ppermute | solution.py:23
  13.2 1.0 %collective-permute-done.1 = f32[3,64]{1,0:T(4,128)S(1)} collective-permute-done((f32[3,64]{1,0:T(4,128)S(1)}, f32[3,64]{1,0:T(4,128)S(1)}, u32[]{:S(2)}, u32[]{:S(2)}) %collective-permute-start.1) | collective-permute-done | bytes 800 | tf_op jit(solution)/shard_map/ppermute | solution.py:23
  14.1 0.2 collective-permute-done
  14.4 0.1 pad_maximum_fusion.1.near_positions
  14.4 0.0 collective-permute-done.5.refs_2_.refs_1_
  14.4 1.2 %shard_map.61.before = f32[96,256]{1,0:T(8,128)S(1)} custom-call(f32[3,256]{1,0:T(4,128)S(1)} %pad_maximum_fusion.1.near_positions, f32[2,56,128]{2,1,0:T(8,128)S(1)} %pad_maximum_fusion.refs_0_, f32[2,56,128]{2,1,0:T(8,128)S(1)} %collective-permute-done.5.refs_2_.refs_1_), custom_call_target="tpu_custom_call" | custom-call | tf_op jit(solution)/shard_map/pallas_call | solution.py:274
  15.6 0.7 %shard_map.62.before = f32[96,256]{1,0:T(8,128)S(1)} custom-call(f32[3,256]{1,0:T(4,128)S(1)} %pad_maximum_fusion.1.near_positions, f32[96,256]{1,0:T(8,128)S(1)} %shard_map.61.before, f32[2,56,128]{2,1,0:T(8,128)S(1)} %collective-permute-done.4.refs_1_.refs_0_), custom_call_target="tpu_custom_call" | custom-call | tf_op jit(solution)/shard_map/pallas_call | solution.py:274
  16.3 0.0 collective-permute-done.6.refs_3_.refs_0_
  16.3 0.7 %shard_map.63 = (f32[96,256]{1,0:T(8,128)S(1)}, f32[96,256]{1,0:T(8,128)S(1)}) custom-call(f32[8,128]{1,0:T(8,128)S(1)} %get-tuple-element.21.scalars, f32[96,64]{1,0:T(8,128)S(1)} %get-tuple-element.26.noise, f32[3,256]{1,0:T(4,128)S(1)} %pad_maximum_fusion.1.near_positions, f32[96,256]{1,0:T(8,128)S(1)} %shard_map.62.before, ...), custom_call_target="tpu_custom_call" | custom-call | tf_op jit(solution)/shard_map/pallas_call | solution.py:274
  17.1 0.6 %collective-permute-start.7 = (f32[96,256]{1,0:T(8,128)S(1)}, f32[96,256]{1,0:T(8,128)S(1)}, u32[]{:S(2)}, u32[]{:S(2)}) collective-permute-start(f32[96,256]{1,0:T(8,128)S(1)} %get-tuple-element.27.refs_4_), channel_id=1, source_target_pairs={{0,3},{1,2},{2,1},{3,0},{4,7},{5,6},{6,5},{7,4},{8,11},{9,10},{10,... | collective-permute-start | bytes 294920 | tf_op jit(solution)/shard_map/ppermute | solution.py:23
  17.7 1.2 %collective-permute-start.8 = (f32[96,256]{1,0:T(8,128)S(1)}, f32[96,256]{1,0:T(8,128)S(1)}, u32[]{:S(2)}, u32[]{:S(2)}) collective-permute-start(f32[96,256]{1,0:T(8,128)S(1)} %get-tuple-element.27.refs_4_), channel_id=1, source_target_pairs={{0,6},{1,7},{2,4},{3,5},{4,2},{5,3},{6,0},{7,1},{8,14},{9,15},{10,... | collective-permute-start | bytes 294920 | tf_op jit(solution)/shard_map/ppermute | solution.py:23
  18.9 1.4 %collective-permute-start.9 = (f32[96,256]{1,0:T(8,128)S(1)}, f32[96,256]{1,0:T(8,128)S(1)}, u32[]{:S(2)}, u32[]{:S(2)}) collective-permute-start(f32[96,256]{1,0:T(8,128)S(1)} %get-tuple-element.27.refs_4_), channel_id=1, source_target_pairs={{0,5},{1,4},{2,7},{3,6},{4,1},{5,0},{6,3},{7,2},{8,13},{9,12},{10,... | collective-permute-start | bytes 294920 | tf_op jit(solution)/shard_map/ppermute | solution.py:23
  20.4 1.4 %shard_map.60 = (bf16[6,256,512]{2,1,0:T(8,128)(2,1)S(1)}, bf16[6,256,512]{2,1,0:T(8,128)(2,1)S(1)}, f32[8,128]{1,0:T(8,128)S(1)}) custom-call(f32[8,128]{1,0:T(8,128)S(1)} %get-tuple-element.21.scalars, f32[8,128]{1,0:T(8,128)S(1)} %get-tuple-element.22.nodes, f32[3,256]{1,0:T(4,128)S(1)} %pad_maximum_fusion.1.near_positions, ...), custom_call_target="tpu_custom_call" | custom-call | tf_op jit(solution)/shard_map/pallas_call | solution.py:274
  21.7 0.0 collective-permute-done.7.refs_0_
  21.8 2.2 %collective-permute-done.8.refs_1_ = f32[96,256]{1,0:T(8,128)S(1)} collective-permute-done((f32[96,256]{1,0:T(8,128)S(1)}, f32[96,256]{1,0:T(8,128)S(1)}, u32[]{:S(2)}, u32[]{:S(2)}) %collective-permute-start.8) | collective-permute-done | bytes 98336 | tf_op jit(solution)/shard_map/ppermute | solution.py:23
  24.0 1.3 %collective-permute-done.9.refs_2_ = f32[96,256]{1,0:T(8,128)S(1)} collective-permute-done((f32[96,256]{1,0:T(8,128)S(1)}, f32[96,256]{1,0:T(8,128)S(1)}, u32[]{:S(2)}, u32[]{:S(2)}) %collective-permute-start.9) | collective-permute-done | bytes 98336 | tf_op jit(solution)/shard_map/ppermute | solution.py:23
  25.3 0.8 %shard_map.64 = (f32[96,64]{1,0:T(8,128)S(1)}, f32[2,48,128]{2,1,0:T(8,128)S(1)}, f32[3,48,128]{2,1,0:T(8,128)S(1)}, f32[3,48,128]{2,1,0:T(8,128)S(1)}) custom-call(f32[8,128]{1,0:T(8,128)S(1)} %get-tuple-element.21.scalars, f32[96,256]{1,0:T(8,128)S(1)} %collective-permute-done.7.refs_0_, f32[96,256]{1,0:T(8,128)S(1)} %collective-permute-done.8.refs_1_, ...), custom_call_target="tpu_custom_call" | custom-call | tf_op jit(solution)/shard_map/pallas_call | solution.py:274
  26.1 0.1 collective-permute-start.10
  26.2 2.9 %collective-permute-start.11 = (f32[2,48,128]{2,1,0:T(8,128)S(1)}, f32[2,48,128]{2,1,0:T(8,128)S(1)}, u32[]{:S(2)}, u32[]{:S(2)}) collective-permute-start(f32[2,48,128]{2,1,0:T(8,128)S(1)} %get-tuple-element.35), channel_id=1, source_target_pairs={{0,26},{1,27},{2,24},{3,25},{4,30},{5,31},{6,28},{7,29},{8,18},{9,... | collective-permute-start | bytes 147464 | tf_op jit(solution)/shard_map/ppermute | solution.py:23
  29.1 2.5 %collective-permute-done.11.last = f32[2,48,128]{2,1,0:T(8,128)S(1)} collective-permute-done((f32[2,48,128]{2,1,0:T(8,128)S(1)}, f32[2,48,128]{2,1,0:T(8,128)S(1)}, u32[]{:S(2)}, u32[]{:S(2)}) %collective-permute-start.11) | collective-permute-done | bytes 49184 | tf_op jit(solution)/shard_map/ppermute | solution.py:23
  31.6 0.3 collective-permute-start.12
  32.0 0.0 collective-permute-done.10.arrived
  32.0 2.4 %collective-permute-start.13 = (f32[48,128]{1,0:T(8,128)S(1)}, f32[48,128]{1,0:T(8,128)S(1)}, u32[]{:S(2)}, u32[]{:S(2)}) collective-permute-start(f32[48,128]{1,0:T(8,128)S(1)} %get-tuple-element.36), channel_id=1, source_target_pairs={{0,18},{1,19},{2,16},{3,17},{4,22},{5,23},{6,20},{7,21},{8,26},{9,... | collective-permute-start | bytes 73736 | tf_op jit(solution)/shard_map/ppermute | solution.py:23
  34.4 0.8 %collective-permute-start.14 = (f32[48,128]{1,0:T(8,128)S(1)}, f32[48,128]{1,0:T(8,128)S(1)}, u32[]{:S(2)}, u32[]{:S(2)}) collective-permute-start(f32[48,128]{1,0:T(8,128)S(1)} %get-tuple-element.37), channel_id=1, source_target_pairs={{0,10},{1,11},{2,8},{3,9},{4,14},{5,15},{6,12},{7,13},{8,2},{9,3},... | collective-permute-start | bytes 73736 | tf_op jit(solution)/shard_map/ppermute | solution.py:23
  35.2 0.0 collective-permute-done.12.last_across
  35.2 1.0 %collective-permute-done.13.refs_0_ = f32[48,128]{1,0:T(8,128)S(1)} collective-permute-done((f32[48,128]{1,0:T(8,128)S(1)}, f32[48,128]{1,0:T(8,128)S(1)}, u32[]{:S(2)}, u32[]{:S(2)}) %collective-permute-start.13) | collective-permute-done | bytes 24608 | tf_op jit(solution)/shard_map/ppermute | solution.py:23
  36.2 1.4 %collective-permute-done.14.refs_1_ = f32[48,128]{1,0:T(8,128)S(1)} collective-permute-done((f32[48,128]{1,0:T(8,128)S(1)}, f32[48,128]{1,0:T(8,128)S(1)}, u32[]{:S(2)}, u32[]{:S(2)}) %collective-permute-start.14) | collective-permute-done | bytes 24608 | tf_op jit(solution)/shard_map/ppermute | solution.py:23
  37.6 0.7 %shard_map.66 = (f32[96,64]{1,0:T(8,128)}, f32[2,96,64]{2,1,0:T(8,128)}) custom-call(f32[8,128]{1,0:T(8,128)S(1)} %get-tuple-element.21.scalars, f32[8,128]{1,0:T(8,128)S(1)} %get-tuple-element.25.weights, f32[96,64]{1,0:T(8,128)S(1)} %get-tuple-element.26.noise, f32[96,64]{1,0:T(8,128)S(1)} %get-tuple-element.31.first_image, ...), custom_call_target="tpu_custom_call" | custom-call | tf_op jit(solution)/shard_map/pallas_call | solution.py:274
  (2 shorter events, 0.0 us)
Async XLA Ops:
  1.6 5.3 %collective-permute-start.3 = (f32[1,56,128]{2,1,0:T(8,128)S(1)}, f32[1,56,128]{2,1,0:T(8,128)S(1)}, u32[]{:S(2)}, u32[]{:S(2)}) collective-permute-start(f32[1,56,128]{2,1,0:T(8,128)S(1)} %bitcast.4), channel_id=1, source_target_pairs={{0,18},{1,19},{2,16},{3,17},{4,22},{5,23},{6,20},{7,21},{8,26},{9,... | collective-permute-start | bytes 86024 | tf_op jit(solution)/shard_map/ppermute | solution.py:23
  6.8 5.2 %collective-permute-start.4 = (f32[2,56,128]{2,1,0:T(8,128)S(1)}, f32[2,56,128]{2,1,0:T(8,128)S(1)}, u32[]{:S(2)}, u32[]{:S(2)}) collective-permute-start(f32[2,56,128]{2,1,0:T(8,128)S(1)} %pad_maximum_fusion.refs_0_), channel_id=1, source_target_pairs={{0,10},{1,11},{2,8},{3,9},{4,14},{5,15},{6,12},{7,13},{8,2},{9,3},... | collective-permute-start | bytes 172040 | tf_op jit(solution)/shard_map/ppermute | solution.py:23
  8.7 4.5 %collective-permute-start.2 = (f32[3,64]{1,0:T(4,128)S(1)}, f32[3,64]{1,0:T(4,128)S(1)}, u32[]{:S(2)}, u32[]{:S(2)}) collective-permute-start(f32[3,64]{1,0:T(4,128)S(1)} %get-tuple-element.23), channel_id=1, source_target_pairs={{0,5},{1,4},{2,7},{3,6},{4,1},{5,0},{6,3},{7,2},{8,13},{9,12},{10,... | collective-permute-start | bytes 2312 | tf_op jit(solution)/shard_map/ppermute | solution.py:23
  11.1 3.0 %collective-permute-start.1 = (f32[3,64]{1,0:T(4,128)S(1)}, f32[3,64]{1,0:T(4,128)S(1)}, u32[]{:S(2)}, u32[]{:S(2)}) collective-permute-start(f32[3,64]{1,0:T(4,128)S(1)} %get-tuple-element.23), channel_id=1, source_target_pairs={{0,6},{1,7},{2,4},{3,5},{4,2},{5,3},{6,0},{7,1},{8,14},{9,15},{10,... | collective-permute-start | bytes 2312 | tf_op jit(solution)/shard_map/ppermute | solution.py:23
  11.3 3.0 %collective-permute-start = (f32[3,64]{1,0:T(4,128)S(1)}, f32[3,64]{1,0:T(4,128)S(1)}, u32[]{:S(2)}, u32[]{:S(2)}) collective-permute-start(f32[3,64]{1,0:T(4,128)S(1)} %get-tuple-element.23), channel_id=1, source_target_pairs={{0,3},{1,2},{2,1},{3,0},{4,7},{5,6},{6,5},{7,4},{8,11},{9,10},{10,... | collective-permute-start | bytes 2312 | tf_op jit(solution)/shard_map/ppermute | solution.py:23
  11.9 2.6 %collective-permute-start.5 = (f32[2,56,128]{2,1,0:T(8,128)S(1)}, f32[2,56,128]{2,1,0:T(8,128)S(1)}, u32[]{:S(2)}, u32[]{:S(2)}) collective-permute-start(f32[2,56,128]{2,1,0:T(8,128)S(1)} %pad_maximum_fusion.refs_0_), channel_id=1, source_target_pairs={{0,2},{1,3},{2,0},{3,1},{4,6},{5,7},{6,4},{7,5},{8,10},{9,11},{10,... | collective-permute-start | bytes 172040 | tf_op jit(solution)/shard_map/ppermute | solution.py:23
  12.0 4.3 %collective-permute-start.6 = (f32[2,56,128]{2,1,0:T(8,128)S(1)}, f32[2,56,128]{2,1,0:T(8,128)S(1)}, u32[]{:S(2)}, u32[]{:S(2)}) collective-permute-start(f32[2,56,128]{2,1,0:T(8,128)S(1)} %collective-permute-done.4.refs_1_.refs_0_), channel_id=1, source_target_pairs={{0,2},{1,3},{2,0},{3,1},{4,6},{5,7},{6,4},{7,5},{8,10},{9,11},{10,... | collective-permute-start | bytes 172040 | tf_op jit(solution)/shard_map/ppermute | solution.py:23
  17.1 4.7 %collective-permute-start.7 = (f32[96,256]{1,0:T(8,128)S(1)}, f32[96,256]{1,0:T(8,128)S(1)}, u32[]{:S(2)}, u32[]{:S(2)}) collective-permute-start(f32[96,256]{1,0:T(8,128)S(1)} %get-tuple-element.27.refs_4_), channel_id=1, source_target_pairs={{0,3},{1,2},{2,1},{3,0},{4,7},{5,6},{6,5},{7,4},{8,11},{9,10},{10,... | collective-permute-start | bytes 294920 | tf_op jit(solution)/shard_map/ppermute | solution.py:23
  17.7 6.3 %collective-permute-start.8 = (f32[96,256]{1,0:T(8,128)S(1)}, f32[96,256]{1,0:T(8,128)S(1)}, u32[]{:S(2)}, u32[]{:S(2)}) collective-permute-start(f32[96,256]{1,0:T(8,128)S(1)} %get-tuple-element.27.refs_4_), channel_id=1, source_target_pairs={{0,6},{1,7},{2,4},{3,5},{4,2},{5,3},{6,0},{7,1},{8,14},{9,15},{10,... | collective-permute-start | bytes 294920 | tf_op jit(solution)/shard_map/ppermute | solution.py:23
  18.9 6.4 %collective-permute-start.9 = (f32[96,256]{1,0:T(8,128)S(1)}, f32[96,256]{1,0:T(8,128)S(1)}, u32[]{:S(2)}, u32[]{:S(2)}) collective-permute-start(f32[96,256]{1,0:T(8,128)S(1)} %get-tuple-element.27.refs_4_), channel_id=1, source_target_pairs={{0,5},{1,4},{2,7},{3,6},{4,1},{5,0},{6,3},{7,2},{8,13},{9,12},{10,... | collective-permute-start | bytes 294920 | tf_op jit(solution)/shard_map/ppermute | solution.py:23
  26.1 5.9 %collective-permute-start.10 = (f32[3,48,128]{2,1,0:T(8,128)S(1)}, f32[3,48,128]{2,1,0:T(8,128)S(1)}, u32[]{:S(2)}, u32[]{:S(2)}) collective-permute-start(f32[3,48,128]{2,1,0:T(8,128)S(1)} %get-tuple-element.33), channel_id=1, source_target_pairs={{0,2},{1,3},{2,0},{3,1},{4,6},{5,7},{6,4},{7,5},{8,10},{9,11},{10,... | collective-permute-start | bytes 221192 | tf_op jit(solution)/shard_map/ppermute | solution.py:23
  26.2 5.5 %collective-permute-start.11 = (f32[2,48,128]{2,1,0:T(8,128)S(1)}, f32[2,48,128]{2,1,0:T(8,128)S(1)}, u32[]{:S(2)}, u32[]{:S(2)}) collective-permute-start(f32[2,48,128]{2,1,0:T(8,128)S(1)} %get-tuple-element.35), channel_id=1, source_target_pairs={{0,26},{1,27},{2,24},{3,25},{4,30},{5,31},{6,28},{7,29},{8,18},{9,... | collective-permute-start | bytes 147464 | tf_op jit(solution)/shard_map/ppermute | solution.py:23
  31.6 3.6 %collective-permute-start.12 = (f32[2,48,128]{2,1,0:T(8,128)S(1)}, f32[2,48,128]{2,1,0:T(8,128)S(1)}, u32[]{:S(2)}, u32[]{:S(2)}) collective-permute-start(f32[2,48,128]{2,1,0:T(8,128)S(1)} %collective-permute-done.11.last), channel_id=1, source_target_pairs={{0,2},{1,3},{2,0},{3,1},{4,6},{5,7},{6,4},{7,5},{8,10},{9,11},{10,... | collective-permute-start | bytes 147464 | tf_op jit(solution)/shard_map/ppermute | solution.py:23
  32.0 4.2 %collective-permute-start.13 = (f32[48,128]{1,0:T(8,128)S(1)}, f32[48,128]{1,0:T(8,128)S(1)}, u32[]{:S(2)}, u32[]{:S(2)}) collective-permute-start(f32[48,128]{1,0:T(8,128)S(1)} %get-tuple-element.36), channel_id=1, source_target_pairs={{0,18},{1,19},{2,16},{3,17},{4,22},{5,23},{6,20},{7,21},{8,26},{9,... | collective-permute-start | bytes 73736 | tf_op jit(solution)/shard_map/ppermute | solution.py:23
  34.4 3.3 %collective-permute-start.14 = (f32[48,128]{1,0:T(8,128)S(1)}, f32[48,128]{1,0:T(8,128)S(1)}, u32[]{:S(2)}, u32[]{:S(2)}) collective-permute-start(f32[48,128]{1,0:T(8,128)S(1)} %get-tuple-element.37), channel_id=1, source_target_pairs={{0,10},{1,11},{2,8},{3,9},{4,14},{5,15},{6,12},{7,13},{8,2},{9,3},... | collective-permute-start | bytes 73736 | tf_op jit(solution)/shard_map/ppermute | solution.py:23

commit v7 on v6

--- a/solution.py
+++ b/solution.py
@@ -35,16 +35,14 @@
     copies = [pltpu.make_async_copy(*move, sems.at[n]) for n, move in enumerate(moves)]
     for copy in copies:
         copy.start()
-    copies[0].wait()
-    copies[1].wait()
+    for copy in copies:
+        copy.wait()
     half = noise.shape[0] // 2
     message[0:half, :] = jnp.concatenate([noise[0:half, :], noise[half:, :]], axis=1)
     spot = positions[...]
     pad = jnp.zeros((8 - spot.shape[0], spot.shape[1]), f32)
     spot = jnp.concatenate([spot, pad], axis=0)
     message[half:, :] = jnp.concatenate([spot, spot], axis=1)
-    copies[2].wait()
-    copies[3].wait()
     highest, lowest = bounds[1], bounds[0]
     scalars[0:4, :] = jnp.full((4, 128), 0.5 * (highest + lowest), f32)
     scalars[4:8, :] = jnp.full((4, 128), 0.5 * (highest - lowest), f32)
@@ -221,7 +219,6 @@
         part = swapped(ref[...], number + 1, width)
         total = total + part
         own = own + part[:, :width]
-    first_image[...] = own
     linear[...] = total / scalars[4:5, 0:1]
     field = [linear[c * vectors : (c + 1) * vectors, :] for c in range(3)]
     value = jnp.concatenate(apply_tiles(field, high, low), axis=0)
@@ -231,6 +228,7 @@
         sent[number] = packed_block(value, count + number, width)
     last[0] = packed_block(value, count - 1, width)
     last[1] = packed_block(value, 2 * count - 1, width)
+    first_image[...] = own
 
 
 def fourth_kernel(kept, arrived, *outgoing):

time: 38.5 us -> 38.5 us (level)
  no operation moved by 1% of the time
where the time goes in v7:
time: 38.5 us; the launch traced here: 38.3 us
  starting transfers between devices  18.9 us (49%)
  waiting for transfers between devices  12.2 us (32%)
  Pallas kernels  6.45 us (17%)
  between operations  0.71 us (2%)
    ppermute x15, starting transfers between devices, exchange(): return lax.ppermute(block, axes, [(i, i ^ mask) for i in range(count)])  18.9 us
    ppermute x15, waiting for transfers between devices, exchange(): return lax.ppermute(block, axes, [(i, i ^ mask) for i in range(count)])  12.2 us
    pallas_call x8, Pallas kernels, call(): pl.pallas_call(kernel, in_specs=[pl.BlockSpec(memory_space=space)] * len(...  6.45 us
  transfers between devices with their start and end apart: 15, of which 9 were waited for; matrix products, arithmetic and copies ran while one was open for 0% of the time, Pallas kernels for 9%

profile of v7, /device:TPU:0, one launch (start us, length us, event | category | flops | bytes accessed | tf_op | source)
XLA Modules:
  0.0 38.3 jit_solution(15817391756195220418)
XLA Ops:
  0.6 0.9 %shard_map.59 = (f32[56,128]{1,0:T(8,128)S(1)}, f32[96,64]{1,0:T(8,128)S(1)}, f32[3,64]{1,0:T(4,128)S(1)}, f32[8,128]{1,0:T(8,128)S(1)}, f32[8,128]{1,0:T(8,128)S(1)}) custom-call(f32[96,64]{1,0:T(8,128)} %bitcast.6, f32[3,64]{1,0:T(4,128)} %positions_in.1, f32[2]{0:T(128)} %bounds_in.1, f32[8,128]{1,0:T(8,128)} %constant.2.clone.nodes_in), custom_call_target="tpu_custom_call" | custom-call | tf_op jit(solution)/shard_map/pallas_call | solution.py:272
  1.6 3.6 %collective-permute-start.3 = (f32[1,56,128]{2,1,0:T(8,128)S(1)}, f32[1,56,128]{2,1,0:T(8,128)S(1)}, u32[]{:S(2)}, u32[]{:S(2)}) collective-permute-start(f32[1,56,128]{2,1,0:T(8,128)S(1)} %bitcast.4), channel_id=1, source_target_pairs={{0,18},{1,19},{2,16},{3,17},{4,22},{5,23},{6,20},{7,21},{8,26},{9,... | collective-permute-start | bytes 86024 | tf_op jit(solution)/shard_map/ppermute | solution.py:23
  5.1 1.7 %collective-permute-done.3 = f32[1,56,128]{2,1,0:T(8,128)S(1)} collective-permute-done((f32[1,56,128]{2,1,0:T(8,128)S(1)}, f32[1,56,128]{2,1,0:T(8,128)S(1)}, u32[]{:S(2)}, u32[]{:S(2)}) %collective-permute-start.3) | collective-permute-done | bytes 28704 | tf_op jit(solution)/shard_map/ppermute | solution.py:23
  6.8 1.8 %collective-permute-start.4 = (f32[2,56,128]{2,1,0:T(8,128)S(1)}, f32[2,56,128]{2,1,0:T(8,128)S(1)}, u32[]{:S(2)}, u32[]{:S(2)}) collective-permute-start(f32[2,56,128]{2,1,0:T(8,128)S(1)} %pad_maximum_fusion.refs_0_), channel_id=1, source_target_pairs={{0,10},{1,11},{2,8},{3,9},{4,14},{5,15},{6,12},{7,13},{8,2},{9,3},... | collective-permute-start | bytes 172040 | tf_op jit(solution)/shard_map/ppermute | solution.py:23
  8.7 2.4 %collective-permute-start.2 = (f32[3,64]{1,0:T(4,128)S(1)}, f32[3,64]{1,0:T(4,128)S(1)}, u32[]{:S(2)}, u32[]{:S(2)}) collective-permute-start(f32[3,64]{1,0:T(4,128)S(1)} %get-tuple-element.23), channel_id=1, source_target_pairs={{0,5},{1,4},{2,7},{3,6},{4,1},{5,0},{6,3},{7,2},{8,13},{9,12},{10,... | collective-permute-start | bytes 2312 | tf_op jit(solution)/shard_map/ppermute | solution.py:23
  11.1 0.2 collective-permute-start.1
  11.3 0.5 %collective-permute-start = (f32[3,64]{1,0:T(4,128)S(1)}, f32[3,64]{1,0:T(4,128)S(1)}, u32[]{:S(2)}, u32[]{:S(2)}) collective-permute-start(f32[3,64]{1,0:T(4,128)S(1)} %get-tuple-element.23), channel_id=1, source_target_pairs={{0,3},{1,2},{2,1},{3,0},{4,7},{5,6},{6,5},{7,4},{8,11},{9,10},{10,... | collective-permute-start | bytes 2312 | tf_op jit(solution)/shard_map/ppermute | solution.py:23
  11.9 0.1 collective-permute-start.5
  12.0 0.0 collective-permute-done.4.refs_1_.refs_0_
  12.0 0.4 %collective-permute-start.6 = (f32[2,56,128]{2,1,0:T(8,128)S(1)}, f32[2,56,128]{2,1,0:T(8,128)S(1)}, u32[]{:S(2)}, u32[]{:S(2)}) collective-permute-start(f32[2,56,128]{2,1,0:T(8,128)S(1)} %collective-permute-done.4.refs_1_.refs_0_), channel_id=1, source_target_pairs={{0,2},{1,3},{2,0},{3,1},{4,6},{5,7},{6,4},{7,5},{8,10},{9,11},{10,... | collective-permute-start | bytes 172040 | tf_op jit(solution)/shard_map/ppermute | solution.py:23
  12.4 0.8 %collective-permute-done.2 = f32[3,64]{1,0:T(4,128)S(1)} collective-permute-done((f32[3,64]{1,0:T(4,128)S(1)}, f32[3,64]{1,0:T(4,128)S(1)}, u32[]{:S(2)}, u32[]{:S(2)}) %collective-permute-start.2) | collective-permute-done | bytes 800 | tf_op jit(solution)/shard_map/ppermute | solution.py:23
  13.1 1.0 %collective-permute-done.1 = f32[3,64]{1,0:T(4,128)S(1)} collective-permute-done((f32[3,64]{1,0:T(4,128)S(1)}, f32[3,64]{1,0:T(4,128)S(1)}, u32[]{:S(2)}, u32[]{:S(2)}) %collective-permute-start.1) | collective-permute-done | bytes 800 | tf_op jit(solution)/shard_map/ppermute | solution.py:23
  14.1 0.2 collective-permute-done
  14.3 0.1 pad_maximum_fusion.1.near_positions
  14.4 0.0 collective-permute-done.5.refs_2_.refs_1_
  14.4 1.2 %shard_map.61.before = f32[96,256]{1,0:T(8,128)S(1)} custom-call(f32[3,256]{1,0:T(4,128)S(1)} %pad_maximum_fusion.1.near_positions, f32[2,56,128]{2,1,0:T(8,128)S(1)} %pad_maximum_fusion.refs_0_, f32[2,56,128]{2,1,0:T(8,128)S(1)} %collective-permute-done.5.refs_2_.refs_1_), custom_call_target="tpu_custom_call" | custom-call | tf_op jit(solution)/shard_map/pallas_call | solution.py:272
  15.6 0.7 %shard_map.62.before = f32[96,256]{1,0:T(8,128)S(1)} custom-call(f32[3,256]{1,0:T(4,128)S(1)} %pad_maximum_fusion.1.near_positions, f32[96,256]{1,0:T(8,128)S(1)} %shard_map.61.before, f32[2,56,128]{2,1,0:T(8,128)S(1)} %collective-permute-done.4.refs_1_.refs_0_), custom_call_target="tpu_custom_call" | custom-call | tf_op jit(solution)/shard_map/pallas_call | solution.py:272
  16.3 0.0 collective-permute-done.6.refs_3_.refs_0_
  16.3 0.7 %shard_map.63 = (f32[96,256]{1,0:T(8,128)S(1)}, f32[96,256]{1,0:T(8,128)S(1)}) custom-call(f32[8,128]{1,0:T(8,128)S(1)} %get-tuple-element.21.scalars, f32[96,64]{1,0:T(8,128)S(1)} %get-tuple-element.26.noise, f32[3,256]{1,0:T(4,128)S(1)} %pad_maximum_fusion.1.near_positions, f32[96,256]{1,0:T(8,128)S(1)} %shard_map.62.before, ...), custom_call_target="tpu_custom_call" | custom-call | tf_op jit(solution)/shard_map/pallas_call | solution.py:272
  17.1 0.6 %collective-permute-start.7 = (f32[96,256]{1,0:T(8,128)S(1)}, f32[96,256]{1,0:T(8,128)S(1)}, u32[]{:S(2)}, u32[]{:S(2)}) collective-permute-start(f32[96,256]{1,0:T(8,128)S(1)} %get-tuple-element.27.refs_4_), channel_id=1, source_target_pairs={{0,3},{1,2},{2,1},{3,0},{4,7},{5,6},{6,5},{7,4},{8,11},{9,10},{10,... | collective-permute-start | bytes 294920 | tf_op jit(solution)/shard_map/ppermute | solution.py:23
  17.7 1.2 %collective-permute-start.8 = (f32[96,256]{1,0:T(8,128)S(1)}, f32[96,256]{1,0:T(8,128)S(1)}, u32[]{:S(2)}, u32[]{:S(2)}) collective-permute-start(f32[96,256]{1,0:T(8,128)S(1)} %get-tuple-element.27.refs_4_), channel_id=1, source_target_pairs={{0,6},{1,7},{2,4},{3,5},{4,2},{5,3},{6,0},{7,1},{8,14},{9,15},{10,... | collective-permute-start | bytes 294920 | tf_op jit(solution)/shard_map/ppermute | solution.py:23
  18.9 1.4 %collective-permute-start.9 = (f32[96,256]{1,0:T(8,128)S(1)}, f32[96,256]{1,0:T(8,128)S(1)}, u32[]{:S(2)}, u32[]{:S(2)}) collective-permute-start(f32[96,256]{1,0:T(8,128)S(1)} %get-tuple-element.27.refs_4_), channel_id=1, source_target_pairs={{0,5},{1,4},{2,7},{3,6},{4,1},{5,0},{6,3},{7,2},{8,13},{9,12},{10,... | collective-permute-start | bytes 294920 | tf_op jit(solution)/shard_map/ppermute | solution.py:23
  20.4 1.4 %shard_map.60 = (bf16[6,256,512]{2,1,0:T(8,128)(2,1)S(1)}, bf16[6,256,512]{2,1,0:T(8,128)(2,1)S(1)}, f32[8,128]{1,0:T(8,128)S(1)}) custom-call(f32[8,128]{1,0:T(8,128)S(1)} %get-tuple-element.21.scalars, f32[8,128]{1,0:T(8,128)S(1)} %get-tuple-element.22.nodes, f32[3,256]{1,0:T(4,128)S(1)} %pad_maximum_fusion.1.near_positions, ...), custom_call_target="tpu_custom_call" | custom-call | tf_op jit(solution)/shard_map/pallas_call | solution.py:272
  21.7 0.0 collective-permute-done.7.refs_0_
  21.8 2.2 %collective-permute-done.8.refs_1_ = f32[96,256]{1,0:T(8,128)S(1)} collective-permute-done((f32[96,256]{1,0:T(8,128)S(1)}, f32[96,256]{1,0:T(8,128)S(1)}, u32[]{:S(2)}, u32[]{:S(2)}) %collective-permute-start.8) | collective-permute-done | bytes 98336 | tf_op jit(solution)/shard_map/ppermute | solution.py:23
  24.0 1.3 %collective-permute-done.9.refs_2_ = f32[96,256]{1,0:T(8,128)S(1)} collective-permute-done((f32[96,256]{1,0:T(8,128)S(1)}, f32[96,256]{1,0:T(8,128)S(1)}, u32[]{:S(2)}, u32[]{:S(2)}) %collective-permute-start.9) | collective-permute-done | bytes 98336 | tf_op jit(solution)/shard_map/ppermute | solution.py:23
  25.3 0.8 %shard_map.64 = (f32[96,64]{1,0:T(8,128)S(1)}, f32[2,48,128]{2,1,0:T(8,128)S(1)}, f32[3,48,128]{2,1,0:T(8,128)S(1)}, f32[3,48,128]{2,1,0:T(8,128)S(1)}) custom-call(f32[8,128]{1,0:T(8,128)S(1)} %get-tuple-element.21.scalars, f32[96,256]{1,0:T(8,128)S(1)} %collective-permute-done.7.refs_0_, f32[96,256]{1,0:T(8,128)S(1)} %collective-permute-done.8.refs_1_, ...), custom_call_target="tpu_custom_call" | custom-call | tf_op jit(solution)/shard_map/pallas_call | solution.py:272
  26.1 0.1 collective-permute-start.10
  26.2 2.9 %collective-permute-start.11 = (f32[2,48,128]{2,1,0:T(8,128)S(1)}, f32[2,48,128]{2,1,0:T(8,128)S(1)}, u32[]{:S(2)}, u32[]{:S(2)}) collective-permute-start(f32[2,48,128]{2,1,0:T(8,128)S(1)} %get-tuple-element.35), channel_id=1, source_target_pairs={{0,26},{1,27},{2,24},{3,25},{4,30},{5,31},{6,28},{7,29},{8,18},{9,... | collective-permute-start | bytes 147464 | tf_op jit(solution)/shard_map/ppermute | solution.py:23
  29.1 2.5 %collective-permute-done.11.last = f32[2,48,128]{2,1,0:T(8,128)S(1)} collective-permute-done((f32[2,48,128]{2,1,0:T(8,128)S(1)}, f32[2,48,128]{2,1,0:T(8,128)S(1)}, u32[]{:S(2)}, u32[]{:S(2)}) %collective-permute-start.11) | collective-permute-done | bytes 49184 | tf_op jit(solution)/shard_map/ppermute | solution.py:23
  31.6 0.3 collective-permute-start.12
  32.0 0.0 collective-permute-done.10.arrived
  32.0 2.3 %collective-permute-start.13 = (f32[48,128]{1,0:T(8,128)S(1)}, f32[48,128]{1,0:T(8,128)S(1)}, u32[]{:S(2)}, u32[]{:S(2)}) collective-permute-start(f32[48,128]{1,0:T(8,128)S(1)} %get-tuple-element.36), channel_id=1, source_target_pairs={{0,18},{1,19},{2,16},{3,17},{4,22},{5,23},{6,20},{7,21},{8,26},{9,... | collective-permute-start | bytes 73736 | tf_op jit(solution)/shard_map/ppermute | solution.py:23
  34.3 0.8 %collective-permute-start.14 = (f32[48,128]{1,0:T(8,128)S(1)}, f32[48,128]{1,0:T(8,128)S(1)}, u32[]{:S(2)}, u32[]{:S(2)}) collective-permute-start(f32[48,128]{1,0:T(8,128)S(1)} %get-tuple-element.37), channel_id=1, source_target_pairs={{0,10},{1,11},{2,8},{3,9},{4,14},{5,15},{6,12},{7,13},{8,2},{9,3},... | collective-permute-start | bytes 73736 | tf_op jit(solution)/shard_map/ppermute | solution.py:23
  35.2 0.0 collective-permute-done.12.last_across
  35.2 1.0 %collective-permute-done.13.refs_0_ = f32[48,128]{1,0:T(8,128)S(1)} collective-permute-done((f32[48,128]{1,0:T(8,128)S(1)}, f32[48,128]{1,0:T(8,128)S(1)}, u32[]{:S(2)}, u32[]{:S(2)}) %collective-permute-start.13) | collective-permute-done | bytes 24608 | tf_op jit(solution)/shard_map/ppermute | solution.py:23
  36.2 1.4 %collective-permute-done.14.refs_1_ = f32[48,128]{1,0:T(8,128)S(1)} collective-permute-done((f32[48,128]{1,0:T(8,128)S(1)}, f32[48,128]{1,0:T(8,128)S(1)}, u32[]{:S(2)}, u32[]{:S(2)}) %collective-permute-start.14) | collective-permute-done | bytes 24608 | tf_op jit(solution)/shard_map/ppermute | solution.py:23
  37.6 0.7 %shard_map.66 = (f32[96,64]{1,0:T(8,128)}, f32[2,96,64]{2,1,0:T(8,128)}) custom-call(f32[8,128]{1,0:T(8,128)S(1)} %get-tuple-element.21.scalars, f32[8,128]{1,0:T(8,128)S(1)} %get-tuple-element.25.weights, f32[96,64]{1,0:T(8,128)S(1)} %get-tuple-element.26.noise, f32[96,64]{1,0:T(8,128)S(1)} %get-tuple-element.31.first_image, ...), custom_call_target="tpu_custom_call" | custom-call | tf_op jit(solution)/shard_map/pallas_call | solution.py:272
  (2 shorter events, 0.0 us)
Async XLA Ops:
  1.6 5.3 %collective-permute-start.3 = (f32[1,56,128]{2,1,0:T(8,128)S(1)}, f32[1,56,128]{2,1,0:T(8,128)S(1)}, u32[]{:S(2)}, u32[]{:S(2)}) collective-permute-start(f32[1,56,128]{2,1,0:T(8,128)S(1)} %bitcast.4), channel_id=1, source_target_pairs={{0,18},{1,19},{2,16},{3,17},{4,22},{5,23},{6,20},{7,21},{8,26},{9,... | collective-permute-start | bytes 86024 | tf_op jit(solution)/shard_map/ppermute | solution.py:23
  6.8 5.2 %collective-permute-start.4 = (f32[2,56,128]{2,1,0:T(8,128)S(1)}, f32[2,56,128]{2,1,0:T(8,128)S(1)}, u32[]{:S(2)}, u32[]{:S(2)}) collective-permute-start(f32[2,56,128]{2,1,0:T(8,128)S(1)} %pad_maximum_fusion.refs_0_), channel_id=1, source_target_pairs={{0,10},{1,11},{2,8},{3,9},{4,14},{5,15},{6,12},{7,13},{8,2},{9,3},... | collective-permute-start | bytes 172040 | tf_op jit(solution)/shard_map/ppermute | solution.py:23
  8.7 4.5 %collective-permute-start.2 = (f32[3,64]{1,0:T(4,128)S(1)}, f32[3,64]{1,0:T(4,128)S(1)}, u32[]{:S(2)}, u32[]{:S(2)}) collective-permute-start(f32[3,64]{1,0:T(4,128)S(1)} %get-tuple-element.23), channel_id=1, source_target_pairs={{0,5},{1,4},{2,7},{3,6},{4,1},{5,0},{6,3},{7,2},{8,13},{9,12},{10,... | collective-permute-start | bytes 2312 | tf_op jit(solution)/shard_map/ppermute | solution.py:23
  11.1 3.0 %collective-permute-start.1 = (f32[3,64]{1,0:T(4,128)S(1)}, f32[3,64]{1,0:T(4,128)S(1)}, u32[]{:S(2)}, u32[]{:S(2)}) collective-permute-start(f32[3,64]{1,0:T(4,128)S(1)} %get-tuple-element.23), channel_id=1, source_target_pairs={{0,6},{1,7},{2,4},{3,5},{4,2},{5,3},{6,0},{7,1},{8,14},{9,15},{10,... | collective-permute-start | bytes 2312 | tf_op jit(solution)/shard_map/ppermute | solution.py:23
  11.3 3.0 %collective-permute-start = (f32[3,64]{1,0:T(4,128)S(1)}, f32[3,64]{1,0:T(4,128)S(1)}, u32[]{:S(2)}, u32[]{:S(2)}) collective-permute-start(f32[3,64]{1,0:T(4,128)S(1)} %get-tuple-element.23), channel_id=1, source_target_pairs={{0,3},{1,2},{2,1},{3,0},{4,7},{5,6},{6,5},{7,4},{8,11},{9,10},{10,... | collective-permute-start | bytes 2312 | tf_op jit(solution)/shard_map/ppermute | solution.py:23
  11.9 2.6 %collective-permute-start.5 = (f32[2,56,128]{2,1,0:T(8,128)S(1)}, f32[2,56,128]{2,1,0:T(8,128)S(1)}, u32[]{:S(2)}, u32[]{:S(2)}) collective-permute-start(f32[2,56,128]{2,1,0:T(8,128)S(1)} %pad_maximum_fusion.refs_0_), channel_id=1, source_target_pairs={{0,2},{1,3},{2,0},{3,1},{4,6},{5,7},{6,4},{7,5},{8,10},{9,11},{10,... | collective-permute-start | bytes 172040 | tf_op jit(solution)/shard_map/ppermute | solution.py:23
  12.0 4.3 %collective-permute-start.6 = (f32[2,56,128]{2,1,0:T(8,128)S(1)}, f32[2,56,128]{2,1,0:T(8,128)S(1)}, u32[]{:S(2)}, u32[]{:S(2)}) collective-permute-start(f32[2,56,128]{2,1,0:T(8,128)S(1)} %collective-permute-done.4.refs_1_.refs_0_), channel_id=1, source_target_pairs={{0,2},{1,3},{2,0},{3,1},{4,6},{5,7},{6,4},{7,5},{8,10},{9,11},{10,... | collective-permute-start | bytes 172040 | tf_op jit(solution)/shard_map/ppermute | solution.py:23
  17.1 4.7 %collective-permute-start.7 = (f32[96,256]{1,0:T(8,128)S(1)}, f32[96,256]{1,0:T(8,128)S(1)}, u32[]{:S(2)}, u32[]{:S(2)}) collective-permute-start(f32[96,256]{1,0:T(8,128)S(1)} %get-tuple-element.27.refs_4_), channel_id=1, source_target_pairs={{0,3},{1,2},{2,1},{3,0},{4,7},{5,6},{6,5},{7,4},{8,11},{9,10},{10,... | collective-permute-start | bytes 294920 | tf_op jit(solution)/shard_map/ppermute | solution.py:23
  17.7 6.3 %collective-permute-start.8 = (f32[96,256]{1,0:T(8,128)S(1)}, f32[96,256]{1,0:T(8,128)S(1)}, u32[]{:S(2)}, u32[]{:S(2)}) collective-permute-start(f32[96,256]{1,0:T(8,128)S(1)} %get-tuple-element.27.refs_4_), channel_id=1, source_target_pairs={{0,6},{1,7},{2,4},{3,5},{4,2},{5,3},{6,0},{7,1},{8,14},{9,15},{10,... | collective-permute-start | bytes 294920 | tf_op jit(solution)/shard_map/ppermute | solution.py:23
  18.9 6.4 %collective-permute-start.9 = (f32[96,256]{1,0:T(8,128)S(1)}, f32[96,256]{1,0:T(8,128)S(1)}, u32[]{:S(2)}, u32[]{:S(2)}) collective-permute-start(f32[96,256]{1,0:T(8,128)S(1)} %get-tuple-element.27.refs_4_), channel_id=1, source_target_pairs={{0,5},{1,4},{2,7},{3,6},{4,1},{5,0},{6,3},{7,2},{8,13},{9,12},{10,... | collective-permute-start | bytes 294920 | tf_op jit(solution)/shard_map/ppermute | solution.py:23
  26.1 5.9 %collective-permute-start.10 = (f32[3,48,128]{2,1,0:T(8,128)S(1)}, f32[3,48,128]{2,1,0:T(8,128)S(1)}, u32[]{:S(2)}, u32[]{:S(2)}) collective-permute-start(f32[3,48,128]{2,1,0:T(8,128)S(1)} %get-tuple-element.33), channel_id=1, source_target_pairs={{0,2},{1,3},{2,0},{3,1},{4,6},{5,7},{6,4},{7,5},{8,10},{9,11},{10,... | collective-permute-start | bytes 221192 | tf_op jit(solution)/shard_map/ppermute | solution.py:23
  26.2 5.5 %collective-permute-start.11 = (f32[2,48,128]{2,1,0:T(8,128)S(1)}, f32[2,48,128]{2,1,0:T(8,128)S(1)}, u32[]{:S(2)}, u32[]{:S(2)}) collective-permute-start(f32[2,48,128]{2,1,0:T(8,128)S(1)} %get-tuple-element.35), channel_id=1, source_target_pairs={{0,26},{1,27},{2,24},{3,25},{4,30},{5,31},{6,28},{7,29},{8,18},{9,... | collective-permute-start | bytes 147464 | tf_op jit(solution)/shard_map/ppermute | solution.py:23
  31.6 3.6 %collective-permute-start.12 = (f32[2,48,128]{2,1,0:T(8,128)S(1)}, f32[2,48,128]{2,1,0:T(8,128)S(1)}, u32[]{:S(2)}, u32[]{:S(2)}) collective-permute-start(f32[2,48,128]{2,1,0:T(8,128)S(1)} %collective-permute-done.11.last), channel_id=1, source_target_pairs={{0,2},{1,3},{2,0},{3,1},{4,6},{5,7},{6,4},{7,5},{8,10},{9,11},{10,... | collective-permute-start | bytes 147464 | tf_op jit(solution)/shard_map/ppermute | solution.py:23
  32.0 4.2 %collective-permute-start.13 = (f32[48,128]{1,0:T(8,128)S(1)}, f32[48,128]{1,0:T(8,128)S(1)}, u32[]{:S(2)}, u32[]{:S(2)}) collective-permute-start(f32[48,128]{1,0:T(8,128)S(1)} %get-tuple-element.36), channel_id=1, source_target_pairs={{0,18},{1,19},{2,16},{3,17},{4,22},{5,23},{6,20},{7,21},{8,26},{9,... | collective-permute-start | bytes 73736 | tf_op jit(solution)/shard_map/ppermute | solution.py:23
  34.3 3.3 %collective-permute-start.14 = (f32[48,128]{1,0:T(8,128)S(1)}, f32[48,128]{1,0:T(8,128)S(1)}, u32[]{:S(2)}, u32[]{:S(2)}) collective-permute-start(f32[48,128]{1,0:T(8,128)S(1)} %get-tuple-element.37), channel_id=1, source_target_pairs={{0,10},{1,11},{2,8},{3,9},{4,14},{5,15},{6,12},{7,13},{8,2},{9,3},... | collective-permute-start | bytes 73736 | tf_op jit(solution)/shard_map/ppermute | solution.py:23
